TPU v7x, 16 devices: a whole 2x2x2 slice. The times are simulated.
16 devices in a mesh: stage: 2 (over z), expert: 8 (over y, x, core).
Axes of the slice: x: 2, y: 2, z: 2, core: 2. Of those that a mesh axis runs over, the one named last changes fastest.
Arguments:
- x_act: bfloat16 [2, 8192, 2048], P('stage', 'expert')
- route_idx: int32 [2, 8192, 8], P('stage', 'expert')
- route_wts: float32 [2, 8192, 8], P('stage', 'expert')
- w_one: bfloat16 [2, 32, 2048, 512], P('stage', 'expert')
- w_three: bfloat16 [2, 32, 2048, 512], P('stage', 'expert')
- w_two: bfloat16 [2, 32, 512, 2048], P('stage', 'expert')
- dy_act: bfloat16 [2, 8192, 2048], P('stage', 'expert')
Outputs:
- output 1: bfloat16 [2, 8192, 2048], P('stage', 'expert')
- output 2: bfloat16 [2, 8192, 2048], P('stage', 'expert')
- output 3: bfloat16 [2, 32, 2048, 512], P('stage', 'expert')
- output 4: bfloat16 [2, 32, 2048, 512], P('stage', 'expert')
- output 5: bfloat16 [2, 32, 512, 2048], P('stage', 'expert')
All inputs are finite; a program needn't handle non-finite values.
Results may differ from a plain program's by a relative error of at most 0.0126552.
Values are sent between devices in bfloat16 or wider.
A program may use at most 1 GiB of HBM per device.

v0:
```python
import jax
import jax.numpy as jnp
from jax import lax
from jax.sharding import PartitionSpec as P


def slot_tables(idx_blk, first_exp, n_exp, capacity):
    n_slot = idx_blk.shape[0] * idx_blk.shape[1]
    slot_ids = idx_blk.reshape(n_slot) - first_exp
    hit_mat = (slot_ids[:, None] == jnp.arange(n_exp, dtype=jnp.int32)[None, :]).astype(jnp.int32)
    slot_rank = jnp.sum(jnp.cumsum(hit_mat, axis=0) * hit_mat, axis=1) - 1
    is_local = (slot_ids >= 0) & (slot_ids < n_exp)
    buf_pos = jnp.where(is_local, slot_ids * capacity + slot_rank, n_exp * capacity)
    slot_at = jnp.full((n_exp * capacity,), n_slot, jnp.int32).at[buf_pos].set(jnp.arange(n_slot, dtype=jnp.int32), mode='drop')
    return buf_pos, slot_at


def take_rows(row_table, row_ids):
    return jnp.take(row_table, row_ids, axis=0, mode='fill', fill_value=0)


def expert_forward(x_buf, w_in_one, w_in_three, w_out):
    pre_one = jnp.einsum('pecd,edf->pecf', x_buf, w_in_one, preferred_element_type=jnp.float32)
    pre_three = jnp.einsum('pecd,edf->pecf', x_buf, w_in_three, preferred_element_type=jnp.float32)
    hidden = (pre_one * jax.nn.sigmoid(pre_one) * pre_three).astype(jnp.bfloat16)
    return jnp.einsum('pecf,efd->pecd', hidden, w_out, preferred_element_type=jnp.float32).astype(jnp.bfloat16)


def expert_backward(x_buf, d_buf, w_in_one, w_in_three, w_out):
    pre_one = jnp.einsum('pecd,edf->pecf', x_buf, w_in_one, preferred_element_type=jnp.float32)
    pre_three = jnp.einsum('pecd,edf->pecf', x_buf, w_in_three, preferred_element_type=jnp.float32)
    sig_one = jax.nn.sigmoid(pre_one)
    act_one = pre_one * sig_one
    hidden = (act_one * pre_three).astype(jnp.bfloat16)
    d_hidden = jnp.einsum('pecd,efd->pecf', d_buf, w_out, preferred_element_type=jnp.float32).astype(jnp.bfloat16).astype(jnp.float32)
    d_three = (d_hidden * act_one).astype(jnp.bfloat16)
    d_one = (d_hidden * pre_three * sig_one * (1.0 + pre_one * (1.0 - sig_one))).astype(jnp.bfloat16)
    dx_buf = (jnp.einsum('pecf,edf->pecd', d_one, w_in_one, preferred_element_type=jnp.float32) + jnp.einsum('pecf,edf->pecd', d_three, w_in_three, preferred_element_type=jnp.float32)).astype(jnp.bfloat16)
    g_one = jnp.einsum('pecd,pecf->edf', x_buf, d_one, preferred_element_type=jnp.float32).astype(jnp.bfloat16)
    g_three = jnp.einsum('pecd,pecf->edf', x_buf, d_three, preferred_element_type=jnp.float32).astype(jnp.bfloat16)
    g_two = jnp.einsum('pecf,pecd->efd', hidden, d_buf, preferred_element_type=jnp.float32).astype(jnp.bfloat16)
    return dx_buf, g_one, g_three, g_two


def solution(mesh):
    n_stage = mesh.shape['stage']
    n_dev = mesh.shape['expert']
    to_next = [(stage_idx, (stage_idx + 1) % n_stage) for stage_idx in range(n_stage)]
    to_prev = [((stage_idx + 1) % n_stage, stage_idx) for stage_idx in range(n_stage)]
    tok_spec = P('stage', 'expert', None)
    w_spec = P('stage', 'expert', None, None)

    def moe_layer(x_act, route_idx, route_wts, w_one, w_three, w_two, dy_act):
        x_src = x_act[0]
        n_tok, model_dim = x_src.shape
        top_k = route_idx.shape[2]
        n_local = w_one.shape[1]
        n_exp = n_local * n_dev
        capacity = 2 * n_tok * top_k // n_exp - 1
        w_in_one, w_in_three, w_out = w_one[0], w_three[0], w_two[0]

        x_dst = lax.ppermute(x_src, 'stage', to_next)
        idx_dst = lax.ppermute(route_idx[0], 'stage', to_next)
        wts_dst = lax.ppermute(route_wts[0], 'stage', to_next)
        buf_pos, slot_at = slot_tables(idx_dst, 0, n_exp, capacity)

        def dispatch(row_src, row_ids):
            send_buf = take_rows(row_src, row_ids).reshape(n_dev, n_local, capacity, model_dim)
            return lax.all_to_all(send_buf, 'expert', 0, 0)

        def combine(buf_rows):
            back_buf = lax.all_to_all(buf_rows, 'expert', 0, 0).reshape(n_exp * capacity, model_dim)
            return take_rows(back_buf, buf_pos).reshape(n_tok, top_k, model_dim)

        out_slot = combine(expert_forward(dispatch(x_dst, slot_at // top_k), w_in_one, w_in_three, w_out))
        y_dst = jnp.sum(wts_dst[:, :, None] * out_slot.astype(jnp.float32), axis=1).astype(jnp.bfloat16)

        x_again, y_dst = lax.optimization_barrier((x_src, y_dst))
        x_dst = lax.ppermute(x_again, 'stage', to_next)
        d_slot = (wts_dst[:, :, None] * dy_act[0][:, None, :].astype(jnp.float32)).astype(jnp.bfloat16).reshape(n_tok * top_k, model_dim)
        dx_buf, g_one, g_three, g_two = expert_backward(dispatch(x_dst, slot_at // top_k), dispatch(d_slot, slot_at), w_in_one, w_in_three, w_out)
        dx_slot = combine(dx_buf)
        dx_dst = jnp.sum(dx_slot.astype(jnp.float32), axis=1).astype(jnp.bfloat16)
        dx_src = lax.ppermute(dx_dst, 'stage', to_prev)
        return y_dst[None], dx_src[None], g_one[None], g_three[None], g_two[None]

    return jax.shard_map(moe_layer, mesh=mesh, in_specs=(tok_spec, tok_spec, tok_spec, w_spec, w_spec, w_spec, tok_spec), out_specs=(tok_spec, tok_spec, w_spec, w_spec, w_spec), check_vma=False)
```

profile of v0, /device:TPU:0, one launch (start us, length us, event | category | flops | bytes accessed | tf_op | source)
XLA Modules:
  0.0 5476.2 jit_solution(16954049768198438993)
XLA Ops:
  4.0 91.2 %collective-permute-done.2 = s32[1024,8]{0,1:T(8,128)S(1)} collective-permute-done((s32[1024,8]{0,1:T(8,128)}, s32[1024,8]{0,1:T(8,128)S(1)}, u32[]{:S(2)}, u32[]{:S(2)}) %collective-permute-start.2) | collective-permute-done | bytes 32800 | tf_op jit(solution)/shard_map/ppermute | solution.py:63
  141.1 124.3 %gather_fusion.1 = bf16[16352,2048]{1,0:T(8,128)(2,1)} fusion(bf16[1024,2048]{1,0:T(8,128)(2,1)} %collective-permute-done.1, s32[16384]{0:T(1024)S(1)} %pad_clamp_fusion.1), kind=kCustom, calls=%fused_computation.clone | custom fusion | bytes 134020992 | tf_op jit(solution)/shard_map/jit(_take)/gather | solution.py:19
  375.0 81.8 %copy.36 = bf16[8,4,511,2048]{3,1,2,0:T(4,128)(2,1)} copy(bf16[8,4,511,2048]{3,2,1,0:T(8,128)(2,1)} %reshape.144) | data formatting | bytes 133955584 | tf_op jit(solution)/shard_map/reshape | solution.py:68
  456.9 739.6 %all_to_all.25 = bf16[8,4,511,2048]{3,1,2,0:T(4,128)(2,1)} all-to-all(bf16[8,4,511,2048]{3,1,2,0:T(4,128)(2,1)} %copy.36), channel_id=1, replica_groups=mesh['stage'=2,'expert'=8] {'expert'}, dimensions={0} | all-to-all | bytes 133955584 | tf_op jit(solution)/shard_map/all_to_all | solution.py:69
  1196.5 109.5 %fusion.6 = f32[4,8,511,512]{3,2,1,0:T(8,128)} fusion(bf16[8,4,511,2048]{3,1,2,0:T(4,128)(2,1)} %all_to_all.25, bf16[1,4,2048,512]{3,2,1,0:T(8,128)(2,1)} %param.15), kind=kOutput, calls=%fused_computation.19 | convolution fusion | flops 34292629504 | bytes 108855296 | tf_op jit(solution)/shard_map/pecd,edf->pecf/dot_general | solution.py:24
  1306.0 109.6 %fusion.91 = bf16[8,4,511,512]{3,2,0,1:T(8,128)(2,1)} fusion(f32[4,8,511,512]{3,2,1,0:T(8,128)} %fusion.6, bf16[1,4,2048,512]{3,2,1,0:T(8,128)(2,1)} %param.14, bf16[8,4,511,2048]{3,1,2,0:T(4,128)(2,1)} %all_to_all.25), kind=kOutput, calls=%fused_computation.41.clone.clone.1 | convolution fusion | flops 34342862848 | bytes 125599744 | tf_op jit(solution)/shard_map/pecd,edf->pecf/dot_general | solution.py:23
  1460.8 82.3 %copy.39 = bf16[8,4,511,2048]{3,1,2,0:T(4,128)(2,1)} copy(bf16[8,4,511,2048]{3,2,0,1:T(8,128)(2,1)} %convert_bitcast_fusion) | data formatting | bytes 133955584 | tf_op jit(solution)/shard_map/convert_element_type | solution.py:26
  1576.9 631.6 %gather_fusion = bf16[16352,2048]{1,0:T(8,128)(2,1)} fusion(bf16[8192,2048]{1,0:T(8,128)(2,1)} %fusion.1, s32[16384]{0:T(1024)S(1)} %pad_clamp_fusion), kind=kCustom, calls=%fused_computation.4 | custom fusion | bytes 134020992 | tf_op jit(solution)/shard_map/jit(_take)/gather | solution.py:19
  2208.5 65.4 %gather.13 = bf16[8,4,511,2048]{3,2,1,0:T(8,128)(2,1)} reshape(bf16[16352,2048]{1,0:T(8,128)(2,1)} %gather_fusion) | data formatting | bytes 133955584 | tf_op jit(solution)/shard_map/jit(_take)/gather | solution.py:19
  2318.3 81.9 %copy.42 = bf16[8,4,511,2048]{3,1,2,0:T(4,128)(2,1)} copy(bf16[8,4,511,2048]{3,2,1,0:T(8,128)(2,1)} %broadcast_select_fusion) | data formatting | bytes 133955584 | tf_op jit(solution)/shard_map/jit(_take)/select_n | solution.py:19
  2520.7 191.2 %gather_fusion.2 = bf16[8192,2048]{1,0:T(8,128)(2,1)} fusion(bf16[16352,2048]{1,0:T(8,128)(2,1)} %reshape.145, s32[8192]{0:T(1024)S(1)} %copy-done.8), kind=kCustom, calls=%fused_computation.1.clone | custom fusion | bytes 67141632 | tf_op jit(solution)/shard_map/jit(_take)/gather | solution.py:19
  2747.0 92.9 %collective-permute-done.3 = bf16[1024,2048]{1,0:T(8,128)(2,1)} collective-permute-done((bf16[1024,2048]{1,0:T(8,128)(2,1)}, bf16[1024,2048]{1,0:T(8,128)(2,1)}, u32[]{:S(2)}, u32[]{:S(2)}) %collective-permute-start.3) | collective-permute-done | bytes 4194336 | tf_op jit(solution)/shard_map/ppermute | solution.py:79
  2839.9 124.5 %gather_fusion.3 = bf16[16352,2048]{1,0:T(8,128)(2,1)} fusion(bf16[1024,2048]{1,0:T(8,128)(2,1)} %collective-permute-done.3, s32[16384]{0:T(1024)S(1)} %copy-done.3), kind=kCustom, calls=%fused_computation.2.clone | custom fusion | bytes 134020992 | tf_op jit(solution)/shard_map/jit(_take)/gather | solution.py:19
  3074.0 81.8 %copy.44 = bf16[8,4,511,2048]{3,1,2,0:T(4,128)(2,1)} copy(bf16[8,4,511,2048]{3,2,1,0:T(8,128)(2,1)} %reshape.146) | data formatting | bytes 133955584 | tf_op jit(solution)/shard_map/reshape | solution.py:68
  3165.7 106.4 %fusion.27 = bf16[4,8,511,512]{3,2,1,0:T(8,128)(2,1)} fusion(bf16[8,4,511,2048]{3,1,2,0:T(4,128)(2,1)} %all-to-all-done.2, bf16[1,4,512,2048]{3,2,1,0:T(8,128)(2,1)} %param.16), kind=kOutput, calls=%fused_computation.51 | convolution fusion | flops 34301001728 | bytes 92110848 | tf_op jit(solution)/shard_map/pecd,efd->pecf/dot_general | solution.py:35
  3272.1 616.0 %all-to-all-done.3 = bf16[8,4,511,2048]{3,1,2,0:T(4,128)(2,1)} async-done(((bf16[8,4,511,2048]{3,1,2,0:T(4,128)(2,1)}), bf16[8,4,511,2048]{3,1,2,0:T(4,128)(2,1)}, u32[]{:S(2)}, u32[]{:S(2)}) %all-to-all-start.3) | async-done | bytes 66977824 | tf_op jit(solution)/shard_map/all_to_all | solution.py:69
  3888.1 101.1 %copy.49 = bf16[8,4,511,2048]{2,3,0,1:T(8,128)(2,1)} copy(bf16[8,4,511,2048]{3,1,2,0:T(4,128)(2,1)} %all-to-all-done.3) | data formatting | bytes 133955584 | tf_op jit(solution)/shard_map/all_to_all | solution.py:69
  4034.8 66.5 %fusion.16 = (bf16[8,4,511,512]{3,2,0,1:T(8,128)(2,1)}, f32[4,8,511,512]{3,2,1,0:T(8,128)}) fusion(f32[4,8,511,512]{3,2,1,0:T(8,128)} %fusion.39, bf16[4,8,511,512]{3,2,1,0:T(8,128)(2,1)} %fusion.27, bf16[8,4,511,2048]{2,3,0,1:T(8,128)(2,1)} %copy.49, bf16[1,4,2048,512]{3,2,1,0:T(8,128)(2,1)} %param.14), kind=kOutput, calls=%fused_computation.33 | convolution fusion | flops 34384723968 | bytes 175833088 | tf_op jit(solution)/shard_map/pecd,edf->pecf/dot_general | solution.py:30
  4157.3 83.6 %fusion.10 = bf16[8,4,511,2048]{3,2,0,1:T(8,128)(2,1)} fusion(f32[4,8,511,2048]{3,2,1,0:T(8,128)} %fusion.33, bf16[1,4,2048,512]{3,2,1,0:T(8,128)(2,1)} %param.15, bf16[4,8,511,512]{3,2,1,0:T(8,128)(2,1)} %fusion.27, f32[4,8,511,512]{3,2,1,0:T(8,128)} %get-tuple-element.17), kind=kOutput, calls=%fused_computation.23 | convolution fusion | flops 34418212864 | bytes 259555328 | tf_op jit(solution)/shard_map/pecf,edf->pecd/dot_general | solution.py:38
  4240.9 82.3 %copy.47 = bf16[8,4,511,2048]{3,1,2,0:T(4,128)(2,1)} copy(bf16[8,4,511,2048]{3,2,0,1:T(8,128)(2,1)} %fusion.10) | data formatting | bytes 133955584 | tf_op jit(solution)/shard_map/convert_element_type | solution.py:38
  4382.0 140.5 %fusion.32 = bf16[1,4,512,2048]{3,2,1,0:T(8,128)(2,1)} fusion(bf16[8,4,511,2048]{3,1,2,0:T(4,128)(2,1)} %all-to-all-done.2, f32[4,8,511,512]{3,2,1,0:T(8,128)} %fusion.39, f32[4,8,511,512]{3,2,1,0:T(8,128)} %get-tuple-element.17), kind=kOutput, calls=%fused_computation.54 | convolution fusion | flops 34347057152 | bytes 142344192 | tf_op jit(solution)/shard_map/pecf,pecd->efd/dot_general | solution.py:41
  4522.4 533.0 %all-to-all-done.4 = bf16[8,4,511,2048]{3,1,2,0:T(4,128)(2,1)} async-done(((bf16[8,4,511,2048]{3,1,2,0:T(4,128)(2,1)}), bf16[8,4,511,2048]{3,1,2,0:T(4,128)(2,1)}, u32[]{:S(2)}, u32[]{:S(2)}) %all-to-all-start.4) | async-done | bytes 66977824 | tf_op jit(solution)/shard_map/all_to_all | solution.py:72
  5099.9 65.5 %reshape.147 = bf16[16352,2048]{1,0:T(8,128)(2,1)} reshape(bf16[8,4,511,2048]{3,2,1,0:T(8,128)(2,1)} %copy.48) | data formatting | bytes 133955584 | tf_op jit(solution)/shard_map/reshape | solution.py:72
  5165.5 191.2 %gather_fusion.4 = bf16[8192,2048]{1,0:T(8,128)(2,1)} fusion(bf16[16352,2048]{1,0:T(8,128)(2,1)} %reshape.147, s32[8192]{0:T(1024)S(1)} %copy-done.9), kind=kCustom, calls=%fused_computation.3.clone | custom fusion | bytes 67141632 | tf_op jit(solution)/shard_map/jit(_take)/gather | solution.py:19
  (97 shorter events, 880.9 us)
Async XLA Ops:
  0.6 140.5 %collective-permute-start.1 = (bf16[1024,2048]{1,0:T(8,128)(2,1)}, bf16[1024,2048]{1,0:T(8,128)(2,1)}, u32[]{:S(2)}, u32[]{:S(2)}) collective-permute-start(bf16[1024,2048]{1,0:T(8,128)(2,1)} %bitcast.200), channel_id=1, source_target_pairs={{0,8},{8,0},{1,9},{9,1},{2,10},{10,2},{3,11},{11,3},{4,12},{12,4},... | collective-permute-start | bytes 12582920 | tf_op jit(solution)/shard_map/ppermute | solution.py:62
  4.0 91.3 %collective-permute-start.2 = (s32[1024,8]{0,1:T(8,128)}, s32[1024,8]{0,1:T(8,128)S(1)}, u32[]{:S(2)}, u32[]{:S(2)}) collective-permute-start(s32[1024,8]{0,1:T(8,128)} %bitcast.202), channel_id=1, source_target_pairs={{0,8},{8,0},{1,9},{9,1},{2,10},{10,2},{3,11},{11,3},{4,12},{12,4},... | collective-permute-start | bytes 98312 | tf_op jit(solution)/shard_map/ppermute | solution.py:63
  95.7 169.8 %copy-start.6 = (s32[8192]{0:T(1024)}, s32[8192]{0:T(1024)S(1)}, u32[]{:S(2)}) copy-start(s32[8192]{0:T(1024)S(1)} %eq.25) | copy-start | bytes 98308
  141.1 124.4 %copy-start.2 = (s32[16384]{0:T(1024)}, s32[16384]{0:T(1024)S(1)}, u32[]{:S(2)}) copy-start(s32[16384]{0:T(1024)S(1)} %pad_clamp_fusion.1) | copy-start | bytes 196612
  141.1 124.4 %copy-start.12 = (pred[16352]{0:T(1024)(128)(4,1)S(1)}, pred[16352]{0:T(1024)(128)(4,1)}, u32[]{:S(2)}) copy-start(pred[16352]{0:T(1024)(128)(4,1)} %get-tuple-element.11) | copy-start | bytes 49060
  1543.1 10.4 copy-start.18
  1543.1 19.3 copy-start.17
  1543.1 20.1 copy-start.5
  1543.1 857.1 %all-to-all-start.1 = ((bf16[8,4,511,2048]{3,1,2,0:T(4,128)(2,1)}), bf16[8,4,511,2048]{3,1,2,0:T(4,128)(2,1)}, u32[]{:S(2)}, u32[]{:S(2)}) async-start(bf16[8,4,511,2048]{3,1,2,0:T(4,128)(2,1)} %copy.39), calls=%async_computation.1 | async-start | bytes 133955584 | tf_op jit(solution)/shard_map/all_to_all | solution.py:72
  1553.5 8.4 collective-permute-start
  1562.2 646.3 %copy-start = (f32[1024,8]{1,0:T(8,128)}, f32[1024,8]{1,0:T(8,128)S(1)}, u32[]{:S(2)}) copy-start(f32[1024,8]{1,0:T(8,128)S(1)} %copy.31) | copy-start | bytes 98308
  2208.5 65.4 %copy-start.16 = (pred[8,4,511]{2,1,0:T(4,128)(4,1)S(1)}, pred[8,4,511]{2,1,0:T(4,128)(4,1)}, u32[]{:S(2)}) copy-start(pred[8,4,511]{2,1,0:T(4,128)(4,1)} %broadcast_in_dim.64) | copy-start | bytes 49060
  2400.2 755.7 %all-to-all-start.2 = ((bf16[8,4,511,2048]{3,1,2,0:T(4,128)(2,1)}), bf16[8,4,511,2048]{3,1,2,0:T(4,128)(2,1)}, u32[]{:S(2)}, u32[]{:S(2)}) async-start(bf16[8,4,511,2048]{3,1,2,0:T(4,128)(2,1)} %copy.42), calls=%async_computation.2 | async-start | bytes 133955584 | tf_op jit(solution)/shard_map/all_to_all | solution.py:69
  2455.4 65.3 %copy-start.8 = (s32[8192]{0:T(1024)S(1)}, s32[8192]{0:T(1024)}, u32[]{:S(2)}) copy-start(s32[8192]{0:T(1024)} %get-tuple-element.14) | copy-start | bytes 98308
  2520.7 191.2 %copy-start.1 = (f32[1024,8]{1,0:T(8,128)S(1)}, f32[1024,8]{1,0:T(8,128)}, u32[]{:S(2)}) copy-start(f32[1024,8]{1,0:T(8,128)} %copy-done) | copy-start | bytes 98308
  2520.7 191.2 %copy-start.14 = (pred[8192]{0:T(1024)(128)(4,1)S(1)}, pred[8192]{0:T(1024)(128)(4,1)}, u32[]{:S(2)}) copy-start(pred[8192]{0:T(1024)(128)(4,1)} %compare_and_fusion.2) | copy-start | bytes 24580
  2712.0 127.9 %copy-start.3 = (s32[16384]{0:T(1024)S(1)}, s32[16384]{0:T(1024)}, u32[]{:S(2)}) copy-start(s32[16384]{0:T(1024)} %copy-done.2) | copy-start | bytes 196612
  2747.0 92.9 %collective-permute-start.3 = (bf16[1024,2048]{1,0:T(8,128)(2,1)}, bf16[1024,2048]{1,0:T(8,128)(2,1)}, u32[]{:S(2)}, u32[]{:S(2)}) collective-permute-start(bf16[1024,2048]{1,0:T(8,128)(2,1)} %bitcast.201), channel_id=1, source_target_pairs={{0,8},{8,0},{1,9},{9,1},{2,10},{10,2},{3,11},{11,3},{4,12},{12,4},... | collective-permute-start | bytes 12582920 | tf_op jit(solution)/shard_map/ppermute | solution.py:79
  2839.9 124.5 %copy-start.13 = (pred[16352]{0:T(1024)(128)(4,1)S(1)}, pred[16352]{0:T(1024)(128)(4,1)}, u32[]{:S(2)}) copy-start(pred[16352]{0:T(1024)(128)(4,1)} %get-tuple-element.11) | copy-start | bytes 49060
  3155.9 732.2 %all-to-all-start.3 = ((bf16[8,4,511,2048]{3,1,2,0:T(4,128)(2,1)}), bf16[8,4,511,2048]{3,1,2,0:T(4,128)(2,1)}, u32[]{:S(2)}, u32[]{:S(2)}) async-start(bf16[8,4,511,2048]{3,1,2,0:T(4,128)(2,1)} %copy.44), calls=%async_computation.3 | async-start | bytes 133955584 | tf_op jit(solution)/shard_map/all_to_all | solution.py:69
  4323.3 732.2 %all-to-all-start.4 = ((bf16[8,4,511,2048]{3,1,2,0:T(4,128)(2,1)}), bf16[8,4,511,2048]{3,1,2,0:T(4,128)(2,1)}, u32[]{:S(2)}, u32[]{:S(2)}) async-start(bf16[8,4,511,2048]{3,1,2,0:T(4,128)(2,1)} %copy.47), calls=%async_computation.4 | async-start | bytes 133955584 | tf_op jit(solution)/shard_map/all_to_all | solution.py:72
  5099.9 65.5 %copy-start.9 = (s32[8192]{0:T(1024)S(1)}, s32[8192]{0:T(1024)}, u32[]{:S(2)}) copy-start(s32[8192]{0:T(1024)} %get-tuple-element.14) | copy-start | bytes 98308
  5165.5 191.2 %copy-start.15 = (pred[8192]{0:T(1024)(128)(4,1)S(1)}, pred[8192]{0:T(1024)(128)(4,1)}, u32[]{:S(2)}) copy-start(pred[8192]{0:T(1024)(128)(4,1)} %compare_and_fusion.2) | copy-start | bytes 24580
  5381.4 89.8 %collective-permute-start.4 = (bf16[1024,2048]{1,0:T(8,128)(2,1)}, bf16[1024,2048]{1,0:T(8,128)(2,1)}, u32[]{:S(2)}, u32[]{:S(2)}) collective-permute-start(bf16[1024,2048]{1,0:T(8,128)(2,1)} %bitcast_reduce_fusion), channel_id=1, source_target_pairs={{8,0},{0,8},{9,1},{1,9},{10,2},{2,10},{11,3},{3,11},{12,4},{4,12},... | collective-permute-start | bytes 12582920 | tf_op jit(solution)/shard_map/ppermute | solution.py:84
  (4 other events, 21.8 us)
where the time goes:
time: 5500 us; the launch traced here: 5480 us
  local copies, waits for them, and re-layouts  2230 us (41%)
  waiting for transfers between devices  1380 us (25%)
  matrix products  859 us (16%)
  blocking collectives  740 us (13%)
  other arithmetic  226 us (4%)
    gather x6, local copies, waits for them, and re-layouts, take_rows(): return jnp.take(row_table, row_ids, axis=0, mode='fill', fill_value=0)  1330 us
    all_to_all x1, blocking collectives, dispatch(): return lax.all_to_all(send_buf, 'expert', 0, 0)  740 us
    all_to_all x2, waiting for transfers between devices, dispatch(): return lax.all_to_all(send_buf, 'expert', 0, 0)  616 us
    all_to_all x2, waiting for transfers between devices, combine(): lax.all_to_all(buf_rows, 'expert', 0, 0)  533 us
    reshape x4, local copies, waits for them, and re-layouts, dispatch(): take_rows(row_src, row_ids).reshape(n_dev, n_local, capacity, model_dim)  294 us
    dot_general x1, matrix products, expert_backward(): jnp.einsum('pecf,pecd->efd', hidden, d_buf, preferred_element_type=jnp.fl...  140 us
    select_n x4, other arithmetic, take_rows(): return jnp.take(row_table, row_ids, axis=0, mode='fill', fill_value=0)  133 us
    reshape x2, local copies, waits for them, and re-layouts, combine(): lax.all_to_all(buf_rows, 'expert', 0, 0)  131 us
  transfers between devices with their start and end apart: 9, of which 5 were waited for; matrix products, arithmetic and copies ran while one was open for 34% of the time, Pallas kernels for 0%

commit v1 on v0

v1 whole, which is shorter than its diff:
```python
import functools

import jax
import jax.numpy as jnp
from jax import lax
from jax.experimental import pallas as pl
from jax.experimental.pallas import tpu as pltpu
from jax.sharding import PartitionSpec as P


F32 = jnp.float32
BF16 = jnp.bfloat16
FWD_CHUNKS = (256, 256, 512)
BWD_CHUNKS = (512, 384, 128)
TILE_F = 256
TILE_A = 128
VMEM_LIMIT = 64000 * 1024


def dot(lhs, rhs):
    return jnp.dot(lhs, rhs, preferred_element_type=F32)


def dot_t(lhs, rhs):
    return lax.dot_general(lhs, rhs, (((1,), (1,)), ((), ())), preferred_element_type=F32)


def dot_a(lhs, rhs):
    return lax.dot_general(lhs, rhs, (((0,), (0,)), ((), ())), preferred_element_type=F32)


def gate_column(gates, expert):
    lanes = lax.broadcasted_iota(jnp.int32, gates.shape, 1)
    return jnp.sum(jnp.where(lanes == expert, gates, 0.0), axis=1, keepdims=True)


def params(semantics):
    return pltpu.CompilerParams(dimension_semantics=semantics, vmem_limit_bytes=VMEM_LIMIT)


def fwd_body(ffn, n_local, first_ref, x_ref, g_ref, w13_ref, w2_ref, y_ref):
    gates = g_ref[0]
    for e in range(n_local):
        gate = gate_column(gates, first_ref[0] + e)
        pre = dot(x_ref[0], w13_ref[e])
        one, three = pre[:, :ffn], pre[:, ffn:]
        hidden = jnp.where(gate > 0.0, one * jax.nn.sigmoid(one) * three, 0.0).astype(BF16)
        out = gate * dot(hidden, w2_ref[e]).astype(BF16).astype(F32)
        if e == 0:
            y_ref[0] = out
        else:
            y_ref[0] += out


def expert_fwd(first, x, gates, w13, w2, start):
    n_src, rows, model = x.shape
    n_local, ffn = w2.shape[:2]
    tile = min(TILE_F, rows)
    steps = rows // tile
    n_exp = gates.shape[2]
    flops = 2 * n_src * rows * n_local * model * ffn * 3
    return pl.pallas_call(
        functools.partial(fwd_body, ffn, n_local),
        grid_spec=pltpu.PrefetchScalarGridSpec(
            num_scalar_prefetch=1,
            grid=(n_src, steps),
            in_specs=[
                pl.BlockSpec((1, tile, model), lambda s, t, _: (s, t, 0)),
                pl.BlockSpec((1, tile, n_exp), lambda s, t, _: (s, start // tile + t, 0)),
                pl.BlockSpec(w13.shape, lambda s, t, _: (0, 0, 0), pipeline_mode=pl.Buffered(1)),
                pl.BlockSpec(w2.shape, lambda s, t, _: (0, 0, 0), pipeline_mode=pl.Buffered(1)),
            ],
            out_specs=pl.BlockSpec((1, tile, model), lambda s, t, _: (s, t, 0)),
        ),
        out_shape=jax.ShapeDtypeStruct((n_src, rows, model), F32),
        compiler_params=params(('arbitrary', 'arbitrary')),
        cost_estimate=pl.CostEstimate(flops=flops, bytes_accessed=n_src * rows * model * 6, transcendentals=0),
        name='expert_fwd',
    )(first, x, gates, w13, w2)


def bwd_body(ffn, n_local, first_ref, x_ref, dy_ref, g_ref, w13_ref, w2_ref, *refs):
    dx_ref, da_ref, h_ref = refs[-3:]
    gates = g_ref[0]
    for e in range(n_local):
        gate = gate_column(gates, first_ref[0] + e)
        live = gate > 0.0
        pre = dot(x_ref[0], w13_ref[e])
        one, three = pre[:, :ffn], pre[:, ffn:]
        sig = jax.nn.sigmoid(one)
        act = one * sig
        h_ref[0, :, e * ffn:(e + 1) * ffn] = jnp.where(live, act * three, 0.0).astype(BF16)
        d_out = (gate * dy_ref[0].astype(F32)).astype(BF16)
        d_hid = dot_t(d_out, w2_ref[e]).astype(BF16).astype(F32)
        d_one = jnp.where(live, d_hid * three * sig * (1.0 + one * (1.0 - sig)), 0.0).astype(BF16)
        d_three = jnp.where(live, d_hid * act, 0.0).astype(BF16)
        d_pre = jnp.concatenate([d_one, d_three], axis=1)
        da_ref[0, :, 2 * e * ffn:2 * (e + 1) * ffn] = d_pre
        dx = dot_t(d_pre, w13_ref[e]).astype(BF16).astype(F32)
        if e == 0:
            dx_ref[0] = dx
        else:
            dx_ref[0] += dx


def expert_bwd(first, x, dy, gates, w13, w2, start, dy_start, rows, carried):
    n_src, n_tok, model = x.shape
    n_local, ffn = w2.shape[:2]
    tile = min(TILE_A, rows)
    steps, base = rows // tile, start // tile
    n_exp = gates.shape[2]
    flops = 2 * n_src * rows * n_local * model * ffn * 5
    at = lambda s, t, _: (s, base + t, 0)
    in_specs = [
        pl.BlockSpec((1, tile, model), at),
        pl.BlockSpec((1, tile, model), lambda s, t, _: (s, dy_start // tile + t, 0)),
        pl.BlockSpec((1, tile, n_exp), at),
        pl.BlockSpec(w13.shape, lambda s, t, _: (0, 0, 0), pipeline_mode=pl.Buffered(1)),
        pl.BlockSpec(w2.shape, lambda s, t, _: (0, 0, 0), pipeline_mode=pl.Buffered(1)),
    ]
    operands = [x, dy, gates, w13, w2]
    aliases = {}
    if carried is not None:
        in_specs += [pl.BlockSpec(memory_space=pl.ANY)] * 2
        operands += list(carried)
        aliases = {6: 1, 7: 2}
    return pl.pallas_call(
        functools.partial(bwd_body, ffn, n_local),
        grid_spec=pltpu.PrefetchScalarGridSpec(
            num_scalar_prefetch=1,
            grid=(n_src, steps),
            in_specs=in_specs,
            out_specs=[
                pl.BlockSpec((1, tile, model), lambda s, t, _: (s, t, 0)),
                pl.BlockSpec((1, tile, 2 * ffn * n_local), at),
                pl.BlockSpec((1, tile, ffn * n_local), at),
            ],
        ),
        out_shape=[
            jax.ShapeDtypeStruct((n_src, rows, model), F32),
            jax.ShapeDtypeStruct((n_src, n_tok, 2 * ffn * n_local), BF16),
            jax.ShapeDtypeStruct((n_src, n_tok, ffn * n_local), BF16),
        ],
        input_output_aliases=aliases,
        compiler_params=params(('arbitrary', 'arbitrary')),
        cost_estimate=pl.CostEstimate(flops=flops, bytes_accessed=n_src * rows * model * 14, transcendentals=0),
        name='expert_bwd',
    )(first, *operands)


def grad_body(ffn, first_ref, x_ref, lo_ref, hi_ref, g_ref, da_ref, h_ref, dw1_ref, dw3_ref, dw2_ref, acc13_ref, acc2_ref):
    e, k = pl.program_id(0), pl.program_id(1)
    half = lo_ref.shape[1]

    @pl.when(k == 0)
    def _():
        acc13_ref[...] = jnp.zeros_like(acc13_ref)
        acc2_ref[...] = jnp.zeros_like(acc2_ref)

    acc13_ref[...] += dot_a(x_ref[0], da_ref[0])
    gate = gate_column(g_ref[0], first_ref[0] + e)
    for part, dy_ref in enumerate((lo_ref, hi_ref)):
        rows = slice(part * half, (part + 1) * half)
        d_out = (gate[rows] * dy_ref[0].astype(F32)).astype(BF16)
        acc2_ref[...] += dot_a(h_ref[0, rows], d_out)

    @pl.when(k == pl.num_programs(1) - 1)
    def _():
        dw1_ref[0] = acc13_ref[:, :ffn].astype(BF16)
        dw3_ref[0] = acc13_ref[:, ffn:].astype(BF16)
        dw2_ref[0] = acc2_ref[...].astype(BF16)


def weight_grads(first, x, dy_lo, dy_hi, gates, d_pre, hidden, n_local):
    n_src, n_tok, model = x.shape
    ffn = hidden.shape[2] // n_local
    half = dy_lo.shape[1]
    n_exp = gates.shape[2]
    flops = 2 * n_src * n_tok * n_local * model * ffn * 3
    at = lambda e, k, _: (k, 0, 0)
    at_e = lambda e, k, _: (k, 0, e)
    out = lambda e, k, _: (e, 0, 0)
    return pl.pallas_call(
        functools.partial(grad_body, ffn),
        grid_spec=pltpu.PrefetchScalarGridSpec(
            num_scalar_prefetch=1,
            grid=(n_local, n_src),
            in_specs=[
                pl.BlockSpec((1, n_tok, model), at),
                pl.BlockSpec((1, half, model), at),
                pl.BlockSpec((1, half, model), at),
                pl.BlockSpec((1, n_tok, n_exp), at),
                pl.BlockSpec((1, n_tok, 2 * ffn), at_e),
                pl.BlockSpec((1, n_tok, ffn), at_e),
            ],
            out_specs=[
                pl.BlockSpec((1, model, ffn), out),
                pl.BlockSpec((1, model, ffn), out),
                pl.BlockSpec((1, ffn, model), out),
            ],
            scratch_shapes=[pltpu.VMEM((model, 2 * ffn), F32), pltpu.VMEM((ffn, model), F32)],
        ),
        out_shape=[
            jax.ShapeDtypeStruct((n_local, model, ffn), BF16),
            jax.ShapeDtypeStruct((n_local, model, ffn), BF16),
            jax.ShapeDtypeStruct((n_local, ffn, model), BF16),
        ],
        compiler_params=params(('arbitrary', 'arbitrary')),
        cost_estimate=pl.CostEstimate(flops=flops, bytes_accessed=n_src * n_tok * model * 4 * n_local, transcendentals=0),
        name='weight_grads',
    )(first, x, dy_lo, dy_hi, gates, d_pre, hidden)


def solution(mesh):
    n_stage = mesh.shape['stage']
    n_dev = mesh.shape['expert']
    to_next = [(stage_idx, (stage_idx + 1) % n_stage) for stage_idx in range(n_stage)]
    to_prev = [((stage_idx + 1) % n_stage, stage_idx) for stage_idx in range(n_stage)]
    tok_spec = P('stage', 'expert', None)
    w_spec = P('stage', 'expert', None, None)

    def moe_body(x_act, route_idx, route_wts, w_one, w_three, w_two, dy_act):
        x_src = x_act[0]
        n_tok, _ = x_src.shape
        n_local = w_one.shape[1]
        n_exp = n_local * n_dev
        first = (lax.axis_index('expert') * n_local).astype(jnp.int32).reshape(1)

        hits = route_idx[0][:, :, None] == jnp.arange(n_exp, dtype=jnp.int32)
        gate_src = jnp.sum(jnp.where(hits, route_wts[0][:, :, None], 0.0), axis=1)
        gate_dst = lax.ppermute(gate_src, 'stage', to_next)
        gates = lax.all_gather(gate_dst, 'expert', axis=0, tiled=False)

        w13 = jnp.concatenate([w_one[0], w_three[0]], axis=2)
        w2 = w_two[0]

        half = n_tok // 2
        dy_lo = lax.all_gather(dy_act[0, :half], 'expert', axis=0, tiled=False)

        y_parts = []
        start = 0
        y_part = None
        for rows in FWD_CHUNKS:
            x_dst = lax.ppermute(x_src[start:start + rows], 'stage', to_next)
            x_all = lax.all_gather(x_dst, 'expert', axis=0, tiled=False)
            if y_part is None:
                x_first = x_all
            else:
                x_all, _ = lax.optimization_barrier((x_all, y_part))
            y_part = expert_fwd(first, x_all, gates, w13, w2, start)
            y_parts.append(lax.psum_scatter(y_part, 'expert', scatter_dimension=0, tiled=False).astype(BF16))
            start += rows
        y_out = jnp.concatenate(y_parts, axis=0)

        dy_hi = lax.all_gather(dy_act[0, half:], 'expert', axis=0, tiled=False)
        x_again, _ = lax.optimization_barrier((x_src, x_first))
        x_dst = lax.ppermute(x_again, 'stage', to_next)
        x_all = lax.all_gather(x_dst, 'expert', axis=0, tiled=False)
        x_all, _ = lax.optimization_barrier((x_all, y_part))

        dx_parts = []
        carried = None
        start = 0
        for rows in BWD_CHUNKS:
            dx_part, d_pre, hidden = expert_bwd(first, x_all, dy_lo if start < half else dy_hi, gates, w13, w2, start, start % half, rows, carried)
            carried = (d_pre, hidden)
            dx_dst = lax.psum_scatter(dx_part, 'expert', scatter_dimension=0, tiled=False).astype(BF16)
            dx_parts.append(lax.ppermute(dx_dst, 'stage', to_prev))
            start += rows
        dx_out = jnp.concatenate(dx_parts, axis=0)

        g_one, g_three, g_two = weight_grads(first, x_all, dy_lo, dy_hi, gates, d_pre, hidden, n_local)
        return y_out[None], dx_out[None], g_one[None], g_three[None], g_two[None]

    return jax.shard_map(moe_body, mesh=mesh, in_specs=(tok_spec, tok_spec, tok_spec, w_spec, w_spec, w_spec, tok_spec), out_specs=(tok_spec, tok_spec, w_spec, w_spec, w_spec), check_vma=False)
```

time: 5500 us -> 1790 us (0.33)
  local copies, waits for them, and re-layouts: 2230 us -> 15.8 us
  Pallas kernels: 0 us -> 1240 us
  waiting for transfers between devices: 1380 us -> 463 us
  matrix products: 859 us -> 0 us
  blocking collectives: 740 us -> 0 us
  other arithmetic: 226 us -> 36.9 us
    gather x6 -> x0, local copies, waits for them, and re-layouts: 1330 us -> none  [take_rows(): return jnp.take(row_table, row_ids, axis=0, mode='fill', fill_value=0)]
    pallas_call x0 -> x7, Pallas kernels: none -> 1240 us  [the longest x3 745 us: expert_bwd(): pl.pallas_call(functools.partial(bwd_body, ffn, n_local), grid_spec=pltpu...]
    all_to_all x4 -> x0, waiting for transfers between devices: 1150 us -> none  [the longest x2 616 us: dispatch(): return lax.all_to_all(send_buf, 'expert', 0, 0)]
    dot_general x11 -> x0, matrix products: 859 us -> none  [the longest x1 140 us: expert_backward(): jnp.einsum('pecf,pecd->efd', hidden, d_buf, preferred_element_type=jnp.fl...]
    all_to_all x1 -> x0, blocking collectives: 740 us -> none  [dispatch(): return lax.all_to_all(send_buf, 'expert', 0, 0)]
    reshape x6 -> x0, local copies, waits for them, and re-layouts: 425 us -> none  [the longest x4 294 us: dispatch(): take_rows(row_src, row_ids).reshape(n_dev, n_local, capacity, model_dim)]
    reduce_scatter x0 -> x6, waiting for transfers between devices: none -> 269 us  [the longest x3 239 us: moe_body(): lax.psum_scatter(dx_part, 'expert', scatter_dimension=0, tiled=False)]
    all_to_all x3 -> x0, local copies, waits for them, and re-layouts: 190 us -> none  [the longest x1 101 us: dispatch(): return lax.all_to_all(send_buf, 'expert', 0, 0)]
  transfers between devices with their start and end apart: 9 -> 21, of which waited for: 5 -> 9; matrix products, arithmetic and copies ran while one was open for 34% -> 2% of each run, Pallas kernels for 0% -> 70%
where the time goes in v1:
time: 1790 us; the launch traced here: 1780 us
  Pallas kernels  1240 us (69%)
  waiting for transfers between devices  463 us (26%)
  other arithmetic  36.9 us (2%)
    pallas_call x3, Pallas kernels, expert_bwd(): pl.pallas_call(functools.partial(bwd_body, ffn, n_local), grid_spec=pltpu...  745 us
    pallas_call x3, Pallas kernels, expert_fwd(): pl.pallas_call(functools.partial(fwd_body, ffn, n_local), grid_spec=pltpu...  258 us
    reduce_scatter x3, waiting for transfers between devices, moe_body(): lax.psum_scatter(dx_part, 'expert', scatter_dimension=0, tiled=False)  239 us
    pallas_call x1, Pallas kernels, weight_grads(): pl.pallas_call(functools.partial(grad_body, ffn), grid_spec=pltpu.Prefetc...  236 us
    ppermute x1, waiting for transfers between devices, moe_body(): x_dst = lax.ppermute(x_again, 'stage', to_next)  88 us
    ppermute x3, waiting for transfers between devices, moe_body(): x_dst = lax.ppermute(x_src[start:start + rows], 'stage', to_next)  87.9 us
  transfers between devices with their start and end apart: 21, of which 9 were waited for; matrix products, arithmetic and copies ran while one was open for 2% of the time, Pallas kernels for 70%

profile of v1, /device:TPU:0, one launch (start us, length us, event | category | flops | bytes accessed | tf_op | source)
XLA Modules:
  0.0 1781.7 jit_solution(11512932425342762978)
XLA Ops:
  8.9 3.3 collective-permute-start
  12.2 23.2 %collective-permute-done = bf16[256,2048]{1,0:T(8,128)(2,1)S(1)} collective-permute-done((bf16[256,2048]{1,0:T(8,128)(2,1)S(1)}, bf16[256,2048]{1,0:T(8,128)(2,1)S(1)}, u32[]{:S(2)}, u32[]{:S(2)}) %collective-permute-start) | collective-permute-done | bytes 1048608 | tf_op jit(solution)/shard_map/ppermute | solution.py:244
  38.3 3.2 collective-permute-done.1
  44.1 21.4 %collective-permute-done.2 = bf16[256,2048]{1,0:T(8,128)(2,1)S(1)} collective-permute-done((bf16[256,2048]{1,0:T(8,128)(2,1)S(1)}, bf16[256,2048]{1,0:T(8,128)(2,1)S(1)}, u32[]{:S(2)}, u32[]{:S(2)}) %collective-permute-start.2) | collective-permute-done | bytes 1048608 | tf_op jit(solution)/shard_map/ppermute | solution.py:244
  69.8 43.3 %collective-permute-done.3 = bf16[512,2048]{1,0:T(8,128)(2,1)S(1)} collective-permute-done((bf16[512,2048]{1,0:T(8,128)(2,1)S(1)}, bf16[512,2048]{1,0:T(8,128)(2,1)S(1)}, u32[]{:S(2)}, u32[]{:S(2)}) %collective-permute-start.3) | collective-permute-done | bytes 2097184 | tf_op jit(solution)/shard_map/ppermute | solution.py:244
  115.7 88.0 %collective-permute-done.4 = bf16[1024,2048]{1,0:T(8,128)(2,1)} collective-permute-done((bf16[1024,2048]{1,0:T(8,128)(2,1)}, bf16[1024,2048]{1,0:T(8,128)(2,1)}, u32[]{:S(2)}, u32[]{:S(2)}) %collective-permute-start.4) | collective-permute-done | bytes 4194336 | tf_op jit(solution)/shard_map/ppermute | solution.py:257
  203.8 4.8 fusion
  209.5 14.2 pad_maximum_fusion.w13_ref
  223.6 3.7 copy.20
  227.3 66.8 %expert_fwd.3 = f32[8,256,2048]{2,1,0:T(8,128)} custom-call(s32[1]{0:T(128)} %bitcast.first_ref, bf16[8,256,2048]{2,1,0:T(8,128)(2,1)} %bitcast.60, f32[8,1024,32]{2,1,0:T(8,128)} %bitcast.41, bf16[4,2048,1024]{2,1,0:T(8,128)(2,1)} %pad_maximum_fusion.w13_ref, bf16[4,512,2048]{2,1,0:T(8,128)(2,1)} %bitcast.50), custom_call_target="tpu_custom_call" | custom-call | flops 51539607552 | bytes 25165824 | tf_op jit(solution)/shard_map/expert_fwd/pallas_call | solution.py:62
  294.3 66.7 %expert_fwd.4 = f32[8,256,2048]{2,1,0:T(8,128)} custom-call(s32[1]{0:T(128)} %bitcast.first_ref, bf16[8,256,2048]{2,1,0:T(8,128)(2,1)} %bitcast.61, f32[8,1024,32]{2,1,0:T(8,128)} %bitcast.42, bf16[4,2048,1024]{2,1,0:T(8,128)(2,1)} %pad_maximum_fusion.w13_ref, bf16[4,512,2048]{2,1,0:T(8,128)(2,1)} %bitcast.51), custom_call_target="tpu_custom_call" | custom-call | flops 51539607552 | bytes 25165824 | tf_op jit(solution)/shard_map/expert_fwd/pallas_call | solution.py:62
  361.1 124.1 %expert_fwd.5 = f32[8,512,2048]{2,1,0:T(8,128)} custom-call(s32[1]{0:T(128)} %bitcast.first_ref, bf16[8,512,2048]{2,1,0:T(8,128)(2,1)} %bitcast.59, f32[8,1024,32]{2,1,0:T(8,128)} %bitcast.43, bf16[4,2048,1024]{2,1,0:T(8,128)(2,1)} %pad_maximum_fusion.w13_ref, bf16[4,512,2048]{2,1,0:T(8,128)(2,1)} %bitcast.52), custom_call_target="tpu_custom_call" | custom-call | flops 103079215104 | bytes 50331648 | tf_op jit(solution)/shard_map/expert_fwd/pallas_call | solution.py:62
  485.2 12.8 all-gather.13.cloned.1.call-done.dy_ref.lo_ref
  498.0 365.4 %expert_bwd.3 = (f32[8,512,2048]{2,1,0:T(8,128)}, bf16[8,1024,4096]{2,1,0:T(8,128)(2,1)}, bf16[8,1024,2048]{2,1,0:T(8,128)(2,1)}) custom-call(s32[1]{0:T(128)} %bitcast.first_ref, bf16[8,1024,2048]{2,1,0:T(8,128)(2,1)} %bitcast.37, bf16[8,512,2048]{2,1,0:T(8,128)(2,1)} %all-gather.13.cloned.1.call-done.dy_ref.lo_ref, f32[8,1024,32]{2,1,0:T(8,128)} %bitcast.44, ...), custom_call_target="tpu_custom_call" | custom-call | flops 171798691840 | bytes 117440512 | tf_op jit(solution)/shard_map/expert_bwd/pallas_call | solution.py:127
  863.4 276.2 %expert_bwd.4 = (f32[8,384,2048]{2,1,0:T(8,128)}, bf16[8,1024,4096]{2,1,0:T(8,128)(2,1)}, bf16[8,1024,2048]{2,1,0:T(8,128)(2,1)}) custom-call(s32[1]{0:T(128)} %bitcast.first_ref, bf16[8,1024,2048]{2,1,0:T(8,128)(2,1)} %bitcast.38, bf16[8,512,2048]{2,1,0:T(8,128)(2,1)} %all-gather.15.cloned.1.call-done.dy_ref.hi_ref, ...), custom_call_target="tpu_custom_call", output_to_operand_aliasing={{1}: (6, {}), {2}: (7, {})} | custom-call | flops 128849018880 | bytes 88080384 | tf_op jit(solution)/shard_map/expert_bwd/pallas_call | solution.py:127
  1140.5 103.0 %expert_bwd.5 = (f32[8,128,2048]{2,1,0:T(8,128)}, bf16[8,1024,4096]{2,1,0:T(8,128)(2,1)}, bf16[8,1024,2048]{2,1,0:T(8,128)(2,1)}) custom-call(s32[1]{0:T(128)} %bitcast.first_ref, bf16[8,1024,2048]{2,1,0:T(8,128)(2,1)} %bitcast.39, bf16[8,512,2048]{2,1,0:T(8,128)(2,1)} %all-gather.15.cloned.1.call-done.dy_ref.hi_ref, ...), custom_call_target="tpu_custom_call", output_to_operand_aliasing={{1}: (6, {}), {2}: (7, {})} | custom-call | flops 42949672960 | bytes 29360128 | tf_op jit(solution)/shard_map/expert_bwd/pallas_call | solution.py:127
  1244.3 2.8 convert_bitcast_fusion.4
  1249.9 40.5 %reduce-scatter.15.cloned.1.call-done = f32[1,384,2048]{2,1,0:T(8,128)} async-done(((f32[8,384,2048]{2,1,0:T(8,128)}), f32[1,384,2048]{2,1,0:T(8,128)}) %reduce-scatter.15.cloned.1.call-update) | async-done | bytes 3145744 | tf_op jit(solution)/shard_map/reduce_scatter | solution.py:267
  1290.3 3.3 convert_bitcast_fusion.2
  1295.1 198.6 %reduce-scatter.13.cloned.1.call-done = f32[1,512,2048]{2,1,0:T(8,128)} async-done(((f32[8,512,2048]{2,1,0:T(8,128)}), f32[1,512,2048]{2,1,0:T(8,128)}) %reduce-scatter.13.cloned.1.call-update) | async-done | bytes 4194320 | tf_op jit(solution)/shard_map/reduce_scatter | solution.py:267
  1493.8 3.8 convert_bitcast_fusion
  1499.1 236.2 %weight_grads.1 = (bf16[4,2048,512]{2,1,0:T(8,128)(2,1)}, bf16[4,2048,512]{2,1,0:T(8,128)(2,1)}, bf16[4,512,2048]{2,1,0:T(8,128)(2,1)}) custom-call(s32[1]{0:T(128)} %bitcast.first_ref, bf16[8,1024,2048]{2,1,0:T(8,128)(2,1)} %bitcast.40, bf16[8,512,2048]{2,1,0:T(8,128)(2,1)} %all-gather.13.cloned.1.call-done.dy_ref.lo_ref, ...), custom_call_target="tpu_custom_call" | custom-call | flops 206158430208 | bytes 268435456 | tf_op jit(solution)/shard_map/weight_grads/pallas_call | solution.py:183
  1736.9 29.5 %reduce-scatter.11.cloned.1.call-done = f32[1,512,2048]{2,1,0:T(8,128)} async-done(((f32[8,512,2048]{2,1,0:T(8,128)}), f32[1,512,2048]{2,1,0:T(8,128)}) %reduce-scatter.11.cloned.1.call-update) | async-done | bytes 4194320 | tf_op jit(solution)/shard_map/reduce_scatter | solution.py:251
  1771.2 3.7 maximum_bitcast_fusion.1
  (68 shorter events, 28.8 us)
Async XLA Ops:
  7.2 29.3 %copy-start.6 = (f32[1,1024,8]{1,2,0:T(8,128)S(1)}, f32[1,1024,8]{1,2,0:T(8,128)}, u32[]{:S(2)}) copy-start(f32[1,1024,8]{1,2,0:T(8,128)} %param.9) | copy-start | bytes 98308
  7.2 107.3 %all-gather.17.cloned.1.call-start = ((), (), s32[]{:S(2)}) async-start(), calls=%async_computation.14 | async-start | bytes 9437184 | tf_op jit(solution)/shard_map/all_gather | solution.py:245
  8.9 26.5 %collective-permute-start = (bf16[256,2048]{1,0:T(8,128)(2,1)S(1)}, bf16[256,2048]{1,0:T(8,128)(2,1)S(1)}, u32[]{:S(2)}, u32[]{:S(2)}) collective-permute-start(bf16[256,2048]{1,0:T(8,128)(2,1)S(1)} %get-tuple-element.39), channel_id=1, source_target_pairs={{0,8},{8,0},{1,9},{9,1},{2,10},{10,2},{3,11},{11,3},{4,12},{12,4},... | collective-permute-start | bytes 3145736 | tf_op jit(solution)/shard_map/ppermute | solution.py:244
  36.4 187.3 %all-gather.19.cloned.1.call-start = ((), (), s32[]{:S(2)}) async-start(), calls=%async_computation.15 | async-start | bytes 1179648 | tf_op jit(solution)/shard_map/all_gather | solution.py:232
  36.6 5.0 collective-permute-start.1
  42.3 252.1 %all-gather.21.cloned.1.call-start = ((), (), s32[]{:S(2)}) async-start(), calls=%async_computation.16 | async-start | bytes 9437184 | tf_op jit(solution)/shard_map/all_gather | solution.py:245
  42.3 23.2 %collective-permute-start.2 = (bf16[256,2048]{1,0:T(8,128)(2,1)S(1)}, bf16[256,2048]{1,0:T(8,128)(2,1)S(1)}, u32[]{:S(2)}, u32[]{:S(2)}) collective-permute-start(bf16[256,2048]{1,0:T(8,128)(2,1)S(1)} %get-tuple-element.40), channel_id=1, source_target_pairs={{0,8},{8,0},{1,9},{9,1},{2,10},{10,2},{3,11},{11,3},{4,12},{12,4},... | collective-permute-start | bytes 3145736 | tf_op jit(solution)/shard_map/ppermute | solution.py:244
  66.5 294.6 %all-gather.23.cloned.1.call-start = ((), (), s32[]{:S(2)}) async-start(), calls=%async_computation.17 | async-start | bytes 18874368 | tf_op jit(solution)/shard_map/all_gather | solution.py:245
  68.3 44.8 %collective-permute-start.3 = (bf16[512,2048]{1,0:T(8,128)(2,1)S(1)}, bf16[512,2048]{1,0:T(8,128)(2,1)S(1)}, u32[]{:S(2)}, u32[]{:S(2)}) collective-permute-start(bf16[512,2048]{1,0:T(8,128)(2,1)S(1)} %slice_bitcast_fusion), channel_id=1, source_target_pairs={{0,8},{8,0},{1,9},{9,1},{2,10},{10,2},{3,11},{11,3},{4,12},{12,4},... | collective-permute-start | bytes 6291464 | tf_op jit(solution)/shard_map/ppermute | solution.py:244
  114.5 370.8 %all-gather.25.cloned.1.call-start = ((), (), s32[]{:S(2)}) async-start(), calls=%async_computation.18 | async-start | bytes 37748736 | tf_op jit(solution)/shard_map/all_gather | solution.py:258
  114.5 89.2 %collective-permute-start.4 = (bf16[1024,2048]{1,0:T(8,128)(2,1)}, bf16[1024,2048]{1,0:T(8,128)(2,1)}, u32[]{:S(2)}, u32[]{:S(2)}) collective-permute-start(bf16[1024,2048]{1,0:T(8,128)(2,1)} %bitcast.56), channel_id=1, source_target_pairs={{0,8},{8,0},{1,9},{9,1},{2,10},{10,2},{3,11},{11,3},{4,12},{12,4},... | collective-permute-start | bytes 12582920 | tf_op jit(solution)/shard_map/ppermute | solution.py:257
  203.8 294.3 %all-gather.13.cloned.1.call-start = ((), (), s32[]{:S(2)}) async-start(), calls=%async_computation.9 | async-start | bytes 18874368 | tf_op jit(solution)/shard_map/all_gather | solution.py:238
  208.7 654.8 %all-gather.15.cloned.1.call-start = ((), (), s32[]{:S(2)}) async-start(), calls=%async_computation.11 | async-start | bytes 18874368 | tf_op jit(solution)/shard_map/all_gather | solution.py:255
  209.4 1034.9 %reduce-scatter.7.cloned.1.call-start = ((), (), s32[]{:S(2)}) async-start(), calls=%async_computation.6 | async-start | bytes 18874368 | tf_op jit(solution)/shard_map/reduce_scatter | solution.py:251
  294.1 953.1 %reduce-scatter.9.cloned.1.call-start = ((), (), s32[]{:S(2)}) async-start(), calls=%async_computation.7 | async-start | bytes 18874368 | tf_op jit(solution)/shard_map/reduce_scatter | solution.py:251
  361.0 929.3 %reduce-scatter.15.cloned.1.call-start = ((), (), s32[]{:S(2)}) async-start(), calls=%async_computation.12 | async-start | bytes 28311552 | tf_op jit(solution)/shard_map/reduce_scatter | solution.py:267
  1139.7 354.1 %reduce-scatter.13.cloned.1.call-start = ((), (), s32[]{:S(2)}) async-start(), calls=%async_computation.10 | async-start | bytes 37748736 | tf_op jit(solution)/shard_map/reduce_scatter | solution.py:267
  1140.5 594.8 %reduce-scatter.17.cloned.1.call-start = ((), (), s32[]{:S(2)}) async-start(), calls=%async_computation.13 | async-start | bytes 9437184 | tf_op jit(solution)/shard_map/reduce_scatter | solution.py:267
  1243.5 522.9 %reduce-scatter.11.cloned.1.call-start = ((), (), s32[]{:S(2)}) async-start(), calls=%async_computation.8 | async-start | bytes 37748736 | tf_op jit(solution)/shard_map/reduce_scatter | solution.py:251
  1293.7 477.6 %collective-permute-start.6 = (bf16[384,2048]{1,0:T(8,128)(2,1)}, bf16[384,2048]{1,0:T(8,128)(2,1)}, u32[]{:S(2)}, u32[]{:S(2)}) collective-permute-start(bf16[384,2048]{1,0:T(8,128)(2,1)} %convert_bitcast_fusion.2), channel_id=1, source_target_pairs={{8,0},{0,8},{9,1},{1,9},{10,2},{2,10},{11,3},{3,11},{12,4},{4,12},... | collective-permute-start | bytes 4718600 | tf_op jit(solution)/shard_map/ppermute | solution.py:268
  1497.6 273.6 %collective-permute-start.5 = (bf16[512,2048]{1,0:T(8,128)(2,1)}, bf16[512,2048]{1,0:T(8,128)(2,1)}, u32[]{:S(2)}, u32[]{:S(2)}) collective-permute-start(bf16[512,2048]{1,0:T(8,128)(2,1)} %convert_bitcast_fusion), channel_id=1, source_target_pairs={{8,0},{0,8},{9,1},{1,9},{10,2},{2,10},{11,3},{3,11},{12,4},{4,12},... | collective-permute-start | bytes 6291464 | tf_op jit(solution)/shard_map/ppermute | solution.py:268
  1735.3 33.7 %copy-start = (bf16[256,2048]{1,0:T(8,128)(2,1)S(1)}, bf16[256,2048]{1,0:T(8,128)(2,1)}, u32[]{:S(2)}) copy-start(bf16[256,2048]{1,0:T(8,128)(2,1)} %convert_bitcast_fusion.4) | copy-start | bytes 3145732
  1735.3 33.7 %copy-start.1 = (bf16[256,2048]{1,0:T(8,128)(2,1)S(1)}, bf16[256,2048]{1,0:T(8,128)(2,1)}, u32[]{:S(2)}) copy-start(bf16[256,2048]{1,0:T(8,128)(2,1)} %convert_bitcast_fusion.3) | copy-start | bytes 3145732
  1736.9 34.4 %collective-permute-start.7 = (bf16[128,2048]{1,0:T(8,128)(2,1)S(1)}, bf16[128,2048]{1,0:T(8,128)(2,1)S(1)}, u32[]{:S(2)}, u32[]{:S(2)}) collective-permute-start(bf16[128,2048]{1,0:T(8,128)(2,1)S(1)} %convert_bitcast_fusion.5), channel_id=1, source_target_pairs={{8,0},{0,8},{9,1},{1,9},{10,2},{2,10},{11,3},{3,11},{12,4},{4,12},... | collective-permute-start | bytes 1572872 | tf_op jit(solution)/shard_map/ppermute | solution.py:268
  (5 other events, 33.2 us)
Sparse Core Ops, SparseCore 0:
  36.5 51.7 all-gather.16
  90.2 19.6 all-gather.18
  112.2 50.4 all-gather.20
  165.1 85.9 all-gather.22
  252.8 156.9 all-gather.24
  412.0 85.9 all-gather.12
  500.5 85.9 all-gather.14
  590.0 110.5 reduce-scatter.6
  704.1 110.5 reduce-scatter.8
  1139.8 150.4 reduce-scatter.14
  1293.9 199.8 reduce-scatter.12
  1497.1 65.8 reduce-scatter.16
  1566.5 199.8 reduce-scatter.10

commit v2 on v0

v2 whole, which is shorter than its diff:
```python
import functools

import jax
import jax.numpy as jnp
from jax import lax
from jax.experimental import pallas as pl
from jax.experimental.pallas import tpu as pltpu
from jax.sharding import PartitionSpec as P


F32 = jnp.float32
BF16 = jnp.bfloat16
FWD_CHUNKS = (256, 768)
BWD_CHUNKS = (512, 256, 256)
TILE_F = 256
TILE_A = 512
VMEM_LIMIT = 65400 * 1024
N_ACC = 3
CORES = 2
MESH = pl.DeviceIdType.MESH


def dot(lhs, rhs):
    return jnp.dot(lhs, rhs, preferred_element_type=F32)


def dot_t(lhs, rhs):
    return lax.dot_general(lhs, rhs, (((1,), (1,)), ((), ())), preferred_element_type=F32)


def dot_a(lhs, rhs):
    return lax.dot_general(lhs, rhs, (((0,), (0,)), ((), ())), preferred_element_type=F32)


def gate_column(gates, expert):
    lanes = lax.broadcasted_iota(jnp.int32, gates.shape, 1)
    return jnp.sum(jnp.where(lanes == expert, gates, 0.0), axis=1, keepdims=True)


def pair_source(step, half, steps):
    core = lax.rem(lax.axis_index('expert'), CORES)
    mine = step // half
    tile = lax.rem(step, half)
    lane = lax.rem(core + 1 + mine, CORES)
    return CORES * (tile // steps) + lane, lax.rem(tile, steps)


def pair_sum(compute, half, steps, tile, inbox_ref, out_ref, acc_ref, send_sem, recv_sem, in_sem, out_sem):
    step = pl.program_id(0)
    last = 2 * half - 1
    me = lax.axis_index('expert')
    other = me + 1 - 2 * lax.rem(me, CORES)

    def at(ref, job):
        return ref.at[job // steps, pl.ds(lax.rem(job, steps) * tile, tile)]

    def send(job):
        slot = lax.rem(job, N_ACC)
        return pltpu.make_async_remote_copy(
            src_ref=acc_ref.at[slot], dst_ref=at(inbox_ref, job), send_sem=send_sem.at[slot], recv_sem=recv_sem.at[job],
            device_id={'expert': other}, device_id_type=MESH)

    def fetch(job):
        slot = lax.rem(job + half, N_ACC)
        return pltpu.make_async_copy(at(inbox_ref, job), acc_ref.at[slot], in_sem.at[slot])

    def store(job):
        slot = lax.rem(job + half, N_ACC)
        return pltpu.make_async_copy(acc_ref.at[slot], at(out_ref, job), out_sem.at[slot])

    @pl.when(step == 0)
    def _():
        barrier = pltpu.get_barrier_semaphore()
        pl.semaphore_signal(barrier, inc=1, device_id={'expert': other}, device_id_type=MESH)
        pl.semaphore_wait(barrier, 1)

    back = step - (N_ACC - 1)

    @pl.when((back >= 0) & (back < half))
    def _():
        send(back).wait_send()

    @pl.when(back >= half)
    def _():
        store(back - half).wait()

    ahead = step + 1 - half

    @pl.when((ahead >= 0) & (ahead < half))
    def _():
        send(ahead).wait_recv()
        fetch(ahead).start()

    acc = acc_ref.at[lax.rem(step, N_ACC)]

    @pl.when(step < half)
    def _():
        acc[...] = jnp.zeros_like(acc)

    @pl.when(step >= half)
    def _():
        fetch(step - half).wait()

    compute(acc)

    @pl.when(step < half)
    def _():
        send(step).start()

    @pl.when(step >= half)
    def _():
        store(step - half).start()

    @pl.when(step == last)
    def _():
        for job in range(half - N_ACC + 1, half):
            store(job).wait()


def fwd_body(ffn, n_local, half, steps, x_ref, g_ref, w13_ref, w2_ref, y_ref, inbox_ref, *scratch):
    tile = x_ref.shape[1]

    def compute(acc):
        for e in range(n_local):
            gate = gate_column(g_ref[0], e)
            pre = dot(x_ref[0], w13_ref[e])
            one, three = pre[:, :ffn], pre[:, ffn:]
            hidden = jnp.where(gate > 0.0, one * jax.nn.sigmoid(one) * three, 0.0).astype(BF16)
            acc[...] += gate * dot(hidden, w2_ref[e]).astype(BF16).astype(F32)

    pair_sum(compute, half, steps, tile, inbox_ref, y_ref, *scratch)


def pair_scratch(tile, model, half):
    return [
        pltpu.VMEM((N_ACC, tile, model), F32),
        pltpu.SemaphoreType.DMA((N_ACC,)),
        pltpu.SemaphoreType.DMA((half,)),
        pltpu.SemaphoreType.DMA((N_ACC,)),
        pltpu.SemaphoreType.DMA((N_ACC,)),
    ]


def whole(array):
    return pl.BlockSpec(array.shape, lambda i: (0,) * array.ndim, pipeline_mode=pl.Buffered(1))


def expert_fwd(x, gates, w13, w2, start, collective_id):
    n_src, rows, model = x.shape
    n_local, ffn = w2.shape[:2]
    tile = min(TILE_F, rows)
    steps = rows // tile
    n_own = n_src // CORES
    half = n_own * steps
    flops = 2 * n_src * rows * n_local * model * ffn * 3

    def at(base):
        def index(i):
            src, t = pair_source(i, half, steps)
            return src, base // tile + t, 0

        return index

    part = jax.ShapeDtypeStruct((n_own, rows, model), F32)
    return pl.pallas_call(
        functools.partial(fwd_body, ffn, n_local, half, steps),
        grid=(2 * half,),
        in_specs=[
            pl.BlockSpec((1, tile, model), at(0)),
            pl.BlockSpec((1, tile, n_local), at(start)),
            whole(w13),
            whole(w2),
        ],
        out_specs=[pl.BlockSpec(memory_space=pl.ANY)] * 2,
        out_shape=[part, part],
        scratch_shapes=pair_scratch(tile, model, half),
        compiler_params=pltpu.CompilerParams(
            dimension_semantics=('arbitrary',), vmem_limit_bytes=VMEM_LIMIT, collective_id=collective_id, has_side_effects=True),
        cost_estimate=pl.CostEstimate(flops=flops, bytes_accessed=n_src * rows * model * 6, transcendentals=0),
        name='expert_fwd',
    )(x, gates, w13, w2)[0]


def bwd_body(ffn, n_local, half, steps, n_carried, x_ref, dy_ref, g_ref, w13_ref, w2_ref, *refs):
    dx_ref, inbox_ref, da_ref, h_ref = refs[n_carried:n_carried + 4]
    tile = x_ref.shape[1]

    def compute(acc):
        def expert(e, carry):
            gate = gate_column(g_ref[0], e)
            live = gate > 0.0
            pre = dot(x_ref[0], w13_ref[e])
            one, three = pre[:, :ffn], pre[:, ffn:]
            sig = jax.nn.sigmoid(one)
            act = one * sig
            h_ref[0, :, pl.ds(pl.multiple_of(e * ffn, ffn), ffn)] = jnp.where(live, act * three, 0.0).astype(BF16)
            d_out = (gate * dy_ref[0].astype(F32)).astype(BF16)
            d_hid = dot_t(d_out, w2_ref[e]).astype(BF16).astype(F32)
            d_one = jnp.where(live, d_hid * three * sig * (1.0 + one * (1.0 - sig)), 0.0).astype(BF16)
            d_three = jnp.where(live, d_hid * act, 0.0).astype(BF16)
            d_pre = jnp.concatenate([d_one, d_three], axis=1)
            da_ref[0, :, pl.ds(pl.multiple_of(2 * e * ffn, 2 * ffn), 2 * ffn)] = d_pre
            acc[...] += dot_t(d_pre, w13_ref[e]).astype(BF16).astype(F32)
            return carry

        lax.fori_loop(0, n_local, expert, 0)

    pair_sum(compute, half, steps, tile, inbox_ref, dx_ref, *refs[n_carried + 4:])


def expert_bwd(x, dy, gates, w13, w2, start, rows, carried, collective_id):
    n_src, n_tok, model = x.shape
    n_local, ffn = w2.shape[:2]
    tile = min(TILE_A, rows)
    steps = rows // tile
    n_own = n_src // CORES
    half = n_own * steps
    flops = 2 * n_src * rows * n_local * model * ffn * 5

    def at(i):
        src, t = pair_source(i, half, steps)
        return src, start // tile + t, 0

    hbm = pl.BlockSpec(memory_space=pl.ANY)
    part = jax.ShapeDtypeStruct((n_own, rows, model), F32)
    outs = pl.pallas_call(
        functools.partial(bwd_body, ffn, n_local, half, steps, len(carried)),
        grid=(2 * half,),
        in_specs=[
            pl.BlockSpec((1, tile, model), at),
            pl.BlockSpec((1, tile, model), at),
            pl.BlockSpec((1, tile, n_local), at),
            whole(w13),
            whole(w2),
        ] + [hbm] * len(carried),
        out_specs=[
            hbm,
            hbm,
            pl.BlockSpec((1, tile, 2 * ffn * n_local), at),
            pl.BlockSpec((1, tile, ffn * n_local), at),
        ],
        out_shape=[
            part,
            part,
            jax.ShapeDtypeStruct((n_src, n_tok, 2 * ffn * n_local), BF16),
            jax.ShapeDtypeStruct((n_src, n_tok, ffn * n_local), BF16),
        ],
        scratch_shapes=pair_scratch(tile, model, half),
        input_output_aliases={5 + i: 2 + i for i in range(len(carried))},
        compiler_params=pltpu.CompilerParams(
            dimension_semantics=('arbitrary',), vmem_limit_bytes=VMEM_LIMIT, collective_id=collective_id, has_side_effects=True),
        cost_estimate=pl.CostEstimate(flops=flops, bytes_accessed=n_src * rows * model * 14, transcendentals=0),
        name='expert_bwd',
    )(x, dy, gates, w13, w2, *carried)
    return outs[0], outs[2:]


def grad_body(ffn, x_ref, dy_ref, g_ref, da_ref, h_ref, dw1_ref, dw3_ref, dw2_ref, acc13_ref, acc2_ref):
    e, k = pl.program_id(0), pl.program_id(1)

    @pl.when(k == 0)
    def _():
        acc13_ref[...] = jnp.zeros_like(acc13_ref)
        acc2_ref[...] = jnp.zeros_like(acc2_ref)

    acc13_ref[...] += dot_a(x_ref[0], da_ref[0])
    d_out = (gate_column(g_ref[0], e) * dy_ref[0].astype(F32)).astype(BF16)
    acc2_ref[...] += dot_a(h_ref[0], d_out)

    @pl.when(k == pl.num_programs(1) - 1)
    def _():
        dw1_ref[0] = acc13_ref[:, :ffn].astype(BF16)
        dw3_ref[0] = acc13_ref[:, ffn:].astype(BF16)
        dw2_ref[0] = acc2_ref[...].astype(BF16)


def weight_grads(x, dy, gates, d_pre, hidden):
    n_src, n_tok, model = x.shape
    n_local = gates.shape[2]
    ffn = hidden.shape[2] // n_local
    flops = 2 * n_src * n_tok * n_local * model * ffn * 3
    at = lambda e, k: (k, 0, 0)
    at_e = lambda e, k: (k, 0, e)
    out = lambda e, k: (e, 0, 0)
    return pl.pallas_call(
        functools.partial(grad_body, ffn),
        grid=(n_local, n_src),
        in_specs=[
            pl.BlockSpec((1, n_tok, model), at),
            pl.BlockSpec((1, n_tok, model), at),
            pl.BlockSpec((1, n_tok, n_local), at),
            pl.BlockSpec((1, n_tok, 2 * ffn), at_e),
            pl.BlockSpec((1, n_tok, ffn), at_e),
        ],
        out_specs=[
            pl.BlockSpec((1, model, ffn), out),
            pl.BlockSpec((1, model, ffn), out),
            pl.BlockSpec((1, ffn, model), out),
        ],
        out_shape=[
            jax.ShapeDtypeStruct((n_local, model, ffn), BF16),
            jax.ShapeDtypeStruct((n_local, model, ffn), BF16),
            jax.ShapeDtypeStruct((n_local, ffn, model), BF16),
        ],
        scratch_shapes=[pltpu.VMEM((model, 2 * ffn), F32), pltpu.VMEM((ffn, model), F32)],
        compiler_params=pltpu.CompilerParams(dimension_semantics=('arbitrary', 'arbitrary'), vmem_limit_bytes=VMEM_LIMIT),
        cost_estimate=pl.CostEstimate(flops=flops, bytes_accessed=n_src * n_tok * model * 4 * n_local, transcendentals=0),
        name='weight_grads',
    )(x, dy, gates, d_pre, hidden)


def solution(mesh):
    n_stage = mesh.shape['stage']
    n_dev = mesh.shape['expert']
    to_next = [(stage_idx, (stage_idx + 1) % n_stage) for stage_idx in range(n_stage)]
    to_prev = [((stage_idx + 1) % n_stage, stage_idx) for stage_idx in range(n_stage)]
    tok_spec = P('stage', 'expert', None)
    w_spec = P('stage', 'expert', None, None)
    same_core = [list(range(core, n_dev, CORES)) for core in range(CORES)]
    n_fwd = len(FWD_CHUNKS)

    def moe_body(x_act, route_idx, route_wts, w_one, w_three, w_two, dy_act):
        x_src = x_act[0]
        n_tok, _ = x_src.shape
        n_local = w_one.shape[1]
        n_exp = n_local * n_dev

        def gather(rows):
            return lax.all_gather(rows, 'expert', axis=0, tiled=False)

        def reduce_rows(part):
            return lax.psum_scatter(part, 'expert', scatter_dimension=0, axis_index_groups=same_core, tiled=False).astype(BF16)

        dy_all = gather(dy_act[0])

        hits = route_idx[0][:, :, None] == jnp.arange(n_exp, dtype=jnp.int32)
        gate_src = jnp.sum(jnp.where(hits, route_wts[0][:, :, None], 0.0), axis=1)
        gate_src = jnp.transpose(gate_src.reshape(n_tok, n_dev, n_local), (1, 2, 0))
        gate_dst = lax.ppermute(gate_src, 'stage', to_next)
        gates = jnp.transpose(lax.all_to_all(gate_dst, 'expert', 0, 0), (0, 2, 1))

        w13 = jnp.concatenate([w_one[0], w_three[0]], axis=2)
        w2 = w_two[0]

        y_parts = []
        start = 0
        y_part = None
        for k, rows in enumerate(FWD_CHUNKS):
            x_dst = lax.ppermute(x_src[start:start + rows], 'stage', to_next)
            x_all = gather(x_dst)
            if y_part is None:
                x_first = x_all
            else:
                x_all, _ = lax.optimization_barrier((x_all, y_part))
            y_part = expert_fwd(x_all, gates, w13, w2, start, k)
            y_parts.append(reduce_rows(y_part))
            start += rows
        y_out = jnp.concatenate(y_parts, axis=0)

        x_again, _ = lax.optimization_barrier((x_src, x_first))
        x_dst = lax.ppermute(x_again, 'stage', to_next)
        x_all = gather(x_dst)
        x_all, _ = lax.optimization_barrier((x_all, y_part))

        dx_parts = []
        carried = ()
        start = 0
        for k, rows in enumerate(BWD_CHUNKS):
            dx_part, carried = expert_bwd(x_all, dy_all, gates, w13, w2, start, rows, carried, n_fwd + k)
            dx_dst = reduce_rows(dx_part)
            dx_parts.append(lax.ppermute(dx_dst, 'stage', to_prev))
            start += rows
        dx_out = jnp.concatenate(dx_parts, axis=0)

        g_one, g_three, g_two = weight_grads(x_all, dy_all, gates, *carried)
        return y_out[None], dx_out[None], g_one[None], g_three[None], g_two[None]

    return jax.shard_map(moe_body, mesh=mesh, in_specs=(tok_spec, tok_spec, tok_spec, w_spec, w_spec, w_spec, tok_spec), out_specs=(tok_spec, tok_spec, w_spec, w_spec, w_spec), check_vma=False)
```

time: 5500 us -> 1480 us (0.27)
  local copies, waits for them, and re-layouts: 2230 us -> 9.78 us
  Pallas kernels: 0 us -> 935 us
  waiting for transfers between devices: 1380 us -> 473 us
  matrix products: 859 us -> 0 us
  blocking collectives: 740 us -> 0 us
  other arithmetic: 226 us -> 36.1 us
    gather x6 -> x0, local copies, waits for them, and re-layouts: 1330 us -> none  [take_rows(): return jnp.take(row_table, row_ids, axis=0, mode='fill', fill_value=0)]
    all_to_all x4 -> x1, waiting for transfers between devices: 1150 us -> 0.01 us  [moe_body(): gates = jnp.transpose(lax.all_to_all(gate_dst, 'expert', 0, 0), (0, 2, 1))]
    pallas_call x0 -> x6, Pallas kernels: none -> 935 us  [the longest x3 442 us: expert_bwd(): pl.pallas_call(functools.partial(bwd_body, ffn, n_local, half, steps, len...]
    dot_general x11 -> x0, matrix products: 859 us -> none  [the longest x1 140 us: expert_backward(): jnp.einsum('pecf,pecd->efd', hidden, d_buf, preferred_element_type=jnp.fl...]
    all_to_all x1 -> x0, blocking collectives: 740 us -> none  [dispatch(): return lax.all_to_all(send_buf, 'expert', 0, 0)]
    reshape x6 -> x1, local copies, waits for them, and re-layouts: 425 us -> 0.04 us  [moe_body(): gate_src = jnp.transpose(gate_src.reshape(n_tok, n_dev, n_local), (1, 2, 0))]
    unnamed x0 -> x14, waiting for transfers between devices: none -> 225 us
    all_to_all x3 -> x1, local copies, waits for them, and re-layouts: 190 us -> 2.68 us  [moe_body(): gates = jnp.transpose(lax.all_to_all(gate_dst, 'expert', 0, 0), (0, 2, 1))]
  transfers between devices with their start and end apart: 9 -> 17, of which waited for: 5 -> 7; matrix products, arithmetic and copies ran while one was open for 34% -> 3% of each run, Pallas kernels for 0% -> 63%
where the time goes in v2:
time: 1480 us
  Pallas kernels  935 us (63%)
  waiting for transfers between devices  473 us (32%)
  other arithmetic  36.1 us (2%)
  starting transfers between devices  16.2 us (1%)
    pallas_call x3, Pallas kernels, expert_bwd(): pl.pallas_call(functools.partial(bwd_body, ffn, n_local, half, steps, len...  442 us
    pallas_call x2, Pallas kernels, expert_fwd(): pl.pallas_call(functools.partial(fwd_body, ffn, n_local, half, steps), gr...  259 us
    pallas_call x1, Pallas kernels, weight_grads(): pl.pallas_call(functools.partial(grad_body, ffn), grid=(n_local, n_src),...  234 us
    unnamed x14, waiting for transfers between devices  225 us
    ppermute x2, waiting for transfers between devices, moe_body(): x_dst = lax.ppermute(x_src[start:start + rows], 'stage', to_next)  90.7 us
    ppermute x1, waiting for transfers between devices, moe_body(): x_dst = lax.ppermute(x_again, 'stage', to_next)  89.7 us
    all_gather x4, waiting for transfers between devices, gather(): return lax.all_gather(rows, 'expert', axis=0, tiled=False)  63.7 us
  transfers between devices with their start and end apart: 17, of which 7 were waited for; matrix products, arithmetic and copies ran while one was open for 3% of the time, Pallas kernels for 63%

profile of v2, /device:TPU:0, one launch (start us, length us, event | category | flops | bytes accessed | tf_op | source)
XLA Modules:
  0.0 1483.9 jit_solution(3595739157923901076)
XLA Ops:
  8.5 3.3 collective-permute-start
  11.8 23.2 %collective-permute-done = bf16[256,2048]{1,0:T(8,128)(2,1)S(1)} collective-permute-done((bf16[256,2048]{1,0:T(8,128)(2,1)S(1)}, bf16[256,2048]{1,0:T(8,128)(2,1)S(1)}, u32[]{:S(2)}, u32[]{:S(2)}) %collective-permute-start) | collective-permute-done | bytes 1048608 | tf_op jit(solution)/shard_map/ppermute | solution.py:349
  40.1 67.5 %collective-permute-done.2 = bf16[768,2048]{1,0:T(8,128)(2,1)S(1)} collective-permute-done((bf16[768,2048]{1,0:T(8,128)(2,1)S(1)}, bf16[768,2048]{1,0:T(8,128)(2,1)S(1)}, u32[]{:S(2)}, u32[]{:S(2)}) %collective-permute-start.2) | collective-permute-done | bytes 3145760 | tf_op jit(solution)/shard_map/ppermute | solution.py:349
  110.9 89.7 %collective-permute-done.3 = bf16[1024,2048]{1,0:T(8,128)(2,1)} collective-permute-done((bf16[1024,2048]{1,0:T(8,128)(2,1)}, bf16[1024,2048]{1,0:T(8,128)(2,1)}, u32[]{:S(2)}, u32[]{:S(2)}) %collective-permute-start.3) | collective-permute-done | bytes 4194336 | tf_op jit(solution)/shard_map/ppermute | solution.py:361
  202.7 3.8 collective-permute-done.1
  207.3 3.4 all-to-all-start
  210.7 14.1 pad_maximum_fusion.w13_ref
  224.8 2.7 copy.28
  227.5 69.0 %expert_fwd.2 = (f32[4,256,2048]{2,1,0:T(8,128)}, f32[4,256,2048]{2,1,0:T(8,128)}) custom-call(bf16[8,256,2048]{2,1,0:T(8,128)(2,1)} %bitcast.57, f32[8,1024,4]{2,1,0:T(8,128)} %bitcast.38, bf16[4,2048,1024]{2,1,0:T(8,128)(2,1)} %pad_maximum_fusion.w13_ref, bf16[4,512,2048]{2,1,0:T(8,128)(2,1)} %bitcast.52), custom_call_target="tpu_custom_call" | custom-call | flops 51539607552 | bytes 25165824 | tf_op jit(solution)/shard_map/expert_fwd/pallas_call | solution.py:165
  296.7 190.3 %expert_fwd.3 = (f32[4,768,2048]{2,1,0:T(8,128)}, f32[4,768,2048]{2,1,0:T(8,128)}) custom-call(bf16[8,768,2048]{2,1,0:T(8,128)(2,1)} %bitcast.51, f32[8,1024,4]{2,1,0:T(8,128)} %bitcast.39, bf16[4,2048,1024]{2,1,0:T(8,128)(2,1)} %pad_maximum_fusion.w13_ref, bf16[4,512,2048]{2,1,0:T(8,128)(2,1)} %bitcast.53), custom_call_target="tpu_custom_call" | custom-call | flops 154618822656 | bytes 75497472 | tf_op jit(solution)/shard_map/expert_fwd/pallas_call | solution.py:165
  487.1 63.7 %all-gather.8.cloned.1.call-done.dy_ref = bf16[8,1024,2048]{2,1,0:T(8,128)(2,1)} async-done(((bf16[1,1024,2048]{2,1,0:T(8,128)(2,1)}), bf16[8,1024,2048]{2,1,0:T(8,128)(2,1)}) %all-gather.8.cloned.1.call-update) | async-done | bytes 33554448 | tf_op jit(solution)/shard_map/all_gather | solution.py:329
  550.8 209.3 %expert_bwd.3 = (f32[4,512,2048]{2,1,0:T(8,128)}, f32[4,512,2048]{2,1,0:T(8,128)}, bf16[8,1024,4096]{2,1,0:T(8,128)(2,1)}, bf16[8,1024,2048]{2,1,0:T(8,128)(2,1)}) custom-call(bf16[8,1024,2048]{2,1,0:T(8,128)(2,1)} %bitcast.47, bf16[8,1024,2048]{2,1,0:T(8,128)(2,1)} %all-gather.8.cloned.1.call-done.dy_ref, f32[8,1024,4]{2,1,0:T(8,128)} %bitcast.40, ...), custom_call_target="tpu_custom_call" | custom-call | flops 171798691840 | bytes 117440512 | tf_op jit(solution)/shard_map/expert_bwd/pallas_call | solution.py:226
  760.1 115.8 %expert_bwd.4 = (f32[4,256,2048]{2,1,0:T(8,128)}, f32[4,256,2048]{2,1,0:T(8,128)}, bf16[8,1024,4096]{2,1,0:T(8,128)(2,1)}, bf16[8,1024,2048]{2,1,0:T(8,128)(2,1)}) custom-call(bf16[8,1024,2048]{2,1,0:T(8,128)(2,1)} %bitcast.48, bf16[8,1024,2048]{2,1,0:T(8,128)(2,1)} %all-gather.8.cloned.1.call-done.dy_ref, ...), custom_call_target="tpu_custom_call", output_to_operand_aliasing={{2}: (5, {}), {3}: (6, {})} | custom-call | flops 85899345920 | bytes 58720256 | tf_op jit(solution)/shard_map/expert_bwd/pallas_call | solution.py:226
  876.0 116.5 %expert_bwd.5 = (f32[4,256,2048]{2,1,0:T(8,128)}, f32[4,256,2048]{2,1,0:T(8,128)}, bf16[8,1024,4096]{2,1,0:T(8,128)(2,1)}, bf16[8,1024,2048]{2,1,0:T(8,128)(2,1)}) custom-call(bf16[8,1024,2048]{2,1,0:T(8,128)(2,1)} %bitcast.49, bf16[8,1024,2048]{2,1,0:T(8,128)(2,1)} %all-gather.8.cloned.1.call-done.dy_ref, ...), custom_call_target="tpu_custom_call", output_to_operand_aliasing={{2}: (5, {}), {3}: (6, {})} | custom-call | flops 85899345920 | bytes 58720256 | tf_op jit(solution)/shard_map/expert_bwd/pallas_call | solution.py:226
  994.0 2.7 convert_bitcast_fusion.4
  996.8 3.1 convert_bitcast_fusion.3
  1001.5 73.8 %reduce-scatter.24.cloned.1.call-done = f32[1,256,2048]{2,1,0:T(8,128)} async-done(((f32[4,256,2048]{2,1,0:T(8,128)}), f32[1,256,2048]{2,1,0:T(8,128)}) %reduce-scatter.24.cloned.1.call-update) | async-done | bytes 2097168
  1075.3 2.7 convert_bitcast_fusion.2
  1079.5 148.8 %reduce-scatter.20.cloned.1.call-done = f32[1,512,2048]{2,1,0:T(8,128)} async-done(((f32[4,512,2048]{2,1,0:T(8,128)}), f32[1,512,2048]{2,1,0:T(8,128)}) %reduce-scatter.20.cloned.1.call-update) | async-done | bytes 4194320
  1228.3 3.8 convert_bitcast_fusion.1
  1233.6 234.2 %weight_grads.1 = (bf16[4,2048,512]{2,1,0:T(8,128)(2,1)}, bf16[4,2048,512]{2,1,0:T(8,128)(2,1)}, bf16[4,512,2048]{2,1,0:T(8,128)(2,1)}) custom-call(bf16[8,1024,2048]{2,1,0:T(8,128)(2,1)} %bitcast.50, bf16[8,1024,2048]{2,1,0:T(8,128)(2,1)} %all-gather.8.cloned.1.call-done.dy_ref, f32[8,1024,4]{2,1,0:T(8,128)} %bitcast.43, ...), custom_call_target="tpu_custom_call" | custom-call | flops 206158430208 | bytes 268435456 | tf_op jit(solution)/shard_map/weight_grads/pallas_call | solution.py:285
  1467.9 3.3 convert_bitcast_fusion
  1471.2 2.4 maximum_bitcast_fusion
  1473.7 3.7 maximum_bitcast_fusion.1
  (50 shorter events, 18.8 us)
Async XLA Ops:
  7.2 102.2 %all-gather.10.cloned.1.call-start = ((), (), s32[]{:S(2)}) async-start(), calls=%async_computation.7 | async-start | bytes 9437184 | tf_op jit(solution)/shard_map/all_gather | solution.py:329
  8.5 26.5 %collective-permute-start = (bf16[256,2048]{1,0:T(8,128)(2,1)S(1)}, bf16[256,2048]{1,0:T(8,128)(2,1)S(1)}, u32[]{:S(2)}, u32[]{:S(2)}) collective-permute-start(bf16[256,2048]{1,0:T(8,128)(2,1)S(1)} %slice_bitcast_fusion.1), channel_id=1, source_target_pairs={{0,8},{8,0},{1,9},{9,1},{2,10},{10,2},{3,11},{11,3},{4,12},{12,4},... | collective-permute-start | bytes 3145736 | tf_op jit(solution)/shard_map/ppermute | solution.py:349
  35.0 1.0 copy-start.2
  36.0 165.3 %copy-start.3 = (f32[1,1024,8]{1,2,0:T(8,128)S(1)}, f32[1,1024,8]{1,2,0:T(8,128)}, u32[]{:S(2)}) copy-start(f32[1,1024,8]{1,2,0:T(8,128)} %param.9) | copy-start | bytes 98308
  36.0 165.3 %copy-start.4 = (s32[1,1024,8]{1,2,0:T(8,128)S(1)}, s32[1,1024,8]{1,2,0:T(8,128)}, u32[]{:S(2)}) copy-start(s32[1,1024,8]{1,2,0:T(8,128)} %param.8) | copy-start | bytes 98308
  36.0 260.7 %all-gather.12.cloned.1.call-start = ((), (), s32[]{:S(2)}) async-start(), calls=%async_computation.8 | async-start | bytes 28311552 | tf_op jit(solution)/shard_map/all_gather | solution.py:329
  38.4 69.3 %collective-permute-start.2 = (bf16[768,2048]{1,0:T(8,128)(2,1)S(1)}, bf16[768,2048]{1,0:T(8,128)(2,1)S(1)}, u32[]{:S(2)}, u32[]{:S(2)}) collective-permute-start(bf16[768,2048]{1,0:T(8,128)(2,1)S(1)} %slice_bitcast_fusion), channel_id=1, source_target_pairs={{0,8},{8,0},{1,9},{9,1},{2,10},{10,2},{3,11},{11,3},{4,12},{12,4},... | collective-permute-start | bytes 9437192 | tf_op jit(solution)/shard_map/ppermute | solution.py:349
  107.7 1.7 copy-start.1
  109.3 377.7 %all-gather.14.cloned.1.call-start = ((), (), s32[]{:S(2)}) async-start(), calls=%async_computation.9 | async-start | bytes 37748736 | tf_op jit(solution)/shard_map/all_gather | solution.py:329
  109.4 91.2 %collective-permute-start.3 = (bf16[1024,2048]{1,0:T(8,128)(2,1)}, bf16[1024,2048]{1,0:T(8,128)(2,1)}, u32[]{:S(2)}, u32[]{:S(2)}) collective-permute-start(bf16[1024,2048]{1,0:T(8,128)(2,1)} %bitcast.37), channel_id=1, source_target_pairs={{0,8},{8,0},{1,9},{9,1},{2,10},{10,2},{3,11},{11,3},{4,12},{12,4},... | collective-permute-start | bytes 12582920 | tf_op jit(solution)/shard_map/ppermute | solution.py:361
  200.7 350.1 %all-gather.8.cloned.1.call-start = ((), (), s32[]{:S(2)}) async-start(), calls=%async_computation.6 | async-start | bytes 37748736 | tf_op jit(solution)/shard_map/all_gather | solution.py:329
  201.5 5.0 collective-permute-start.1
  207.3 17.5 %all-to-all-start = ((f32[8,4,1024]{2,1,0:T(4,128)}), f32[8,4,1024]{2,1,0:T(4,128)S(1)}, u32[]{:S(2)}, u32[]{:S(2)}) async-start(f32[8,4,1024]{2,1,0:T(4,128)} %copy.27), calls=%async_computation | async-start | bytes 262144 | tf_op jit(solution)/shard_map/all_to_all | solution.py:340
  210.6 783.4 %reduce-scatter.16.cloned.1.call-start = ((), (), s32[]{:S(2)}) async-start(), calls=%async_computation.10 | async-start | bytes 10485760
  296.5 700.3 %reduce-scatter.22.cloned.1.call-start = ((), (), s32[]{:S(2)}) async-start(), calls=%async_computation.13 | async-start | bytes 10485760
  875.9 199.4 %reduce-scatter.24.cloned.1.call-start = ((), (), s32[]{:S(2)}) async-start(), calls=%async_computation.14 | async-start | bytes 10485760
  992.5 235.8 %reduce-scatter.20.cloned.1.call-start = ((), (), s32[]{:S(2)}) async-start(), calls=%async_computation.12 | async-start | bytes 20971520
  993.3 474.6 %reduce-scatter.18.cloned.1.call-start = ((), (), s32[]{:S(2)}) async-start(), calls=%async_computation.11 | async-start | bytes 31457280
  999.9 473.8 %collective-permute-start.5 = (bf16[256,2048]{1,0:T(8,128)(2,1)}, bf16[256,2048]{1,0:T(8,128)(2,1)}, u32[]{:S(2)}, u32[]{:S(2)}) collective-permute-start(bf16[256,2048]{1,0:T(8,128)(2,1)} %convert_bitcast_fusion.3), channel_id=1, source_target_pairs={{8,0},{0,8},{9,1},{1,9},{10,2},{2,10},{11,3},{3,11},{12,4},{4,12},... | collective-permute-start | bytes 3145736 | tf_op jit(solution)/shard_map/ppermute | solution.py:371
  1078.0 395.6 %collective-permute-start.6 = (bf16[256,2048]{1,0:T(8,128)(2,1)}, bf16[256,2048]{1,0:T(8,128)(2,1)}, u32[]{:S(2)}, u32[]{:S(2)}) collective-permute-start(bf16[256,2048]{1,0:T(8,128)(2,1)} %convert_bitcast_fusion.2), channel_id=1, source_target_pairs={{8,0},{0,8},{9,1},{1,9},{10,2},{2,10},{11,3},{3,11},{12,4},{4,12},... | collective-permute-start | bytes 3145736 | tf_op jit(solution)/shard_map/ppermute | solution.py:371
  1232.1 241.5 %collective-permute-start.4 = (bf16[512,2048]{1,0:T(8,128)(2,1)}, bf16[512,2048]{1,0:T(8,128)(2,1)}, u32[]{:S(2)}, u32[]{:S(2)}) collective-permute-start(bf16[512,2048]{1,0:T(8,128)(2,1)} %convert_bitcast_fusion.1), channel_id=1, source_target_pairs={{8,0},{0,8},{9,1},{1,9},{10,2},{2,10},{11,3},{3,11},{12,4},{4,12},... | collective-permute-start | bytes 6291464 | tf_op jit(solution)/shard_map/ppermute | solution.py:371
  1467.8 3.4 copy-start
Sparse Core Ops, SparseCore 0:
  36.1 51.7 all-gather.9
  109.5 123.8 all-gather.11
  235.2 156.9 all-gather.13
  393.8 156.9 all-gather.7
  553.6 82.5 reduce-scatter.15
  876.1 82.5 reduce-scatter.21
  992.6 82.6 reduce-scatter.23
  1078.3 149.9 reduce-scatter.19
  1231.4 217.9 reduce-scatter.17

commit v3 on v2

v3 whole, which is shorter than its diff:
```python
import functools

import jax
import jax.numpy as jnp
from jax import lax
from jax.experimental import pallas as pl
from jax.experimental.pallas import tpu as pltpu
from jax.sharding import PartitionSpec as P


F32 = jnp.float32
BF16 = jnp.bfloat16
FWD_CHUNKS = ((384, 384), (640, 320))
BWD_TILE = 512
DX_SPLIT = 768
VMEM_LIMIT = 65400 * 1024
N_ACC = 3
CORES = 2
MESH = pl.DeviceIdType.MESH


def dot(lhs, rhs):
    return jnp.dot(lhs, rhs, preferred_element_type=F32)


def dot_t(lhs, rhs):
    return lax.dot_general(lhs, rhs, (((1,), (1,)), ((), ())), preferred_element_type=F32)


def dot_a(lhs, rhs):
    return lax.dot_general(lhs, rhs, (((0,), (0,)), ((), ())), preferred_element_type=F32)


def gate_column(gates, expert):
    lanes = lax.broadcasted_iota(jnp.int32, gates.shape, 1)
    return jnp.sum(jnp.where(lanes == expert, gates, 0.0), axis=1, keepdims=True)


def pair_source(step, half, steps):
    core = lax.rem(lax.axis_index('expert'), CORES)
    mine = step // half
    tile = lax.rem(step, half)
    lane = lax.rem(core + 1 + mine, CORES)
    return CORES * (tile // steps) + lane, lax.rem(tile, steps)


def pair_sum(compute, half, steps, tile, inbox_ref, pieces, acc_ref, send_sem, recv_sem, in_sem, out_sem):
    step = pl.program_id(0)
    last = 2 * half - 1
    me = lax.axis_index('expert')
    other = me + 1 - 2 * lax.rem(me, CORES)

    def at(ref, job):
        return ref.at[job // steps, pl.ds(lax.rem(job, steps) * tile, tile)]

    class Store:
        def __init__(self, job):
            slot = lax.rem(job + half, N_ACC)
            self.copies = [
                pltpu.make_async_copy(
                    acc_ref.at[slot, pl.ds(row, rows)],
                    out_ref.at[job // steps, pl.ds(first + lax.rem(job, steps) * tile, rows)],
                    out_sem.at[slot, k])
                for k, (out_ref, first, row, rows) in enumerate(pieces)]

        def start(self):
            for copy in self.copies:
                copy.start()

        def wait(self):
            for copy in self.copies:
                copy.wait()

    def send(job):
        slot = lax.rem(job, N_ACC)
        return pltpu.make_async_remote_copy(
            src_ref=acc_ref.at[slot], dst_ref=at(inbox_ref, job), send_sem=send_sem.at[slot], recv_sem=recv_sem.at[job],
            device_id={'expert': other}, device_id_type=MESH)

    def fetch(job):
        slot = lax.rem(job + half, N_ACC)
        return pltpu.make_async_copy(at(inbox_ref, job), acc_ref.at[slot], in_sem.at[slot])

    @pl.when(step == 0)
    def _():
        barrier = pltpu.get_barrier_semaphore()
        pl.semaphore_signal(barrier, inc=1, device_id={'expert': other}, device_id_type=MESH)
        pl.semaphore_wait(barrier, 1)

    back = step - (N_ACC - 1)

    @pl.when((back >= 0) & (back < half))
    def _():
        send(back).wait_send()

    @pl.when(back >= half)
    def _():
        Store(back - half).wait()

    ahead = step + 1 - half

    @pl.when((ahead >= 0) & (ahead < half))
    def _():
        send(ahead).wait_recv()
        fetch(ahead).start()

    acc = acc_ref.at[lax.rem(step, N_ACC)]

    @pl.when(step < half)
    def _():
        acc[...] = jnp.zeros_like(acc)

    @pl.when(step >= half)
    def _():
        fetch(step - half).wait()

    compute(acc)

    @pl.when(step < half)
    def _():
        send(step).start()

    @pl.when(step >= half)
    def _():
        Store(step - half).start()

    @pl.when(step == last)
    def _():
        for job in range(half - N_ACC + 1, half):
            Store(job).wait()


def fwd_body(ffn, n_local, half, steps, start, n_carried, x_ref, g_ref, w13_ref, w2_ref, *refs):
    y_ref, inbox_ref = refs[n_carried:n_carried + 2]
    tile = x_ref.shape[1]

    def compute(acc):
        for e in range(n_local):
            gate = gate_column(g_ref[0], e)
            pre = dot(x_ref[0], w13_ref[e])
            one, three = pre[:, :ffn], pre[:, ffn:]
            hidden = jnp.where(gate > 0.0, one * jax.nn.sigmoid(one) * three, 0.0).astype(BF16)
            acc[...] += gate * dot(hidden, w2_ref[e]).astype(BF16).astype(F32)

    pair_sum(compute, half, steps, tile, inbox_ref, [(y_ref, start, 0, tile)], *refs[n_carried + 2:])


def pair_scratch(tile, model, half, n_pieces):
    return [
        pltpu.VMEM((N_ACC, tile, model), F32),
        pltpu.SemaphoreType.DMA((N_ACC,)),
        pltpu.SemaphoreType.DMA((half,)),
        pltpu.SemaphoreType.DMA((N_ACC,)),
        pltpu.SemaphoreType.DMA((N_ACC, n_pieces)),
    ]


def pair_params(collective_id):
    return pltpu.CompilerParams(
        dimension_semantics=('arbitrary',), vmem_limit_bytes=VMEM_LIMIT, collective_id=collective_id, has_side_effects=True)


def whole(array):
    return pl.BlockSpec(array.shape, lambda i: (0,) * array.ndim, pipeline_mode=pl.Buffered(1))


HBM = pl.BlockSpec(memory_space=pl.ANY)


def expert_fwd(x, gates, w13, w2, tile, start, n_tok, carried, collective_id):
    n_src, rows, model = x.shape
    n_local, ffn = w2.shape[:2]
    steps = rows // tile
    n_own = n_src // CORES
    half = n_own * steps
    flops = 2 * n_src * rows * n_local * model * ffn * 3

    def at(i):
        src, t = pair_source(i, half, steps)
        return src, t, 0

    return pl.pallas_call(
        functools.partial(fwd_body, ffn, n_local, half, steps, start, len(carried)),
        grid=(2 * half,),
        in_specs=[
            pl.BlockSpec((1, tile, model), at),
            pl.BlockSpec((1, tile, n_local), at),
            whole(w13),
            whole(w2),
        ] + [HBM] * len(carried),
        out_specs=[HBM, HBM],
        out_shape=[jax.ShapeDtypeStruct((n_own, n_tok, model), F32), jax.ShapeDtypeStruct((n_own, rows, model), F32)],
        scratch_shapes=pair_scratch(tile, model, half, 1),
        input_output_aliases={4 + i: i for i in range(len(carried))},
        compiler_params=pair_params(collective_id),
        cost_estimate=pl.CostEstimate(flops=flops, bytes_accessed=n_src * rows * model * 6, transcendentals=0),
        name='expert_fwd',
    )(x, gates, w13, w2, *carried)[0]


def bwd_body(ffn, n_local, half, steps, pieces, n_carried, x_ref, dy_ref, g_ref, w13_ref, w2_ref, *refs):
    lo_ref, hi_ref, da_ref, h_ref, inbox_ref = refs[n_carried:n_carried + 5]
    tile = x_ref.shape[2]

    def compute(acc):
        def expert(e, carry):
            gate = gate_column(g_ref[0], e)
            live = gate > 0.0
            pre = dot(x_ref[0, 0], w13_ref[e])
            one, three = pre[:, :ffn], pre[:, ffn:]
            sig = jax.nn.sigmoid(one)
            act = one * sig
            h_ref[0, :, pl.ds(pl.multiple_of(e * ffn, ffn), ffn)] = jnp.where(live, act * three, 0.0).astype(BF16)
            d_out = (gate * dy_ref[0, 0].astype(F32)).astype(BF16)
            d_hid = dot_t(d_out, w2_ref[e]).astype(BF16).astype(F32)
            d_one = jnp.where(live, d_hid * three * sig * (1.0 + one * (1.0 - sig)), 0.0).astype(BF16)
            d_three = jnp.where(live, d_hid * act, 0.0).astype(BF16)
            d_pre = jnp.concatenate([d_one, d_three], axis=1)
            da_ref[0, :, pl.ds(pl.multiple_of(2 * e * ffn, 2 * ffn), 2 * ffn)] = d_pre
            acc[...] += dot_t(d_pre, w13_ref[e]).astype(BF16).astype(F32)
            return carry

        lax.fori_loop(0, n_local, expert, 0)

    outs = [((lo_ref, hi_ref)[which], first, row, rows) for which, first, row, rows in pieces]
    pair_sum(compute, half, steps, tile, inbox_ref, outs, *refs[n_carried + 5:])


def expert_bwd(rows_in, gates, w13, w2, start, n_tok, pieces, carried, collective_id):
    n_src, _, rows, model = rows_in.shape
    n_local, ffn = w2.shape[:2]
    tile = min(BWD_TILE, rows)
    steps = rows // tile
    n_own = n_src // CORES
    half = n_own * steps
    flops = 2 * n_src * rows * n_local * model * ffn * 5

    def rows_of(which):
        def index(i):
            src, t = pair_source(i, half, steps)
            return src, which, t, 0

        return index

    def at(i):
        src, t = pair_source(i, half, steps)
        return src, start // tile + t, 0

    outs = pl.pallas_call(
        functools.partial(bwd_body, ffn, n_local, half, steps, pieces, len(carried)),
        grid=(2 * half,),
        in_specs=[
            pl.BlockSpec((1, 1, tile, model), rows_of(1)),
            pl.BlockSpec((1, 1, tile, model), rows_of(0)),
            pl.BlockSpec((1, tile, n_local), at),
            whole(w13),
            whole(w2),
        ] + [HBM] * len(carried),
        out_specs=[
            HBM,
            HBM,
            pl.BlockSpec((1, tile, 2 * ffn * n_local), at),
            pl.BlockSpec((1, tile, ffn * n_local), at),
            HBM,
        ],
        out_shape=[
            jax.ShapeDtypeStruct((n_own, DX_SPLIT, model), F32),
            jax.ShapeDtypeStruct((n_own, n_tok - DX_SPLIT, model), F32),
            jax.ShapeDtypeStruct((n_src, n_tok, 2 * ffn * n_local), BF16),
            jax.ShapeDtypeStruct((n_src, n_tok, ffn * n_local), BF16),
            jax.ShapeDtypeStruct((n_own, rows, model), F32),
        ],
        scratch_shapes=pair_scratch(tile, model, half, len(pieces)),
        input_output_aliases={5 + i: i for i in range(len(carried))},
        compiler_params=pair_params(collective_id),
        cost_estimate=pl.CostEstimate(flops=flops, bytes_accessed=n_src * rows * model * 14, transcendentals=0),
        name='expert_bwd',
    )(rows_in, rows_in, gates, w13, w2, *carried)
    return outs[:4]


def grad_body(ffn, lo_ref, hi_ref, g_ref, da_ref, h_ref, dw1_ref, dw3_ref, dw2_ref, acc13_ref, acc2_ref):
    e, k = pl.program_id(0), pl.program_id(1)

    @pl.when(k == 0)
    def _():
        acc13_ref[...] = jnp.zeros_like(acc13_ref)
        acc2_ref[...] = jnp.zeros_like(acc2_ref)

    acc13_ref[...] += dot_a(jnp.concatenate([lo_ref[0, 1], hi_ref[0, 1]], axis=0), da_ref[0])
    d_out = jnp.concatenate([lo_ref[0, 0], hi_ref[0, 0]], axis=0).astype(F32)
    d_out = (gate_column(g_ref[0], e) * d_out).astype(BF16)
    acc2_ref[...] += dot_a(h_ref[0], d_out)

    @pl.when(k == pl.num_programs(1) - 1)
    def _():
        dw1_ref[0] = acc13_ref[:, :ffn].astype(BF16)
        dw3_ref[0] = acc13_ref[:, ffn:].astype(BF16)
        dw2_ref[0] = acc2_ref[...].astype(BF16)


def weight_grads(lo, hi, gates, d_pre, hidden):
    n_src, n_tok, n_local = gates.shape
    model = lo.shape[3]
    ffn = hidden.shape[2] // n_local
    flops = 2 * n_src * n_tok * n_local * model * ffn * 3
    at = lambda e, k: (k, 0, 0)
    at_e = lambda e, k: (k, 0, e)
    out = lambda e, k: (e, 0, 0)
    return pl.pallas_call(
        functools.partial(grad_body, ffn),
        grid=(n_local, n_src),
        in_specs=[
            pl.BlockSpec((1,) + lo.shape[1:], lambda e, k: (k, 0, 0, 0)),
            pl.BlockSpec((1,) + hi.shape[1:], lambda e, k: (k, 0, 0, 0)),
            pl.BlockSpec((1, n_tok, n_local), at),
            pl.BlockSpec((1, n_tok, 2 * ffn), at_e),
            pl.BlockSpec((1, n_tok, ffn), at_e),
        ],
        out_specs=[
            pl.BlockSpec((1, model, ffn), out),
            pl.BlockSpec((1, model, ffn), out),
            pl.BlockSpec((1, ffn, model), out),
        ],
        out_shape=[
            jax.ShapeDtypeStruct((n_local, model, ffn), BF16),
            jax.ShapeDtypeStruct((n_local, model, ffn), BF16),
            jax.ShapeDtypeStruct((n_local, ffn, model), BF16),
        ],
        scratch_shapes=[pltpu.VMEM((model, 2 * ffn), F32), pltpu.VMEM((ffn, model), F32)],
        compiler_params=pltpu.CompilerParams(dimension_semantics=('arbitrary', 'arbitrary'), vmem_limit_bytes=VMEM_LIMIT),
        cost_estimate=pl.CostEstimate(flops=flops, bytes_accessed=n_src * n_tok * model * 4 * n_local, transcendentals=0),
        name='weight_grads',
    )(lo, hi, gates, d_pre, hidden)


def solution(mesh):
    n_stage = mesh.shape['stage']
    n_dev = mesh.shape['expert']
    to_next = [(stage_idx, (stage_idx + 1) % n_stage) for stage_idx in range(n_stage)]
    to_prev = [((stage_idx + 1) % n_stage, stage_idx) for stage_idx in range(n_stage)]
    tok_spec = P('stage', 'expert', None)
    w_spec = P('stage', 'expert', None, None)
    same_core = [list(range(core, n_dev, CORES)) for core in range(CORES)]
    n_fwd = len(FWD_CHUNKS)

    def moe_body(x_act, route_idx, route_wts, w_one, w_three, w_two, dy_act):
        x_src = x_act[0]
        n_tok, _ = x_src.shape
        n_local = w_one.shape[1]
        n_exp = n_local * n_dev

        def gather(rows):
            return lax.all_gather(rows, 'expert', axis=0, tiled=False)

        def reduce_rows(part):
            return lax.psum_scatter(part, 'expert', scatter_dimension=0, axis_index_groups=same_core, tiled=False).astype(BF16)

        hits = route_idx[0][:, :, None] == jnp.arange(n_exp, dtype=jnp.int32)
        gate_src = jnp.sum(jnp.where(hits, route_wts[0][:, :, None], 0.0), axis=1)
        gate_src = jnp.transpose(gate_src.reshape(n_tok, n_dev, n_local), (1, 2, 0))
        gate_dst = lax.ppermute(gate_src, 'stage', to_next)
        gates = jnp.transpose(lax.all_to_all(gate_dst, 'expert', 0, 0), (0, 2, 1))

        w13 = jnp.concatenate([w_one[0], w_three[0]], axis=2)
        w2 = w_two[0]

        half = n_tok // 2
        carried = ()
        start = 0
        for k, (rows, tile) in enumerate(FWD_CHUNKS):
            x_dst = lax.ppermute(x_src[start:start + rows], 'stage', to_next)
            x_all = gather(x_dst)
            if k == 0:
                x_first = x_all
            y_part = expert_fwd(x_all, gates[:, start:start + rows], w13, w2, tile, start, n_tok, carried, k)
            carried = (y_part,)
            start += rows
        y_out = reduce_rows(y_part)

        x_again, _ = lax.optimization_barrier((x_src, x_first))
        both = []
        for rows in (slice(0, half), slice(half, n_tok)):
            x_dst = lax.ppermute(x_again[rows], 'stage', to_next)
            both.append(gather(jnp.stack([dy_act[0, rows], x_dst])))
        lo, hi = both

        lo_now, _ = lax.optimization_barrier((lo, y_part))
        carried = expert_bwd(lo_now, gates, w13, w2, 0, n_tok, [(0, 0, 0, half)], (), n_fwd)
        cut = DX_SPLIT - half
        carried = expert_bwd(hi, gates, w13, w2, half, n_tok, [(0, half, 0, cut), (1, 0, cut, half - cut)], carried, n_fwd + 1)
        dx_parts = []
        for k in range(2):
            dx_dst = reduce_rows(carried[k])
            dx_parts.append(lax.ppermute(dx_dst, 'stage', to_prev))
        dx_out = jnp.concatenate(dx_parts, axis=0)

        g_one, g_three, g_two = weight_grads(lo, hi, gates, *carried[2:])
        return y_out[None], dx_out[None], g_one[None], g_three[None], g_two[None]

    return jax.shard_map(moe_body, mesh=mesh, in_specs=(tok_spec, tok_spec, tok_spec, w_spec, w_spec, w_spec, tok_spec), out_specs=(tok_spec, tok_spec, w_spec, w_spec, w_spec), check_vma=False)
```

time: 1480 us -> 1540 us (1.041)
  waiting for transfers between devices: 473 us -> 542 us
  Pallas kernels: 935 us -> 900 us
    unnamed x14 -> x10, waiting for transfers between devices: 225 us -> 348 us
    all_gather x4, waiting for transfers between devices: 63.7 us -> 7.97 us  [gather(): return lax.all_gather(rows, 'expert', axis=0, tiled=False)]
    pallas_call x5 -> x4, Pallas kernels: 701 us -> 665 us  [the longest x2 418 us: expert_bwd(): pl.pallas_call(functools.partial(bwd_body, ffn, n_local, half, steps, pie...]
    ppermute x1 -> x2, waiting for transfers between devices: 89.7 us -> 91.7 us  [moe_body(): x_dst = lax.ppermute(x_again[rows], 'stage', to_next)]
  transfers between devices with their start and end apart: 17 -> 15, of which waited for: 7 -> 9; matrix products, arithmetic and copies ran while one was open for 3% -> 3% of each run, Pallas kernels for 63% -> 45%
where the time goes in v3:
time: 1540 us; the launch traced here: 1530 us
  Pallas kernels  900 us (58%)
  waiting for transfers between devices  542 us (35%)
  other arithmetic  38.4 us (2%)
  local copies, waits for them, and re-layouts  21.3 us (1%)
  starting transfers between devices  16.4 us (1%)
    pallas_call x2, Pallas kernels, expert_bwd(): pl.pallas_call(functools.partial(bwd_body, ffn, n_local, half, steps, pie...  418 us
    unnamed x10, waiting for transfers between devices  348 us
    pallas_call x2, Pallas kernels, expert_fwd(): pl.pallas_call(functools.partial(fwd_body, ffn, n_local, half, steps, sta...  247 us
    pallas_call x1, Pallas kernels, weight_grads(): pl.pallas_call(functools.partial(grad_body, ffn), grid=(n_local, n_src),...  235 us
    ppermute x2, waiting for transfers between devices, moe_body(): x_dst = lax.ppermute(x_again[rows], 'stage', to_next)  91.7 us
    ppermute x2, waiting for transfers between devices, moe_body(): x_dst = lax.ppermute(x_src[start:start + rows], 'stage', to_next)  90.7 us
  transfers between devices with their start and end apart: 15, of which 9 were waited for; matrix products, arithmetic and copies ran while one was open for 3% of the time, Pallas kernels for 45%

profile of v3, /device:TPU:0, one launch (start us, length us, event | category | flops | bytes accessed | tf_op | source)
XLA Modules:
  0.0 1532.0 jit_solution(4083519114458001642)
XLA Ops:
  8.7 3.3 collective-permute-start.2
  12.0 34.4 %collective-permute-done.2 = bf16[384,2048]{1,0:T(8,128)(2,1)S(1)} collective-permute-done((bf16[384,2048]{1,0:T(8,128)(2,1)S(1)}, bf16[384,2048]{1,0:T(8,128)(2,1)S(1)}, u32[]{:S(2)}, u32[]{:S(2)}) %collective-permute-start.2) | collective-permute-done | bytes 1572896 | tf_op jit(solution)/shard_map/ppermute | solution.py:372
  51.5 56.3 %collective-permute-done = bf16[640,2048]{1,0:T(8,128)(2,1)S(1)} collective-permute-done((bf16[640,2048]{1,0:T(8,128)(2,1)S(1)}, bf16[640,2048]{1,0:T(8,128)(2,1)S(1)}, u32[]{:S(2)}, u32[]{:S(2)}) %collective-permute-start) | collective-permute-done | bytes 2621472 | tf_op jit(solution)/shard_map/ppermute | solution.py:372
  109.4 7.9 all-gather.11.cloned.1.call-done
  117.3 4.2 fusion.1
  123.4 45.9 %collective-permute-done.4 = bf16[512,2048]{1,0:T(8,128)(2,1)S(1)} collective-permute-done((bf16[512,2048]{1,0:T(8,128)(2,1)S(1)}, bf16[512,2048]{1,0:T(8,128)(2,1)S(1)}, u32[]{:S(2)}, u32[]{:S(2)}) %collective-permute-start.4) | collective-permute-done | bytes 2097184 | tf_op jit(solution)/shard_map/ppermute | solution.py:384
  173.2 45.8 %collective-permute-done.3 = bf16[512,2048]{1,0:T(8,128)(2,1)S(1)} collective-permute-done((bf16[512,2048]{1,0:T(8,128)(2,1)}, bf16[512,2048]{1,0:T(8,128)(2,1)S(1)}, u32[]{:S(2)}, u32[]{:S(2)}) %collective-permute-start.3) | collective-permute-done | bytes 2097184 | tf_op jit(solution)/shard_map/ppermute | solution.py:384
  223.9 3.5 collective-permute-done.1
  228.2 3.4 all-to-all-start
  231.9 15.0 pad_maximum_fusion.w13_ref
  249.6 2.7 slice.41.g_ref
  252.3 3.4 slice.40.g_ref
  255.8 94.3 %expert_fwd.2 = (f32[4,1024,2048]{2,1,0:T(8,128)}, f32[4,384,2048]{2,1,0:T(8,128)}) custom-call(bf16[8,384,2048]{2,1,0:T(8,128)(2,1)} %bitcast.50, f32[8,384,4]{2,1,0:T(8,128)} %slice.41.g_ref, bf16[4,2048,1024]{2,1,0:T(8,128)(2,1)} %pad_maximum_fusion.w13_ref, bf16[4,512,2048]{2,1,0:T(8,128)(2,1)} %bitcast.51), custom_call_target="tpu_custom_call" | custom-call | flops 77309411328 | bytes 37748736 | tf_op jit(solution)/shard_map/expert_fwd/pallas_call | solution.py:182
  350.1 153.2 %expert_fwd.3 = (f32[4,1024,2048]{2,1,0:T(8,128)}, f32[4,640,2048]{2,1,0:T(8,128)}) custom-call(bf16[8,640,2048]{2,1,0:T(8,128)(2,1)} %bitcast.49, f32[8,640,4]{2,1,0:T(8,128)} %slice.40.g_ref, bf16[4,2048,1024]{2,1,0:T(8,128)(2,1)} %pad_maximum_fusion.w13_ref, bf16[4,512,2048]{2,1,0:T(8,128)(2,1)} %bitcast.52, ...), custom_call_target="tpu_custom_call", output_to_operand_aliasing={{0}: (4, {})} | custom-call | flops 128849018880 | bytes 62914560 | tf_op jit(solution)/shard_map/expert_fwd/pallas_call | solution.py:182
  503.3 209.2 %expert_bwd.2 = (f32[4,768,2048]{2,1,0:T(8,128)}, f32[4,256,2048]{2,1,0:T(8,128)}, bf16[8,1024,4096]{2,1,0:T(8,128)(2,1)}, bf16[8,1024,2048]{2,1,0:T(8,128)(2,1)}, f32[4,512,2048]{2,1,0:T(8,128)}) custom-call(bf16[8,2,512,2048]{3,2,1,0:T(8,128)(2,1)} %bitcast.43, bf16[8,2,512,2048]{3,2,1,0:T(8,128)(2,1)} %bitcast.44, f32[8,1024,4]{2,1,0:T(8,128)} %bitcast.33, ...), custom_call_target="tpu_custom_call" | custom-call | flops 171798691840 | bytes 117440512 | tf_op jit(solution)/shard_map/expert_bwd/pallas_call | solution.py:249
  712.5 208.6 %expert_bwd.3 = (f32[4,768,2048]{2,1,0:T(8,128)}, f32[4,256,2048]{2,1,0:T(8,128)}, bf16[8,1024,4096]{2,1,0:T(8,128)(2,1)}, bf16[8,1024,2048]{2,1,0:T(8,128)(2,1)}, f32[4,512,2048]{2,1,0:T(8,128)}) custom-call(bf16[8,2,512,2048]{3,2,1,0:T(8,128)(2,1)} %bitcast.46, ...), custom_call_target="tpu_custom_call", output_to_operand_aliasing={{0}: (5, {}), {1}: (6, {}), {2}: (7, {}), {3}: (8, {})} | custom-call | flops 171798691840 | bytes 117440512 | tf_op jit(solution)/shard_map/expert_bwd/pallas_call | solution.py:249
  922.5 82.8 %reduce-scatter.14.cloned.1.call-done = f32[1,256,2048]{2,1,0:T(8,128)} async-done(((f32[4,256,2048]{2,1,0:T(8,128)}), f32[1,256,2048]{2,1,0:T(8,128)}) %reduce-scatter.14.cloned.1.call-update) | async-done | bytes 2097168
  1005.3 2.7 convert_bitcast_fusion.1
  1009.5 216.7 %reduce-scatter.12.cloned.1.call-done = f32[1,768,2048]{2,1,0:T(8,128)} async-done(((f32[4,768,2048]{2,1,0:T(8,128)}), f32[1,768,2048]{2,1,0:T(8,128)}) %reduce-scatter.12.cloned.1.call-update) | async-done | bytes 6291472
  1226.2 4.9 convert_bitcast_fusion
  1232.6 234.5 %weight_grads.1 = (bf16[4,2048,512]{2,1,0:T(8,128)(2,1)}, bf16[4,2048,512]{2,1,0:T(8,128)(2,1)}, bf16[4,512,2048]{2,1,0:T(8,128)(2,1)}) custom-call(bf16[8,2,512,2048]{3,2,1,0:T(8,128)(2,1)} %bitcast.45, bf16[8,2,512,2048]{3,2,1,0:T(8,128)(2,1)} %bitcast.48, f32[8,1024,4]{2,1,0:T(8,128)} %bitcast.35, bf16[8,1024,4096]{2,1,0:T(8,128)(2,1)} %get-tuple-element.30.da_ref, ...), custom_call_target="tpu_custom_call" | custom-call | flops 206158430208 | bytes 268435456 | tf_op jit(solution)/shard_map/weight_grads/pallas_call | solution.py:310
  1467.1 46.9 %reduce-scatter.10.cloned.1.call-done = f32[1,1024,2048]{2,1,0:T(8,128)} async-done(((f32[4,1024,2048]{2,1,0:T(8,128)}), f32[1,1024,2048]{2,1,0:T(8,128)}) %reduce-scatter.10.cloned.1.call-update) | async-done | bytes 8388624
  1514.1 6.0 convert_element_type.16
  1520.1 4.8 maximum_bitcast_fusion
  (46 shorter events, 26.9 us)
Async XLA Ops:
  7.2 110.1 %all-gather.11.cloned.1.call-start = ((), (), s32[]{:S(2)}) async-start(), calls=%async_computation.5 | async-start | bytes 14155776 | tf_op jit(solution)/shard_map/all_gather | solution.py:354
  8.7 37.7 %collective-permute-start.2 = (bf16[384,2048]{1,0:T(8,128)(2,1)S(1)}, bf16[384,2048]{1,0:T(8,128)(2,1)S(1)}, u32[]{:S(2)}, u32[]{:S(2)}) collective-permute-start(bf16[384,2048]{1,0:T(8,128)(2,1)S(1)} %slice_bitcast_fusion.1), channel_id=1, source_target_pairs={{0,8},{8,0},{1,9},{9,1},{2,10},{10,2},{3,11},{11,3},{4,12},{12,4},... | collective-permute-start | bytes 4718600 | tf_op jit(solution)/shard_map/ppermute | solution.py:372
  46.4 1.1 copy-start.2
  47.6 302.5 %all-gather.9.cloned.1.call-start = ((), (), s32[]{:S(2)}) async-start(), calls=%async_computation.4 | async-start | bytes 23592960 | tf_op jit(solution)/shard_map/all_gather | solution.py:354
  49.7 58.1 %collective-permute-start = (bf16[640,2048]{1,0:T(8,128)(2,1)S(1)}, bf16[640,2048]{1,0:T(8,128)(2,1)S(1)}, u32[]{:S(2)}, u32[]{:S(2)}) collective-permute-start(bf16[640,2048]{1,0:T(8,128)(2,1)S(1)} %slice_bitcast_fusion), channel_id=1, source_target_pairs={{0,8},{8,0},{1,9},{9,1},{2,10},{10,2},{3,11},{11,3},{4,12},{12,4},... | collective-permute-start | bytes 7864328 | tf_op jit(solution)/shard_map/ppermute | solution.py:372
  107.8 1.5 copy-start.1
  109.3 394.0 %all-gather.15.cloned.1.call-start = ((), (), s32[]{:S(2)}) async-start(), calls=%async_computation.7 | async-start | bytes 37748736 | tf_op jit(solution)/shard_map/all_gather | solution.py:354
  117.3 5.7 copy-start
  121.5 47.8 %collective-permute-start.4 = (bf16[512,2048]{1,0:T(8,128)(2,1)S(1)}, bf16[512,2048]{1,0:T(8,128)(2,1)S(1)}, u32[]{:S(2)}, u32[]{:S(2)}) collective-permute-start(bf16[512,2048]{1,0:T(8,128)(2,1)S(1)} %get-tuple-element.37), channel_id=1, source_target_pairs={{0,8},{8,0},{1,9},{9,1},{2,10},{10,2},{3,11},{11,3},{4,12},{12,4},... | collective-permute-start | bytes 6291464 | tf_op jit(solution)/shard_map/ppermute | solution.py:384
  171.7 540.9 %all-gather.13.cloned.1.call-start = ((), (), s32[]{:S(2)}) async-start(), calls=%async_computation.6 | async-start | bytes 37748736 | tf_op jit(solution)/shard_map/all_gather | solution.py:354
  171.7 47.3 %collective-permute-start.3 = (bf16[512,2048]{1,0:T(8,128)(2,1)}, bf16[512,2048]{1,0:T(8,128)(2,1)S(1)}, u32[]{:S(2)}, u32[]{:S(2)}) collective-permute-start(bf16[512,2048]{1,0:T(8,128)(2,1)} %get-tuple-element.38), channel_id=1, source_target_pairs={{0,8},{8,0},{1,9},{9,1},{2,10},{10,2},{3,11},{11,3},{4,12},{12,4},... | collective-permute-start | bytes 6291464 | tf_op jit(solution)/shard_map/ppermute | solution.py:384
  221.4 0.8 copy-start.3
  221.4 0.8 copy-start.4
  222.4 5.0 collective-permute-start.1
  228.2 18.8 %all-to-all-start = ((f32[8,4,1024]{2,1,0:T(4,128)}), f32[8,4,1024]{2,1,0:T(4,128)S(1)}, u32[]{:S(2)}, u32[]{:S(2)}) async-start(f32[8,4,1024]{2,1,0:T(4,128)} %copy.28), calls=%async_computation | async-start | bytes 262144 | tf_op jit(solution)/shard_map/all_to_all | solution.py:363
  231.6 773.7 %reduce-scatter.14.cloned.1.call-start = ((), (), s32[]{:S(2)}) async-start(), calls=%async_computation.10 | async-start | bytes 10485760
  921.2 305.0 %reduce-scatter.12.cloned.1.call-start = ((), (), s32[]{:S(2)}) async-start(), calls=%async_computation.9 | async-start | bytes 31457280
  921.8 592.3 %reduce-scatter.10.cloned.1.call-start = ((), (), s32[]{:S(2)}) async-start(), calls=%async_computation.8 | async-start | bytes 41943040
  1008.0 512.1 %collective-permute-start.6 = (bf16[256,2048]{1,0:T(8,128)(2,1)}, bf16[256,2048]{1,0:T(8,128)(2,1)}, u32[]{:S(2)}, u32[]{:S(2)}) collective-permute-start(bf16[256,2048]{1,0:T(8,128)(2,1)} %convert_bitcast_fusion.1), channel_id=1, source_target_pairs={{8,0},{0,8},{9,1},{1,9},{10,2},{2,10},{11,3},{3,11},{12,4},{4,12},... | collective-permute-start | bytes 3145736 | tf_op jit(solution)/shard_map/ppermute | solution.py:395
  1231.1 289.0 %collective-permute-start.5 = (bf16[768,2048]{1,0:T(8,128)(2,1)}, bf16[768,2048]{1,0:T(8,128)(2,1)}, u32[]{:S(2)}, u32[]{:S(2)}) collective-permute-start(bf16[768,2048]{1,0:T(8,128)(2,1)} %convert_bitcast_fusion), channel_id=1, source_target_pairs={{8,0},{0,8},{9,1},{1,9},{10,2},{2,10},{11,3},{3,11},{12,4},{4,12},... | collective-permute-start | bytes 9437192 | tf_op jit(solution)/shard_map/ppermute | solution.py:395
Sparse Core Ops, SparseCore 0:
  47.7 69.4 all-gather.10
  119.7 103.6 all-gather.8
  225.8 158.8 all-gather.14
  387.0 159.4 all-gather.12
  921.3 83.9 reduce-scatter.13
  1008.2 217.9 reduce-scatter.11
  1229.2 284.7 reduce-scatter.9

commit v4 on v3

--- a/solution.py
+++ b/solution.py
@@ -10,9 +10,9 @@
 
 F32 = jnp.float32
 BF16 = jnp.bfloat16
-FWD_CHUNKS = ((384, 384), (640, 320))
-BWD_TILE = 512
-DX_SPLIT = 768
+FWD_CHUNKS = ((256, 256), (768, 256))
+FWD_STAGES = (0, 7, 13, 19)
+BWD_STAGES = (0, 2, 4, 6)
 VMEM_LIMIT = 65400 * 1024
 N_ACC = 3
 CORES = 2
@@ -44,7 +44,7 @@
     return CORES * (tile // steps) + lane, lax.rem(tile, steps)
 
 
-def pair_sum(compute, half, steps, tile, inbox_ref, pieces, acc_ref, send_sem, recv_sem, in_sem, out_sem):
+def pair_sum(compute, half, steps, tile, inbox_ref, pieces, exchange, acc_ref, send_sem, recv_sem, in_sem, out_sem):
     step = pl.program_id(0)
     last = 2 * half - 1
     me = lax.axis_index('expert')
@@ -83,9 +83,14 @@
 
     @pl.when(step == 0)
     def _():
+        peers = [other] + (exchange.peers if exchange else [])
         barrier = pltpu.get_barrier_semaphore()
-        pl.semaphore_signal(barrier, inc=1, device_id={'expert': other}, device_id_type=MESH)
-        pl.semaphore_wait(barrier, 1)
+        for peer in peers:
+            pl.semaphore_signal(barrier, inc=1, device_id={'expert': peer}, device_id_type=MESH)
+        pl.semaphore_wait(barrier, len(peers))
+
+    if exchange:
+        exchange.advance(step)
 
     back = step - (N_ACC - 1)
 
@@ -128,21 +133,139 @@
     def _():
         for job in range(half - N_ACC + 1, half):
             Store(job).wait()
-
-
-def fwd_body(ffn, n_local, half, steps, start, n_carried, x_ref, g_ref, w13_ref, w2_ref, *refs):
+        if exchange:
+            exchange.finish()
+
+
+class Exchange:
+    def __init__(self, ref, send_sem, recv_sem, stages):
+        me = lax.axis_index('expert')
+        flip = lambda dev, bit: dev + bit - 2 * bit * lax.rem(dev // bit, 2)
+        core, x, y = flip(me, 1), flip(me, 2), flip(me, 4)
+        diag = flip(x, 4)
+        self.peers = [x, y]
+        self.stages = stages
+        rows = ref.shape[1] // 2
+        first, second, both = pl.ds(0, rows), pl.ds(rows, rows), pl.ds(0, 2 * rows)
+        plan = [
+            (first, me, x, x),
+            (second, me, y, y),
+            (second, me, x, x),
+            (first, me, y, y),
+            (both, me, core, core),
+            (first, x, diag, y),
+            (second, y, diag, x),
+            (first, x, flip(x, 1), core),
+            (second, y, flip(y, 1), core),
+            (second, x, flip(x, 1), core),
+            (first, y, flip(y, 1), core),
+            (first, diag, flip(diag, 1), core),
+            (second, diag, flip(diag, 1), core),
+        ]
+
+        def copy(k, block):
+            part, _, _, to = plan[k]
+            return pltpu.make_async_remote_copy(
+                src_ref=ref.at[block, part], dst_ref=ref.at[block, part], send_sem=send_sem.at[k], recv_sem=recv_sem.at[k],
+                device_id={'expert': to}, device_id_type=MESH)
+
+        self.out = [copy(k, plan[k][1]) for k in range(len(plan))]
+        self.into = [copy(k, plan[k][2]) for k in range(len(plan))]
+
+    def advance(self, step):
+        for at, arrived, started in zip(self.stages, ((), (0, 1), (2, 3), (5, 6)), ((0, 1, 2, 3, 4), (5, 6, 7, 8), (9, 10), (11, 12))):
+            @pl.when(step == at)
+            def _(arrived=arrived, started=started):
+                for k in arrived:
+                    self.into[k].wait_recv()
+                for k in started:
+                    self.out[k].start()
+
+    def finish(self):
+        for k in (4,) + tuple(range(7, 13)):
+            self.into[k].wait_recv()
+        for copy in self.out:
+            copy.wait_send()
+
+
+N_COPIES = 13
+EXCHANGE_SEMS = [pltpu.SemaphoreType.DMA((N_COPIES,)), pltpu.SemaphoreType.DMA((N_COPIES,))]
+
+
+def place_body(x_ref, out_ref):
+    out_ref[0] = x_ref[...]
+
+
+def place(x, first, rows, n_dev):
+    model = x.shape[1]
+    return pl.pallas_call(
+        place_body,
+        grid=(1,),
+        in_specs=[pl.BlockSpec((rows, model), lambda i: (first // rows, 0))],
+        out_specs=pl.BlockSpec((1, rows, model), lambda i: (lax.axis_index('expert'), 0, 0)),
+        out_shape=jax.ShapeDtypeStruct((n_dev, rows, model), x.dtype),
+        name='place',
+    )(x)
+
+
+class Weights:
+    def __init__(self, n_local, hbm, vmem, sem):
+        self.copies = [[pltpu.make_async_copy(src.at[e], dst.at[e], sem.at[e, k]) for k, (src, dst) in enumerate(zip(hbm, vmem))]
+                       for e in range(n_local)]
+        self.at = lambda e: [pltpu.make_async_copy(src.at[e], dst.at[e], sem.at[e, k]) for k, (src, dst) in enumerate(zip(hbm, vmem))]
+
+    def start(self):
+        for pair in self.copies:
+            for copy in pair:
+                copy.start()
+
+    def wait(self, e):
+        for copy in self.at(e):
+            copy.wait()
+
+
+def weight_scratch(w13, w2):
+    return [pltpu.VMEM(w13.shape, BF16), pltpu.VMEM(w2.shape, BF16), pltpu.SemaphoreType.DMA((w13.shape[0], 2))]
+
+
+def fwd_body(ffn, n_local, half, steps, start, stages, n_carried, x_ref, g_ref, w13_hbm, w2_hbm, *refs):
     y_ref, inbox_ref = refs[n_carried:n_carried + 2]
+    rest = list(refs[n_carried + 2:])
+    buf_ref = rest.pop(0) if stages else None
+    w13_ref, w2_ref, w_sem = rest[:3]
+    scratch = rest[3:8]
+    exchange = Exchange(buf_ref, *rest[8:], stages) if stages else None
     tile = x_ref.shape[1]
+    weights = Weights(n_local, (w13_hbm, w2_hbm), (w13_ref, w2_ref), w_sem)
+    step = pl.program_id(0)
+
+    def expert(acc, e):
+        gate = gate_column(g_ref[0], e)
+        pre = dot(x_ref[0], w13_ref[e])
+        one, three = pre[:, :ffn], pre[:, ffn:]
+        hidden = jnp.where(gate > 0.0, one * jax.nn.sigmoid(one) * three, 0.0).astype(BF16)
+        acc[...] += gate * dot(hidden, w2_ref[e]).astype(BF16).astype(F32)
 
     def compute(acc):
-        for e in range(n_local):
-            gate = gate_column(g_ref[0], e)
-            pre = dot(x_ref[0], w13_ref[e])
-            one, three = pre[:, :ffn], pre[:, ffn:]
-            hidden = jnp.where(gate > 0.0, one * jax.nn.sigmoid(one) * three, 0.0).astype(BF16)
-            acc[...] += gate * dot(hidden, w2_ref[e]).astype(BF16).astype(F32)
-
-    pair_sum(compute, half, steps, tile, inbox_ref, [(y_ref, start, 0, tile)], *refs[n_carried + 2:])
+        @pl.when(step == 0)
+        def _():
+            def one_by_one(e, carry):
+                weights.wait(e)
+                expert(acc, e)
+                return carry
+
+            lax.fori_loop(0, n_local, one_by_one, 0)
+
+        @pl.when(step > 0)
+        def _():
+            for e in range(n_local):
+                expert(acc, e)
+
+    @pl.when(step == 0)
+    def _():
+        weights.start()
+
+    pair_sum(compute, half, steps, tile, inbox_ref, [(y_ref, start, 0, tile)], exchange, *scratch)
 
 
 def pair_scratch(tile, model, half, n_pieces):
@@ -160,58 +283,71 @@
         dimension_semantics=('arbitrary',), vmem_limit_bytes=VMEM_LIMIT, collective_id=collective_id, has_side_effects=True)
 
 
-def whole(array):
-    return pl.BlockSpec(array.shape, lambda i: (0,) * array.ndim, pipeline_mode=pl.Buffered(1))
-
-
 HBM = pl.BlockSpec(memory_space=pl.ANY)
 
 
-def expert_fwd(x, gates, w13, w2, tile, start, n_tok, carried, collective_id):
+def expert_fwd(x, gates, w13, w2, tile, start, n_tok, carried, hosted, stages, collective_id):
     n_src, rows, model = x.shape
     n_local, ffn = w2.shape[:2]
     steps = rows // tile
     n_own = n_src // CORES
     half = n_own * steps
     flops = 2 * n_src * rows * n_local * model * ffn * 3
+    extra = list(carried) + list(hosted)
 
     def at(i):
         src, t = pair_source(i, half, steps)
         return src, t, 0
 
-    return pl.pallas_call(
-        functools.partial(fwd_body, ffn, n_local, half, steps, start, len(carried)),
+    aliases = {4 + i: i for i in range(len(carried))}
+    aliases.update({4 + len(carried) + i: 2 + i for i in range(len(hosted))})
+    outs = pl.pallas_call(
+        functools.partial(fwd_body, ffn, n_local, half, steps, start, stages, len(extra)),
         grid=(2 * half,),
         in_specs=[
             pl.BlockSpec((1, tile, model), at),
             pl.BlockSpec((1, tile, n_local), at),
-            whole(w13),
-            whole(w2),
-        ] + [HBM] * len(carried),
-        out_specs=[HBM, HBM],
-        out_shape=[jax.ShapeDtypeStruct((n_own, n_tok, model), F32), jax.ShapeDtypeStruct((n_own, rows, model), F32)],
-        scratch_shapes=pair_scratch(tile, model, half, 1),
-        input_output_aliases={4 + i: i for i in range(len(carried))},
+            HBM,
+            HBM,
+        ] + [HBM] * len(extra),
+        out_specs=[HBM] * (2 + len(hosted)),
+        out_shape=[jax.ShapeDtypeStruct((n_own, n_tok, model), F32), jax.ShapeDtypeStruct((n_own, rows, model), F32)]
+        + [jax.ShapeDtypeStruct(h.shape, h.dtype) for h in hosted],
+        scratch_shapes=weight_scratch(w13, w2) + pair_scratch(tile, model, half, 1) + EXCHANGE_SEMS * len(hosted),
+        input_output_aliases=aliases,
         compiler_params=pair_params(collective_id),
         cost_estimate=pl.CostEstimate(flops=flops, bytes_accessed=n_src * rows * model * 6, transcendentals=0),
         name='expert_fwd',
-    )(x, gates, w13, w2, *carried)[0]
-
-
-def bwd_body(ffn, n_local, half, steps, pieces, n_carried, x_ref, dy_ref, g_ref, w13_ref, w2_ref, *refs):
-    lo_ref, hi_ref, da_ref, h_ref, inbox_ref = refs[n_carried:n_carried + 5]
-    tile = x_ref.shape[2]
+    )(x, gates, w13, w2, *extra)
+    return outs[0], outs[2:]
+
+
+def bwd_body(ffn, n_local, half, steps, pieces, stages, n_carried, x_ref, dy_ref, g_ref, w13_hbm, w2_hbm, *refs):
+    refs = list(refs[n_carried:])
+    n_out = len(pieces)
+    outs, (da_ref, h_ref, inbox_ref), rest = refs[:n_out], refs[n_out:n_out + 3], refs[n_out + 3:]
+    buf_ref = rest.pop(0) if stages else None
+    w13_ref, w2_ref, w_sem = rest[:3]
+    scratch = rest[3:8]
+    exchange = Exchange(buf_ref, *rest[8:], stages) if stages else None
+    tile = g_ref.shape[1]
+    weights = Weights(n_local, (w13_hbm, w2_hbm), (w13_ref, w2_ref), w_sem)
+    step = pl.program_id(0)
 
     def compute(acc):
         def expert(e, carry):
+            @pl.when(step == 0)
+            def _():
+                weights.wait(e)
+
             gate = gate_column(g_ref[0], e)
             live = gate > 0.0
-            pre = dot(x_ref[0, 0], w13_ref[e])
+            pre = dot(x_ref[...].reshape(tile, x_ref.shape[-1]), w13_ref[e])
             one, three = pre[:, :ffn], pre[:, ffn:]
             sig = jax.nn.sigmoid(one)
             act = one * sig
             h_ref[0, :, pl.ds(pl.multiple_of(e * ffn, ffn), ffn)] = jnp.where(live, act * three, 0.0).astype(BF16)
-            d_out = (gate * dy_ref[0, 0].astype(F32)).astype(BF16)
+            d_out = (gate * dy_ref[...].reshape(tile, dy_ref.shape[-1]).astype(F32)).astype(BF16)
             d_hid = dot_t(d_out, w2_ref[e]).astype(BF16).astype(F32)
             d_one = jnp.where(live, d_hid * three * sig * (1.0 + one * (1.0 - sig)), 0.0).astype(BF16)
             d_three = jnp.where(live, d_hid * act, 0.0).astype(BF16)
@@ -222,64 +358,67 @@
 
         lax.fori_loop(0, n_local, expert, 0)
 
-    outs = [((lo_ref, hi_ref)[which], first, row, rows) for which, first, row, rows in pieces]
-    pair_sum(compute, half, steps, tile, inbox_ref, outs, *refs[n_carried + 5:])
-
-
-def expert_bwd(rows_in, gates, w13, w2, start, n_tok, pieces, carried, collective_id):
-    n_src, _, rows, model = rows_in.shape
+    @pl.when(step == 0)
+    def _():
+        weights.start()
+
+    places = [(ref, 0, row, rows) for ref, (row, rows) in zip(outs, pieces)]
+    pair_sum(compute, half, steps, tile, inbox_ref, places, exchange, *scratch)
+
+
+def expert_bwd(x, dy, which, gates, w13, w2, start, pieces, carried, hosted, stages, collective_id):
+    n_src, model = x.shape[0], x.shape[-1]
+    n_tok = gates.shape[1]
     n_local, ffn = w2.shape[:2]
-    tile = min(BWD_TILE, rows)
-    steps = rows // tile
-    n_own = n_src // CORES
-    half = n_own * steps
-    flops = 2 * n_src * rows * n_local * model * ffn * 5
-
-    def rows_of(which):
+    tile = x.shape[-2]
+    steps = 1
+    half = n_src // CORES
+    flops = 2 * n_src * tile * n_local * model * ffn * 5
+    extra = list(carried) + list(hosted)
+    n_out = len(pieces)
+
+    def rows_of(array, k):
         def index(i):
             src, t = pair_source(i, half, steps)
-            return src, which, t, 0
-
-        return index
+            return (src, t, 0) if array.ndim == 3 else (src, k, t, 0)
+
+        return pl.BlockSpec((1,) * (array.ndim - 2) + (tile, model), index)
 
     def at(i):
         src, t = pair_source(i, half, steps)
         return src, start // tile + t, 0
 
+    aliases = {5 + i: n_out + i for i in range(len(carried))}
+    aliases.update({5 + len(carried) + i: n_out + 3 + i for i in range(len(hosted))})
     outs = pl.pallas_call(
-        functools.partial(bwd_body, ffn, n_local, half, steps, pieces, len(carried)),
+        functools.partial(bwd_body, ffn, n_local, half, steps, pieces, stages, len(extra)),
         grid=(2 * half,),
         in_specs=[
-            pl.BlockSpec((1, 1, tile, model), rows_of(1)),
-            pl.BlockSpec((1, 1, tile, model), rows_of(0)),
+            rows_of(x, which[0]),
+            rows_of(dy, which[1]),
             pl.BlockSpec((1, tile, n_local), at),
-            whole(w13),
-            whole(w2),
-        ] + [HBM] * len(carried),
-        out_specs=[
             HBM,
             HBM,
+        ] + [HBM] * len(extra),
+        out_specs=[HBM] * n_out + [
             pl.BlockSpec((1, tile, 2 * ffn * n_local), at),
             pl.BlockSpec((1, tile, ffn * n_local), at),
-            HBM,
-        ],
-        out_shape=[
-            jax.ShapeDtypeStruct((n_own, DX_SPLIT, model), F32),
-            jax.ShapeDtypeStruct((n_own, n_tok - DX_SPLIT, model), F32),
+        ] + [HBM] * (1 + len(hosted)),
+        out_shape=[jax.ShapeDtypeStruct((half, rows, model), F32) for _, rows in pieces] + [
             jax.ShapeDtypeStruct((n_src, n_tok, 2 * ffn * n_local), BF16),
             jax.ShapeDtypeStruct((n_src, n_tok, ffn * n_local), BF16),
-            jax.ShapeDtypeStruct((n_own, rows, model), F32),
-        ],
-        scratch_shapes=pair_scratch(tile, model, half, len(pieces)),
-        input_output_aliases={5 + i: i for i in range(len(carried))},
+            jax.ShapeDtypeStruct((half, tile, model), F32),
+        ] + [jax.ShapeDtypeStruct(h.shape, h.dtype) for h in hosted],
+        scratch_shapes=weight_scratch(w13, w2) + pair_scratch(tile, model, half, n_out) + EXCHANGE_SEMS * len(hosted),
+        input_output_aliases=aliases,
         compiler_params=pair_params(collective_id),
-        cost_estimate=pl.CostEstimate(flops=flops, bytes_accessed=n_src * rows * model * 14, transcendentals=0),
+        cost_estimate=pl.CostEstimate(flops=flops, bytes_accessed=n_src * tile * model * 14, transcendentals=0),
         name='expert_bwd',
-    )(rows_in, rows_in, gates, w13, w2, *carried)
-    return outs[:4]
-
-
-def grad_body(ffn, lo_ref, hi_ref, g_ref, da_ref, h_ref, dw1_ref, dw3_ref, dw2_ref, acc13_ref, acc2_ref):
+    )(x, dy, gates, w13, w2, *extra)
+    return outs[:n_out], outs[n_out:n_out + 2], outs[n_out + 3:]
+
+
+def grad_body(ffn, lo_ref, x_ref, dy_ref, g_ref, da_ref, h_ref, dw1_ref, dw3_ref, dw2_ref, acc13_ref, acc2_ref):
     e, k = pl.program_id(0), pl.program_id(1)
 
     @pl.when(k == 0)
@@ -287,8 +426,8 @@
         acc13_ref[...] = jnp.zeros_like(acc13_ref)
         acc2_ref[...] = jnp.zeros_like(acc2_ref)
 
-    acc13_ref[...] += dot_a(jnp.concatenate([lo_ref[0, 1], hi_ref[0, 1]], axis=0), da_ref[0])
-    d_out = jnp.concatenate([lo_ref[0, 0], hi_ref[0, 0]], axis=0).astype(F32)
+    acc13_ref[...] += dot_a(jnp.concatenate([lo_ref[0, 1], x_ref[0]], axis=0), da_ref[0])
+    d_out = jnp.concatenate([lo_ref[0, 0], dy_ref[0]], axis=0).astype(F32)
     d_out = (gate_column(g_ref[0], e) * d_out).astype(BF16)
     acc2_ref[...] += dot_a(h_ref[0], d_out)
 
@@ -299,7 +438,7 @@
         dw2_ref[0] = acc2_ref[...].astype(BF16)
 
 
-def weight_grads(lo, hi, gates, d_pre, hidden):
+def weight_grads(lo, x_hi, dy_hi, gates, d_pre, hidden):
     n_src, n_tok, n_local = gates.shape
     model = lo.shape[3]
     ffn = hidden.shape[2] // n_local
@@ -312,7 +451,8 @@
         grid=(n_local, n_src),
         in_specs=[
             pl.BlockSpec((1,) + lo.shape[1:], lambda e, k: (k, 0, 0, 0)),
-            pl.BlockSpec((1,) + hi.shape[1:], lambda e, k: (k, 0, 0, 0)),
+            pl.BlockSpec((1,) + x_hi.shape[1:], at),
+            pl.BlockSpec((1,) + dy_hi.shape[1:], at),
             pl.BlockSpec((1, n_tok, n_local), at),
             pl.BlockSpec((1, n_tok, 2 * ffn), at_e),
             pl.BlockSpec((1, n_tok, ffn), at_e),
@@ -331,7 +471,7 @@
         compiler_params=pltpu.CompilerParams(dimension_semantics=('arbitrary', 'arbitrary'), vmem_limit_bytes=VMEM_LIMIT),
         cost_estimate=pl.CostEstimate(flops=flops, bytes_accessed=n_src * n_tok * model * 4 * n_local, transcendentals=0),
         name='weight_grads',
-    )(lo, hi, gates, d_pre, hidden)
+    )(lo, x_hi, dy_hi, gates, d_pre, hidden)
 
 
 def solution(mesh):
@@ -366,6 +506,7 @@
         w2 = w_two[0]
 
         half = n_tok // 2
+        dy_hi = place(dy_act[0], half, half, n_dev)
         carried = ()
         start = 0
         for k, (rows, tile) in enumerate(FWD_CHUNKS):
@@ -373,29 +514,30 @@
             x_all = gather(x_dst)
             if k == 0:
                 x_first = x_all
-            y_part = expert_fwd(x_all, gates[:, start:start + rows], w13, w2, tile, start, n_tok, carried, k)
+            hosted, stages = ((dy_hi,), FWD_STAGES) if k == n_fwd - 1 else ((), ())
+            y_part, arrived = expert_fwd(x_all, gates[:, start:start + rows], w13, w2, tile, start, n_tok, carried, hosted, stages, k)
             carried = (y_part,)
             start += rows
+        dy_hi, = arrived
         y_out = reduce_rows(y_part)
 
         x_again, _ = lax.optimization_barrier((x_src, x_first))
-        both = []
-        for rows in (slice(0, half), slice(half, n_tok)):
-            x_dst = lax.ppermute(x_again[rows], 'stage', to_next)
-            both.append(gather(jnp.stack([dy_act[0, rows], x_dst])))
-        lo, hi = both
+        x_dst = lax.ppermute(x_again[:half], 'stage', to_next)
+        lo = gather(jnp.stack([dy_act[0, :half], x_dst]))
+        x_dst = lax.ppermute(x_again[half:], 'stage', to_next)
+        x_hi = place(x_dst, 0, half, n_dev)
 
         lo_now, _ = lax.optimization_barrier((lo, y_part))
-        carried = expert_bwd(lo_now, gates, w13, w2, 0, n_tok, [(0, 0, 0, half)], (), n_fwd)
-        cut = DX_SPLIT - half
-        carried = expert_bwd(hi, gates, w13, w2, half, n_tok, [(0, half, 0, cut), (1, 0, cut, half - cut)], carried, n_fwd + 1)
+        dx_lo, carried, (x_hi,) = expert_bwd(lo_now, lo_now, (1, 0), gates, w13, w2, 0, ((0, half),), (), (x_hi,), BWD_STAGES, n_fwd)
+        cut = half // 2
+        dx_hi, carried, _ = expert_bwd(x_hi, dy_hi, (0, 0), gates, w13, w2, half, ((0, cut), (cut, cut)), carried, (), (), n_fwd + 1)
         dx_parts = []
-        for k in range(2):
-            dx_dst = reduce_rows(carried[k])
+        for part in list(dx_lo) + list(dx_hi):
+            dx_dst = reduce_rows(part)
             dx_parts.append(lax.ppermute(dx_dst, 'stage', to_prev))
         dx_out = jnp.concatenate(dx_parts, axis=0)
 
-        g_one, g_three, g_two = weight_grads(lo, hi, gates, *carried[2:])
+        g_one, g_three, g_two = weight_grads(lo, x_hi, dy_hi, gates, *carried)
         return y_out[None], dx_out[None], g_one[None], g_three[None], g_two[None]
 
     return jax.shard_map(moe_body, mesh=mesh, in_specs=(tok_spec, tok_spec, tok_spec, w_spec, w_spec, w_spec, tok_spec), out_specs=(tok_spec, tok_spec, w_spec, w_spec, w_spec), check_vma=False)

time: 1540 us -> 1490 us (0.968)
  waiting for transfers between devices: 542 us -> 498 us
    ppermute x2, waiting for transfers between devices: 91.7 us -> 44.5 us  [the longest x1 44.5 us: moe_body(): x_dst = lax.ppermute(x_again[:half], 'stage', to_next)]
    unnamed x10 -> x11, waiting for transfers between devices: 348 us -> 357 us
  transfers between devices with their start and end apart: 15 -> 16, of which waited for: 9 -> 9; matrix products, arithmetic and copies ran while one was open for 3% -> 3% of each run, Pallas kernels for 45% -> 33%
where the time goes in v4:
time: 1490 us; the launch traced here: 1480 us
  Pallas kernels  899 us (60%)
  waiting for transfers between devices  498 us (33%)
  other arithmetic  36.5 us (2%)
  local copies, waits for them, and re-layouts  18.2 us (1%)
  starting transfers between devices  17.3 us (1%)
    pallas_call x2, Pallas kernels, expert_bwd(): pl.pallas_call(functools.partial(bwd_body, ffn, n_local, half, steps, pie...  409 us
    unnamed x11, waiting for transfers between devices  357 us
    pallas_call x2, Pallas kernels, expert_fwd(): pl.pallas_call(functools.partial(fwd_body, ffn, n_local, half, steps, sta...  249 us
    pallas_call x1, Pallas kernels, weight_grads(): pl.pallas_call(functools.partial(grad_body, ffn), grid=(n_local, n_src),...  235 us
    ppermute x2, waiting for transfers between devices, moe_body(): x_dst = lax.ppermute(x_src[start:start + rows], 'stage', to_next)  90.8 us
    ppermute x1, waiting for transfers between devices, moe_body(): x_dst = lax.ppermute(x_again[:half], 'stage', to_next)  44.5 us
  transfers between devices with their start and end apart: 16, of which 9 were waited for; matrix products, arithmetic and copies ran while one was open for 3% of the time, Pallas kernels for 33%

profile of v4, /device:TPU:0, one launch (start us, length us, event | category | flops | bytes accessed | tf_op | source)
XLA Modules:
  0.0 1483.8 jit_solution(5997546960218952487)
XLA Ops:
  8.5 3.3 collective-permute-start.2
  11.8 23.2 %collective-permute-done.2 = bf16[256,2048]{1,0:T(8,128)(2,1)S(1)} collective-permute-done((bf16[256,2048]{1,0:T(8,128)(2,1)S(1)}, bf16[256,2048]{1,0:T(8,128)(2,1)S(1)}, u32[]{:S(2)}, u32[]{:S(2)}) %collective-permute-start.2) | collective-permute-done | bytes 1048608 | tf_op jit(solution)/shard_map/ppermute | solution.py:513
  40.1 67.6 %collective-permute-done = bf16[768,2048]{1,0:T(8,128)(2,1)} collective-permute-done((bf16[768,2048]{1,0:T(8,128)(2,1)S(1)}, bf16[768,2048]{1,0:T(8,128)(2,1)}, u32[]{:S(2)}, u32[]{:S(2)}) %collective-permute-start) | collective-permute-done | bytes 3145760 | tf_op jit(solution)/shard_map/ppermute | solution.py:513
  107.8 4.1 fusion
  113.4 44.5 %collective-permute-done.3 = bf16[512,2048]{1,0:T(8,128)(2,1)S(1)} collective-permute-done((bf16[512,2048]{1,0:T(8,128)(2,1)S(1)}, bf16[512,2048]{1,0:T(8,128)(2,1)S(1)}, u32[]{:S(2)}, u32[]{:S(2)}) %collective-permute-start.3) | collective-permute-done | bytes 2097184 | tf_op jit(solution)/shard_map/ppermute | solution.py:525
  157.9 3.1 pad_maximum_fusion.1
  162.5 3.8 collective-permute-done.1
  167.1 3.4 all-to-all-start
  170.5 14.0 pad_maximum_fusion.w13_hbm
  184.5 3.1 place.2.refs_1_
  192.6 3.8 slice.36.g_ref
  197.9 63.8 %expert_fwd.2 = (f32[4,1024,2048]{2,1,0:T(8,128)}, f32[4,256,2048]{2,1,0:T(8,128)}) custom-call(bf16[8,256,2048]{2,1,0:T(8,128)(2,1)} %bitcast.52, f32[8,256,4]{2,1,0:T(8,128)} %slice.37.g_ref, bf16[4,2048,1024]{2,1,0:T(8,128)(2,1)} %pad_maximum_fusion.w13_hbm, bf16[4,512,2048]{2,1,0:T(8,128)(2,1)} %bitcast.48), custom_call_target="tpu_custom_call" | custom-call | flops 51539607552 | bytes 25165824 | tf_op jit(solution)/shard_map/expert_fwd/pallas_call | solution.py:304
  261.7 3.1 place.3.refs_0_
  264.8 185.6 %expert_fwd.3 = (f32[4,1024,2048]{2,1,0:T(8,128)}, f32[4,768,2048]{2,1,0:T(8,128)}, bf16[8,512,2048]{2,1,0:T(8,128)(2,1)}) custom-call(bf16[8,768,2048]{2,1,0:T(8,128)(2,1)} %bitcast.47, f32[8,768,4]{2,1,0:T(8,128)} %slice.36.g_ref, bf16[4,2048,1024]{2,1,0:T(8,128)(2,1)} %pad_maximum_fusion.w13_hbm, ...), custom_call_target="tpu_custom_call", output_to_operand_aliasing={{0}: (4, {}), {2}: (5, {})} | custom-call | flops 154618822656 | bytes 75497472 | tf_op jit(solution)/shard_map/expert_fwd/pallas_call | solution.py:304
  452.8 204.8 %expert_bwd.2 = (f32[4,512,2048]{2,1,0:T(8,128)}, bf16[8,1024,4096]{2,1,0:T(8,128)(2,1)}, bf16[8,1024,2048]{2,1,0:T(8,128)(2,1)}, f32[4,512,2048]{2,1,0:T(8,128)}, bf16[8,512,2048]{2,1,0:T(8,128)(2,1)}) custom-call(bf16[8,2,512,2048]{3,2,1,0:T(8,128)(2,1)} %bitcast.44, bf16[8,2,512,2048]{3,2,1,0:T(8,128)(2,1)} %bitcast.45, ...), custom_call_target="tpu_custom_call", output_to_operand_aliasing={{4}: (5, {})} | custom-call | flops 171798691840 | bytes 117440512 | tf_op jit(solution)/shard_map/expert_bwd/pallas_call | solution.py:393
  657.7 204.0 %expert_bwd.3 = (f32[4,256,2048]{2,1,0:T(8,128)}, f32[4,256,2048]{2,1,0:T(8,128)}, bf16[8,1024,4096]{2,1,0:T(8,128)(2,1)}, bf16[8,1024,2048]{2,1,0:T(8,128)(2,1)}, f32[4,512,2048]{2,1,0:T(8,128)}) custom-call(bf16[8,512,2048]{2,1,0:T(8,128)(2,1)} %get-tuple-element.26.x_ref, ...), custom_call_target="tpu_custom_call", output_to_operand_aliasing={{2}: (5, {}), {3}: (6, {})} | custom-call | flops 171798691840 | bytes 117440512 | tf_op jit(solution)/shard_map/expert_bwd/pallas_call | solution.py:393
  863.7 80.8 %reduce-scatter.19.cloned.1.call-done = f32[1,256,2048]{2,1,0:T(8,128)} async-done(((f32[4,256,2048]{2,1,0:T(8,128)}), f32[1,256,2048]{2,1,0:T(8,128)}) %reduce-scatter.19.cloned.1.call-update) | async-done | bytes 2097168
  948.7 81.3 %reduce-scatter.17.cloned.1.call-done = f32[1,256,2048]{2,1,0:T(8,128)} async-done(((f32[4,256,2048]{2,1,0:T(8,128)}), f32[1,256,2048]{2,1,0:T(8,128)}) %reduce-scatter.17.cloned.1.call-update) | async-done | bytes 2097168
  1034.1 148.7 %reduce-scatter.15.cloned.1.call-done = f32[1,512,2048]{2,1,0:T(8,128)} async-done(((f32[4,512,2048]{2,1,0:T(8,128)}), f32[1,512,2048]{2,1,0:T(8,128)}) %reduce-scatter.15.cloned.1.call-update) | async-done | bytes 4194320
  1182.8 3.8 convert_bitcast_fusion
  1188.1 234.8 %weight_grads.1 = (bf16[4,2048,512]{2,1,0:T(8,128)(2,1)}, bf16[4,2048,512]{2,1,0:T(8,128)(2,1)}, bf16[4,512,2048]{2,1,0:T(8,128)(2,1)}) custom-call(bf16[8,2,512,2048]{3,2,1,0:T(8,128)(2,1)} %bitcast.46, bf16[8,512,2048]{2,1,0:T(8,128)(2,1)} %get-tuple-element.26.x_ref, bf16[8,512,2048]{2,1,0:T(8,128)(2,1)} %get-tuple-element.27.dy_ref, ...), custom_call_target="tpu_custom_call" | custom-call | flops 206158430208 | bytes 268435456 | tf_op jit(solution)/shard_map/weight_grads/pallas_call | solution.py:449
  1422.9 3.8 maximum_bitcast_fusion
  1426.7 43.9 %reduce-scatter.13.cloned.1.call-done = f32[1,1024,2048]{2,1,0:T(8,128)} async-done(((f32[4,1024,2048]{2,1,0:T(8,128)}), f32[1,1024,2048]{2,1,0:T(8,128)}) %reduce-scatter.13.cloned.1.call-update) | async-done | bytes 8388624
  1470.7 6.0 convert_element_type.22
  (47 shorter events, 30.9 us)
Async XLA Ops:
  7.2 100.7 %all-gather.9.cloned.1.call-start = ((), (), s32[]{:S(2)}) async-start(), calls=%async_computation.6 | async-start | bytes 9437184 | tf_op jit(solution)/shard_map/all_gather | solution.py:494
  8.5 26.5 %collective-permute-start.2 = (bf16[256,2048]{1,0:T(8,128)(2,1)S(1)}, bf16[256,2048]{1,0:T(8,128)(2,1)S(1)}, u32[]{:S(2)}, u32[]{:S(2)}) collective-permute-start(bf16[256,2048]{1,0:T(8,128)(2,1)S(1)} %slice_bitcast_fusion.1), channel_id=1, source_target_pairs={{0,8},{8,0},{1,9},{9,1},{2,10},{10,2},{3,11},{11,3},{4,12},{12,4},... | collective-permute-start | bytes 3145736 | tf_op jit(solution)/shard_map/ppermute | solution.py:513
  35.0 1.0 copy-start
  36.0 228.8 %all-gather.7.cloned.1.call-start = ((), (), s32[]{:S(2)}) async-start(), calls=%async_computation.5 | async-start | bytes 28311552 | tf_op jit(solution)/shard_map/all_gather | solution.py:494
  38.3 119.5 %slice-start = ((bf16[1,1024,2048]{2,1,0:T(8,128)(2,1)}), bf16[1,512,2048]{2,1,0:T(8,128)(2,1)S(1)}, s32[]{:S(2)}) async-start(bf16[1,1024,2048]{2,1,0:T(8,128)(2,1)} %param.13), calls=%async_computation.12 | async-start | bytes 4194304 | tf_op jit(solution)/shard_map/slice | solution.py:526
  38.3 69.4 %collective-permute-start = (bf16[768,2048]{1,0:T(8,128)(2,1)S(1)}, bf16[768,2048]{1,0:T(8,128)(2,1)}, u32[]{:S(2)}, u32[]{:S(2)}) collective-permute-start(bf16[768,2048]{1,0:T(8,128)(2,1)S(1)} %slice_bitcast_fusion), channel_id=1, source_target_pairs={{0,8},{8,0},{1,9},{9,1},{2,10},{10,2},{3,11},{11,3},{4,12},{12,4},... | collective-permute-start | bytes 9437192 | tf_op jit(solution)/shard_map/ppermute | solution.py:513
  107.8 345.1 %all-gather.11.cloned.1.call-start = ((), (), s32[]{:S(2)}) async-start(), calls=%async_computation.7 | async-start | bytes 37748736 | tf_op jit(solution)/shard_map/all_gather | solution.py:494
  111.9 49.1 %copy-start.1 = (f32[1,1024,8]{1,2,0:T(8,128)S(1)}, f32[1,1024,8]{1,2,0:T(8,128)}, u32[]{:S(2)}) copy-start(f32[1,1024,8]{1,2,0:T(8,128)} %param.9) | copy-start | bytes 98308
  111.9 49.1 %copy-start.2 = (s32[1,1024,8]{1,2,0:T(8,128)S(1)}, s32[1,1024,8]{1,2,0:T(8,128)}, u32[]{:S(2)}) copy-start(s32[1,1024,8]{1,2,0:T(8,128)} %param.8) | copy-start | bytes 98308
  111.9 45.9 %collective-permute-start.3 = (bf16[512,2048]{1,0:T(8,128)(2,1)S(1)}, bf16[512,2048]{1,0:T(8,128)(2,1)S(1)}, u32[]{:S(2)}, u32[]{:S(2)}) collective-permute-start(bf16[512,2048]{1,0:T(8,128)(2,1)S(1)} %get-tuple-element.38), channel_id=1, source_target_pairs={{0,8},{8,0},{1,9},{9,1},{2,10},{10,2},{3,11},{11,3},{4,12},{12,4},... | collective-permute-start | bytes 6291464 | tf_op jit(solution)/shard_map/ppermute | solution.py:525
  161.3 5.0 collective-permute-start.1
  167.1 20.6 %all-to-all-start = ((f32[8,4,1024]{2,1,0:T(4,128)}), f32[8,4,1024]{2,1,0:T(4,128)S(1)}, u32[]{:S(2)}, u32[]{:S(2)}) async-start(f32[8,4,1024]{2,1,0:T(4,128)} %copy.28), calls=%async_computation | async-start | bytes 262144 | tf_op jit(solution)/shard_map/all_to_all | solution.py:503
  170.4 774.0 %reduce-scatter.19.cloned.1.call-start = ((), (), s32[]{:S(2)}) async-start(), calls=%async_computation.11 | async-start | bytes 10485760
  196.3 65.3 %collective-permute-start.4 = (bf16[512,2048]{1,0:T(8,128)(2,1)}, bf16[512,2048]{1,0:T(8,128)(2,1)}, u32[]{:S(2)}, u32[]{:S(2)}) collective-permute-start(bf16[512,2048]{1,0:T(8,128)(2,1)} %get-tuple-element.37), channel_id=1, source_target_pairs={{0,8},{8,0},{1,9},{9,1},{2,10},{10,2},{3,11},{11,3},{4,12},{12,4},... | collective-permute-start | bytes 6291464 | tf_op jit(solution)/shard_map/ppermute | solution.py:527
  861.7 168.2 %reduce-scatter.17.cloned.1.call-start = ((), (), s32[]{:S(2)}) async-start(), calls=%async_computation.10 | async-start | bytes 10485760
  862.3 320.5 %reduce-scatter.15.cloned.1.call-start = ((), (), s32[]{:S(2)}) async-start(), calls=%async_computation.9 | async-start | bytes 20971520
  862.9 607.8 %reduce-scatter.13.cloned.1.call-start = ((), (), s32[]{:S(2)}) async-start(), calls=%async_computation.8 | async-start | bytes 41943040
  947.2 475.7 %collective-permute-start.7 = (bf16[256,2048]{1,0:T(8,128)(2,1)}, bf16[256,2048]{1,0:T(8,128)(2,1)}, u32[]{:S(2)}, u32[]{:S(2)}) collective-permute-start(bf16[256,2048]{1,0:T(8,128)(2,1)} %convert_bitcast_fusion.1), channel_id=1, source_target_pairs={{8,0},{0,8},{9,1},{1,9},{10,2},{2,10},{11,3},{3,11},{12,4},{4,12},... | collective-permute-start | bytes 3145736 | tf_op jit(solution)/shard_map/ppermute | solution.py:537
  1032.7 390.2 %collective-permute-start.6 = (bf16[256,2048]{1,0:T(8,128)(2,1)}, bf16[256,2048]{1,0:T(8,128)(2,1)}, u32[]{:S(2)}, u32[]{:S(2)}) collective-permute-start(bf16[256,2048]{1,0:T(8,128)(2,1)} %convert_bitcast_fusion.2), channel_id=1, source_target_pairs={{8,0},{0,8},{9,1},{1,9},{10,2},{2,10},{11,3},{3,11},{12,4},{4,12},... | collective-permute-start | bytes 3145736 | tf_op jit(solution)/shard_map/ppermute | solution.py:537
  1186.6 236.3 %collective-permute-start.5 = (bf16[512,2048]{1,0:T(8,128)(2,1)}, bf16[512,2048]{1,0:T(8,128)(2,1)}, u32[]{:S(2)}, u32[]{:S(2)}) collective-permute-start(bf16[512,2048]{1,0:T(8,128)(2,1)} %convert_bitcast_fusion), channel_id=1, source_target_pairs={{8,0},{0,8},{9,1},{1,9},{10,2},{2,10},{11,3},{3,11},{12,4},{4,12},... | collective-permute-start | bytes 6291464 | tf_op jit(solution)/shard_map/ppermute | solution.py:537
Sparse Core Ops, SparseCore 0:
  36.1 51.7 all-gather.8
  107.9 123.8 all-gather.6
  234.2 218.6 all-gather.10
  861.9 82.5 reduce-scatter.18
  947.3 82.5 reduce-scatter.16
  1032.8 149.9 reduce-scatter.14
  1185.8 284.8 reduce-scatter.12

commit v5 on v4

--- a/solution.py
+++ b/solution.py
@@ -10,9 +10,10 @@
 
 F32 = jnp.float32
 BF16 = jnp.bfloat16
-FWD_CHUNKS = ((256, 256), (768, 256))
-FWD_STAGES = (0, 7, 13, 19)
-BWD_STAGES = (0, 2, 4, 6)
+BWD_ROWS = (256, 384, 384)
+FWD_ROWS = (512, 512)
+FWD_TILE = 256
+STAGES = (0, 3, 5, 7)
 VMEM_LIMIT = 65400 * 1024
 N_ACC = 3
 CORES = 2
@@ -44,7 +45,7 @@
     return CORES * (tile // steps) + lane, lax.rem(tile, steps)
 
 
-def pair_sum(compute, half, steps, tile, inbox_ref, pieces, exchange, acc_ref, send_sem, recv_sem, in_sem, out_sem):
+def pair_sum(compute, half, steps, tile, inbox_ref, out, exchange, acc_ref, send_sem, recv_sem, in_sem, out_sem):
     step = pl.program_id(0)
     last = 2 * half - 1
     me = lax.axis_index('expert')
@@ -53,23 +54,11 @@
     def at(ref, job):
         return ref.at[job // steps, pl.ds(lax.rem(job, steps) * tile, tile)]
 
-    class Store:
-        def __init__(self, job):
-            slot = lax.rem(job + half, N_ACC)
-            self.copies = [
-                pltpu.make_async_copy(
-                    acc_ref.at[slot, pl.ds(row, rows)],
-                    out_ref.at[job // steps, pl.ds(first + lax.rem(job, steps) * tile, rows)],
-                    out_sem.at[slot, k])
-                for k, (out_ref, first, row, rows) in enumerate(pieces)]
-
-        def start(self):
-            for copy in self.copies:
-                copy.start()
-
-        def wait(self):
-            for copy in self.copies:
-                copy.wait()
+    def store(job):
+        slot = lax.rem(job + half, N_ACC)
+        out_ref, first = out
+        rows = pl.ds(first + lax.rem(job, steps) * tile, tile)
+        return pltpu.make_async_copy(acc_ref.at[slot], out_ref.at[job // steps, rows], out_sem.at[slot])
 
     def send(job):
         slot = lax.rem(job, N_ACC)
@@ -100,7 +89,7 @@
 
     @pl.when(back >= half)
     def _():
-        Store(back - half).wait()
+        store(back - half).wait()
 
     ahead = step + 1 - half
 
@@ -127,12 +116,12 @@
 
     @pl.when(step >= half)
     def _():
-        Store(step - half).start()
+        store(step - half).start()
 
     @pl.when(step == last)
     def _():
         for job in range(half - N_ACC + 1, half):
-            Store(job).wait()
+            store(job).wait()
         if exchange:
             exchange.finish()
 
@@ -228,13 +217,7 @@
     return [pltpu.VMEM(w13.shape, BF16), pltpu.VMEM(w2.shape, BF16), pltpu.SemaphoreType.DMA((w13.shape[0], 2))]
 
 
-def fwd_body(ffn, n_local, half, steps, start, stages, n_carried, x_ref, g_ref, w13_hbm, w2_hbm, *refs):
-    y_ref, inbox_ref = refs[n_carried:n_carried + 2]
-    rest = list(refs[n_carried + 2:])
-    buf_ref = rest.pop(0) if stages else None
-    w13_ref, w2_ref, w_sem = rest[:3]
-    scratch = rest[3:8]
-    exchange = Exchange(buf_ref, *rest[8:], stages) if stages else None
+def fwd_body(ffn, n_local, half, steps, x_ref, g_ref, w13_hbm, w2_hbm, y_ref, inbox_ref, w13_ref, w2_ref, w_sem, *scratch):
     tile = x_ref.shape[1]
     weights = Weights(n_local, (w13_hbm, w2_hbm), (w13_ref, w2_ref), w_sem)
     step = pl.program_id(0)
@@ -265,16 +248,16 @@
     def _():
         weights.start()
 
-    pair_sum(compute, half, steps, tile, inbox_ref, [(y_ref, start, 0, tile)], exchange, *scratch)
-
-
-def pair_scratch(tile, model, half, n_pieces):
+    pair_sum(compute, half, steps, tile, inbox_ref, (y_ref, 0), None, *scratch)
+
+
+def pair_scratch(tile, model, half):
     return [
         pltpu.VMEM((N_ACC, tile, model), F32),
         pltpu.SemaphoreType.DMA((N_ACC,)),
         pltpu.SemaphoreType.DMA((half,)),
         pltpu.SemaphoreType.DMA((N_ACC,)),
-        pltpu.SemaphoreType.DMA((N_ACC, n_pieces)),
+        pltpu.SemaphoreType.DMA((N_ACC,)),
     ]
 
 
@@ -286,50 +269,40 @@
 HBM = pl.BlockSpec(memory_space=pl.ANY)
 
 
-def expert_fwd(x, gates, w13, w2, tile, start, n_tok, carried, hosted, stages, collective_id):
+def expert_fwd(x, gates, w13, w2, collective_id):
     n_src, rows, model = x.shape
     n_local, ffn = w2.shape[:2]
+    tile = FWD_TILE
     steps = rows // tile
     n_own = n_src // CORES
     half = n_own * steps
     flops = 2 * n_src * rows * n_local * model * ffn * 3
-    extra = list(carried) + list(hosted)
 
     def at(i):
         src, t = pair_source(i, half, steps)
         return src, t, 0
 
-    aliases = {4 + i: i for i in range(len(carried))}
-    aliases.update({4 + len(carried) + i: 2 + i for i in range(len(hosted))})
-    outs = pl.pallas_call(
-        functools.partial(fwd_body, ffn, n_local, half, steps, start, stages, len(extra)),
+    part = jax.ShapeDtypeStruct((n_own, rows, model), F32)
+    return pl.pallas_call(
+        functools.partial(fwd_body, ffn, n_local, half, steps),
         grid=(2 * half,),
-        in_specs=[
-            pl.BlockSpec((1, tile, model), at),
-            pl.BlockSpec((1, tile, n_local), at),
-            HBM,
-            HBM,
-        ] + [HBM] * len(extra),
-        out_specs=[HBM] * (2 + len(hosted)),
-        out_shape=[jax.ShapeDtypeStruct((n_own, n_tok, model), F32), jax.ShapeDtypeStruct((n_own, rows, model), F32)]
-        + [jax.ShapeDtypeStruct(h.shape, h.dtype) for h in hosted],
-        scratch_shapes=weight_scratch(w13, w2) + pair_scratch(tile, model, half, 1) + EXCHANGE_SEMS * len(hosted),
-        input_output_aliases=aliases,
+        in_specs=[pl.BlockSpec((1, tile, model), at), pl.BlockSpec((1, tile, n_local), at), HBM, HBM],
+        out_specs=[HBM, HBM],
+        out_shape=[part, part],
+        scratch_shapes=weight_scratch(w13, w2) + pair_scratch(tile, model, half),
         compiler_params=pair_params(collective_id),
         cost_estimate=pl.CostEstimate(flops=flops, bytes_accessed=n_src * rows * model * 6, transcendentals=0),
         name='expert_fwd',
-    )(x, gates, w13, w2, *extra)
-    return outs[0], outs[2:]
-
-
-def bwd_body(ffn, n_local, half, steps, pieces, stages, n_carried, x_ref, dy_ref, g_ref, w13_hbm, w2_hbm, *refs):
-    refs = list(refs[n_carried:])
-    n_out = len(pieces)
-    outs, (da_ref, h_ref, inbox_ref), rest = refs[:n_out], refs[n_out:n_out + 3], refs[n_out + 3:]
-    buf_ref = rest.pop(0) if stages else None
+    )(x, gates, w13, w2)[0]
+
+
+def bwd_body(ffn, n_local, half, first, n_carried, n_hosted, x_ref, dy_ref, g_ref, w13_hbm, w2_hbm, *refs):
+    refs = list(refs[n_carried + n_hosted:])
+    (dx_ref, da_ref, h_ref, inbox_ref), rest = refs[:4], refs[4:]
+    buf_ref = rest.pop(0) if n_hosted else None
     w13_ref, w2_ref, w_sem = rest[:3]
     scratch = rest[3:8]
-    exchange = Exchange(buf_ref, *rest[8:], stages) if stages else None
+    exchange = Exchange(buf_ref, *rest[8:], STAGES) if n_hosted else None
     tile = g_ref.shape[1]
     weights = Weights(n_local, (w13_hbm, w2_hbm), (w13_ref, w2_ref), w_sem)
     step = pl.program_id(0)
@@ -362,63 +335,62 @@
     def _():
         weights.start()
 
-    places = [(ref, 0, row, rows) for ref, (row, rows) in zip(outs, pieces)]
-    pair_sum(compute, half, steps, tile, inbox_ref, places, exchange, *scratch)
-
-
-def expert_bwd(x, dy, which, gates, w13, w2, start, pieces, carried, hosted, stages, collective_id):
+    pair_sum(compute, half, 1, tile, inbox_ref, (dx_ref, first), exchange, *scratch)
+
+
+def expert_bwd(x, dy, which, gates, w13, w2, dx_rows, first, carried, hosted, collective_id):
     n_src, model = x.shape[0], x.shape[-1]
-    n_tok = gates.shape[1]
     n_local, ffn = w2.shape[:2]
     tile = x.shape[-2]
-    steps = 1
     half = n_src // CORES
     flops = 2 * n_src * tile * n_local * model * ffn * 5
-    extra = list(carried) + list(hosted)
-    n_out = len(pieces)
+
+    def at(i):
+        src, _ = pair_source(i, half, 1)
+        return src, 0, 0
 
     def rows_of(array, k):
-        def index(i):
-            src, t = pair_source(i, half, steps)
-            return (src, t, 0) if array.ndim == 3 else (src, k, t, 0)
-
-        return pl.BlockSpec((1,) * (array.ndim - 2) + (tile, model), index)
-
-    def at(i):
-        src, t = pair_source(i, half, steps)
-        return src, start // tile + t, 0
-
-    aliases = {5 + i: n_out + i for i in range(len(carried))}
-    aliases.update({5 + len(carried) + i: n_out + 3 + i for i in range(len(hosted))})
+        def stacked(i):
+            src, _ = pair_source(i, half, 1)
+            return src, k, 0, 0
+
+        return pl.BlockSpec((1,) * (array.ndim - 2) + (tile, model), at if array.ndim == 3 else stacked)
+
+    aliases = {5 + i: 0 for i in range(len(carried))}
+    aliases.update({5 + len(carried) + i: 4 + i for i in range(len(hosted))})
     outs = pl.pallas_call(
-        functools.partial(bwd_body, ffn, n_local, half, steps, pieces, stages, len(extra)),
+        functools.partial(bwd_body, ffn, n_local, half, first, len(carried), len(hosted)),
         grid=(2 * half,),
-        in_specs=[
-            rows_of(x, which[0]),
-            rows_of(dy, which[1]),
-            pl.BlockSpec((1, tile, n_local), at),
+        in_specs=[rows_of(x, which[0]), rows_of(dy, which[1]), pl.BlockSpec((1, tile, n_local), at)]
+        + [HBM] * (2 + len(carried) + len(hosted)),
+        out_specs=[
             HBM,
-            HBM,
-        ] + [HBM] * len(extra),
-        out_specs=[HBM] * n_out + [
             pl.BlockSpec((1, tile, 2 * ffn * n_local), at),
             pl.BlockSpec((1, tile, ffn * n_local), at),
         ] + [HBM] * (1 + len(hosted)),
-        out_shape=[jax.ShapeDtypeStruct((half, rows, model), F32) for _, rows in pieces] + [
-            jax.ShapeDtypeStruct((n_src, n_tok, 2 * ffn * n_local), BF16),
-            jax.ShapeDtypeStruct((n_src, n_tok, ffn * n_local), BF16),
+        out_shape=[
+            jax.ShapeDtypeStruct((half, dx_rows, model), F32),
+            jax.ShapeDtypeStruct((n_src, tile, 2 * ffn * n_local), BF16),
+            jax.ShapeDtypeStruct((n_src, tile, ffn * n_local), BF16),
             jax.ShapeDtypeStruct((half, tile, model), F32),
         ] + [jax.ShapeDtypeStruct(h.shape, h.dtype) for h in hosted],
-        scratch_shapes=weight_scratch(w13, w2) + pair_scratch(tile, model, half, n_out) + EXCHANGE_SEMS * len(hosted),
+        scratch_shapes=weight_scratch(w13, w2) + pair_scratch(tile, model, half) + EXCHANGE_SEMS * len(hosted),
         input_output_aliases=aliases,
         compiler_params=pair_params(collective_id),
         cost_estimate=pl.CostEstimate(flops=flops, bytes_accessed=n_src * tile * model * 14, transcendentals=0),
         name='expert_bwd',
-    )(x, dy, gates, w13, w2, *extra)
-    return outs[:n_out], outs[n_out:n_out + 2], outs[n_out + 3:]
-
-
-def grad_body(ffn, lo_ref, x_ref, dy_ref, g_ref, da_ref, h_ref, dw1_ref, dw3_ref, dw2_ref, acc13_ref, acc2_ref):
+    )(x, dy, gates, w13, w2, *carried, *hosted)
+    return outs[0], outs[1], outs[2], outs[4:]
+
+
+def rows_joined(refs):
+    parts = [ref[...].reshape(ref.shape[-2:]) for ref in refs]
+    return parts[0] if len(parts) == 1 else jnp.concatenate(parts, axis=0)
+
+
+def grad_body(ffn, n_parts, g_ref, *refs):
+    x_refs, dy_refs, da_refs, h_refs = (refs[k * n_parts:(k + 1) * n_parts] for k in range(4))
+    dw1_ref, dw3_ref, dw2_ref, acc13_ref, acc2_ref = refs[4 * n_parts:]
     e, k = pl.program_id(0), pl.program_id(1)
 
     @pl.when(k == 0)
@@ -426,10 +398,9 @@
         acc13_ref[...] = jnp.zeros_like(acc13_ref)
         acc2_ref[...] = jnp.zeros_like(acc2_ref)
 
-    acc13_ref[...] += dot_a(jnp.concatenate([lo_ref[0, 1], x_ref[0]], axis=0), da_ref[0])
-    d_out = jnp.concatenate([lo_ref[0, 0], dy_ref[0]], axis=0).astype(F32)
-    d_out = (gate_column(g_ref[0], e) * d_out).astype(BF16)
-    acc2_ref[...] += dot_a(h_ref[0], d_out)
+    acc13_ref[...] += dot_a(rows_joined(x_refs), rows_joined(da_refs))
+    d_out = (gate_column(g_ref[0], e) * rows_joined(dy_refs).astype(F32)).astype(BF16)
+    acc2_ref[...] += dot_a(rows_joined(h_refs), d_out)
 
     @pl.when(k == pl.num_programs(1) - 1)
     def _():
@@ -438,25 +409,27 @@
         dw2_ref[0] = acc2_ref[...].astype(BF16)
 
 
-def weight_grads(lo, x_hi, dy_hi, gates, d_pre, hidden):
+def weight_grads(gates, xs, dys, d_pres, hiddens):
     n_src, n_tok, n_local = gates.shape
-    model = lo.shape[3]
-    ffn = hidden.shape[2] // n_local
+    model = xs[0][0].shape[-1]
+    ffn = hiddens[0].shape[2] // n_local
     flops = 2 * n_src * n_tok * n_local * model * ffn * 3
     at = lambda e, k: (k, 0, 0)
     at_e = lambda e, k: (k, 0, e)
     out = lambda e, k: (e, 0, 0)
+
+    def rows_of(array, which):
+        block = (1,) * (array.ndim - 2) + array.shape[-2:]
+        return pl.BlockSpec(block, at if array.ndim == 3 else (lambda e, k: (k, which, 0, 0)))
+
     return pl.pallas_call(
-        functools.partial(grad_body, ffn),
+        functools.partial(grad_body, ffn, len(xs)),
         grid=(n_local, n_src),
-        in_specs=[
-            pl.BlockSpec((1,) + lo.shape[1:], lambda e, k: (k, 0, 0, 0)),
-            pl.BlockSpec((1,) + x_hi.shape[1:], at),
-            pl.BlockSpec((1,) + dy_hi.shape[1:], at),
-            pl.BlockSpec((1, n_tok, n_local), at),
-            pl.BlockSpec((1, n_tok, 2 * ffn), at_e),
-            pl.BlockSpec((1, n_tok, ffn), at_e),
-        ],
+        in_specs=[pl.BlockSpec((1, n_tok, n_local), at)]
+        + [rows_of(*x) for x in xs]
+        + [rows_of(*dy) for dy in dys]
+        + [pl.BlockSpec((1, d.shape[1], 2 * ffn), at_e) for d in d_pres]
+        + [pl.BlockSpec((1, h.shape[1], ffn), at_e) for h in hiddens],
         out_specs=[
             pl.BlockSpec((1, model, ffn), out),
             pl.BlockSpec((1, model, ffn), out),
@@ -471,7 +444,7 @@
         compiler_params=pltpu.CompilerParams(dimension_semantics=('arbitrary', 'arbitrary'), vmem_limit_bytes=VMEM_LIMIT),
         cost_estimate=pl.CostEstimate(flops=flops, bytes_accessed=n_src * n_tok * model * 4 * n_local, transcendentals=0),
         name='weight_grads',
-    )(lo, x_hi, dy_hi, gates, d_pre, hidden)
+    )(gates, *[x for x, _ in xs], *[dy for dy, _ in dys], *d_pres, *hiddens)
 
 
 def solution(mesh):
@@ -482,7 +455,6 @@
     tok_spec = P('stage', 'expert', None)
     w_spec = P('stage', 'expert', None, None)
     same_core = [list(range(core, n_dev, CORES)) for core in range(CORES)]
-    n_fwd = len(FWD_CHUNKS)
 
     def moe_body(x_act, route_idx, route_wts, w_one, w_three, w_two, dy_act):
         x_src = x_act[0]
@@ -505,39 +477,51 @@
         w13 = jnp.concatenate([w_one[0], w_three[0]], axis=2)
         w2 = w_two[0]
 
-        half = n_tok // 2
-        dy_hi = place(dy_act[0], half, half, n_dev)
-        carried = ()
-        start = 0
-        for k, (rows, tile) in enumerate(FWD_CHUNKS):
-            x_dst = lax.ppermute(x_src[start:start + rows], 'stage', to_next)
-            x_all = gather(x_dst)
-            if k == 0:
-                x_first = x_all
-            hosted, stages = ((dy_hi,), FWD_STAGES) if k == n_fwd - 1 else ((), ())
-            y_part, arrived = expert_fwd(x_all, gates[:, start:start + rows], w13, w2, tile, start, n_tok, carried, hosted, stages, k)
-            carried = (y_part,)
-            start += rows
-        dy_hi, = arrived
-        y_out = reduce_rows(y_part)
-
-        x_again, _ = lax.optimization_barrier((x_src, x_first))
-        x_dst = lax.ppermute(x_again[:half], 'stage', to_next)
-        lo = gather(jnp.stack([dy_act[0, :half], x_dst]))
-        x_dst = lax.ppermute(x_again[half:], 'stage', to_next)
-        x_hi = place(x_dst, 0, half, n_dev)
-
-        lo_now, _ = lax.optimization_barrier((lo, y_part))
-        dx_lo, carried, (x_hi,) = expert_bwd(lo_now, lo_now, (1, 0), gates, w13, w2, 0, ((0, half),), (), (x_hi,), BWD_STAGES, n_fwd)
-        cut = half // 2
-        dx_hi, carried, _ = expert_bwd(x_hi, dy_hi, (0, 0), gates, w13, w2, half, ((0, cut), (cut, cut)), carried, (), (), n_fwd + 1)
+        def spans(sizes):
+            ends = [sum(sizes[:k + 1]) for k in range(len(sizes))]
+            return [slice(end - size, end) for end, size in zip(ends, sizes)]
+
+        bwd, fwd = spans(BWD_ROWS), spans(FWD_ROWS)
+        dx_rows = sum(BWD_ROWS[:2]), BWD_ROWS[2]
+
+        def hop(rows):
+            return lax.ppermute(x_src[rows], 'stage', to_next)
+
+        dys = [(gather(dy_act[0, bwd[0]]), 0)]
+        xs = [(gather(hop(bwd[0])), 0)]
+        for k in (1, 2):
+            x_dst = hop(bwd[k])
+            both = gather(jnp.stack([dy_act[0, bwd[k]], x_dst]))
+            dys.append((both, 0))
+            xs.append((both, 1))
+
+        d_pres, hiddens, x_fwd = [], [], []
         dx_parts = []
-        for part in list(dx_lo) + list(dx_hi):
-            dx_dst = reduce_rows(part)
-            dx_parts.append(lax.ppermute(dx_dst, 'stage', to_prev))
+        for k in range(3):
+            carried, hosted = (), ()
+            if k == 1:
+                carried = (dx_part,)
+            if k > 0:
+                x_dst = hop(fwd[k - 1])
+                hosted = (place(x_dst, 0, FWD_ROWS[k - 1], n_dev),)
+            dx_part, d_pre, hidden, arrived = expert_bwd(
+                xs[k][0], dys[k][0], (xs[k][1], dys[k][1]), gates[:, bwd[k]], w13, w2,
+                dx_rows[k // 2], BWD_ROWS[0] if k == 1 else 0, carried, hosted, k)
+            x_fwd += arrived
+            d_pres.append(d_pre)
+            hiddens.append(hidden)
+            if k > 0:
+                dx_dst = reduce_rows(dx_part)
+                dx_parts.append(lax.ppermute(dx_dst, 'stage', to_prev))
         dx_out = jnp.concatenate(dx_parts, axis=0)
 
-        g_one, g_three, g_two = weight_grads(lo, x_hi, dy_hi, gates, *carried)
+        y_parts = []
+        for k in range(2):
+            y_part = expert_fwd(x_fwd[k], gates[:, fwd[k]], w13, w2, 3 + k)
+            y_parts.append(reduce_rows(y_part))
+        y_out = jnp.concatenate(y_parts, axis=0)
+
+        g_one, g_three, g_two = weight_grads(gates, xs, dys, d_pres, hiddens)
         return y_out[None], dx_out[None], g_one[None], g_three[None], g_two[None]
 
     return jax.shard_map(moe_body, mesh=mesh, in_specs=(tok_spec, tok_spec, tok_spec, w_spec, w_spec, w_spec, tok_spec), out_specs=(tok_spec, tok_spec, w_spec, w_spec, w_spec), check_vma=False)

time: 1490 us -> 1200 us (0.81)
  waiting for transfers between devices: 498 us -> 181 us
  Pallas kernels: 899 us -> 918 us
    unnamed x11 -> x12, waiting for transfers between devices: 357 us -> 0.2 us
    ppermute x1, waiting for transfers between devices: 3.79 us -> 45.9 us  [moe_body(): gate_dst = lax.ppermute(gate_src, 'stage', to_next)]
    pallas_call x5 -> x6, Pallas kernels: 893 us -> 912 us  [the longest x3 431 us: expert_bwd(): pl.pallas_call(functools.partial(bwd_body, ffn, n_local, half, first, len...]
    ppermute x4 -> x5, waiting for transfers between devices: 135 us -> 135 us  [hop(): return lax.ppermute(x_src[rows], 'stage', to_next)]
  transfers between devices with their start and end apart: 16 -> 17, of which waited for: 9 -> 5; matrix products, arithmetic and copies ran while one was open for 3% -> 5% of each run, Pallas kernels for 33% -> 77%
where the time goes in v5:
time: 1200 us
  Pallas kernels  918 us (76%)
  waiting for transfers between devices  181 us (15%)
  other arithmetic  38.4 us (3%)
  local copies, waits for them, and re-layouts  28.1 us (2%)
  starting transfers between devices  16.7 us (1%)
  between operations  14.5 us (1%)
    pallas_call x3, Pallas kernels, expert_bwd(): pl.pallas_call(functools.partial(bwd_body, ffn, n_local, half, first, len...  431 us
    pallas_call x2, Pallas kernels, expert_fwd(): pl.pallas_call(functools.partial(fwd_body, ffn, n_local, half, steps), gr...  245 us
    pallas_call x1, Pallas kernels, weight_grads(): pl.pallas_call(functools.partial(grad_body, ffn, len(xs)), grid=(n_local,...  236 us
    ppermute x5, waiting for transfers between devices, hop(): return lax.ppermute(x_src[rows], 'stage', to_next)  135 us
    ppermute x1, waiting for transfers between devices, moe_body(): gate_dst = lax.ppermute(gate_src, 'stage', to_next)  45.9 us
  transfers between devices with their start and end apart: 17, of which 5 were waited for; matrix products, arithmetic and copies ran while one was open for 5% of the time, Pallas kernels for 77%

profile of v5, /device:TPU:0, one launch (start us, length us, event | category | flops | bytes accessed | tf_op | source)
XLA Modules:
  0.0 1196.4 jit_solution(711909942472374752)
XLA Ops:
  9.6 3.3 collective-permute-start.4
  13.2 34.1 %collective-permute-done.4 = bf16[384,2048]{1,0:T(8,128)(2,1)S(1)} collective-permute-done((bf16[384,2048]{1,0:T(8,128)(2,1)S(1)}, bf16[384,2048]{1,0:T(8,128)(2,1)S(1)}, u32[]{:S(2)}, u32[]{:S(2)}) %collective-permute-start.4) | collective-permute-done | bytes 1572896 | tf_op jit(solution)/shard_map/ppermute | solution.py:488
  54.8 22.7 %collective-permute-done.2 = bf16[256,2048]{1,0:T(8,128)(2,1)} collective-permute-done((bf16[256,2048]{1,0:T(8,128)(2,1)S(1)}, bf16[256,2048]{1,0:T(8,128)(2,1)}, u32[]{:S(2)}, u32[]{:S(2)}) %collective-permute-start.2) | collective-permute-done | bytes 1048608 | tf_op jit(solution)/shard_map/ppermute | solution.py:488
  79.0 33.2 %collective-permute-done = bf16[384,2048]{1,0:T(8,128)(2,1)S(1)} collective-permute-done((bf16[384,2048]{1,0:T(8,128)(2,1)S(1)}, bf16[384,2048]{1,0:T(8,128)(2,1)S(1)}, u32[]{:S(2)}, u32[]{:S(2)}) %collective-permute-start) | collective-permute-done | bytes 1572896 | tf_op jit(solution)/shard_map/ppermute | solution.py:488
  114.2 4.8 slice_bitcast_fusion.1
  121.4 45.9 %collective-permute-done.1 = f32[8,4,1024]{2,0,1:T(8,128)S(1)} collective-permute-done((f32[8,4,1024]{2,0,1:T(8,128)S(1)}, f32[8,4,1024]{2,0,1:T(8,128)S(1)}, u32[]{:S(2)}, u32[]{:S(2)}) %collective-permute-start.1) | collective-permute-done | bytes 131104 | tf_op jit(solution)/shard_map/ppermute | solution.py:474
  168.0 3.4 all-to-all-start
  171.5 14.2 %pad_maximum_fusion.w13_hbm = bf16[4,2048,1024]{2,1,0:T(8,128)(2,1)} fusion(bf16[4,2048,512]{2,1,0:T(8,128)(2,1)} %bitcast.44, bf16[4,2048,512]{2,1,0:T(8,128)(2,1)} %bitcast.45), kind=kLoop, calls=%fused_computation | loop fusion | flops 33554432 | bytes 33554432 | tf_op jit(solution)/shard_map/concatenate | solution.py:477
  185.7 2.7 copy.27
  188.3 3.9 fusion.1
  193.5 3.0 place.3.refs_0_
  196.6 160.6 %expert_bwd.5 = (f32[4,384,2048]{2,1,0:T(8,128)}, bf16[8,384,4096]{2,1,0:T(8,128)(2,1)}, bf16[8,384,2048]{2,1,0:T(8,128)(2,1)}, f32[4,384,2048]{2,1,0:T(8,128)}, bf16[8,512,2048]{2,1,0:T(8,128)(2,1)}) custom-call(bf16[8,2,384,2048]{3,2,1,0:T(8,128)(2,1)} %bitcast.51, bf16[8,2,384,2048]{3,2,1,0:T(8,128)(2,1)} %bitcast.52, ...), custom_call_target="tpu_custom_call", output_to_operand_aliasing={{4}: (5, {})} | custom-call | flops 128849018880 | bytes 88080384 | tf_op jit(solution)/shard_map/expert_bwd/pallas_call | solution.py:361
  361.0 44.6 %collective-permute-done.3.x_ref = bf16[512,2048]{1,0:T(8,128)(2,1)S(1)} collective-permute-done((bf16[512,2048]{1,0:T(8,128)(2,1)}, bf16[512,2048]{1,0:T(8,128)(2,1)S(1)}, u32[]{:S(2)}, u32[]{:S(2)}) %collective-permute-start.3) | collective-permute-done | bytes 2097184 | tf_op jit(solution)/shard_map/ppermute | solution.py:488
  406.9 3.0 place.2.refs_1_
  410.0 110.7 %expert_bwd.3 = (f32[4,640,2048]{2,1,0:T(8,128)}, bf16[8,256,4096]{2,1,0:T(8,128)(2,1)}, bf16[8,256,2048]{2,1,0:T(8,128)(2,1)}, f32[4,256,2048]{2,1,0:T(8,128)}) custom-call(bf16[8,256,2048]{2,1,0:T(8,128)(2,1)} %bitcast.64, bf16[8,256,2048]{2,1,0:T(8,128)(2,1)} %all-gather.8.cloned.1.call-done.dy_ref.refs_3_, f32[8,256,4]{2,1,0:T(8,128)} %slice.73.g_ref, ...), custom_call_target="tpu_custom_call" | custom-call | flops 85899345920 | bytes 58720256 | tf_op jit(solution)/shard_map/expert_bwd/pallas_call | solution.py:361
  520.7 159.7 %expert_bwd.4 = (f32[4,640,2048]{2,1,0:T(8,128)}, bf16[8,384,4096]{2,1,0:T(8,128)(2,1)}, bf16[8,384,2048]{2,1,0:T(8,128)(2,1)}, f32[4,384,2048]{2,1,0:T(8,128)}, bf16[8,512,2048]{2,1,0:T(8,128)(2,1)}) custom-call(bf16[8,2,384,2048]{3,2,1,0:T(8,128)(2,1)} %bitcast.55, ...), custom_call_target="tpu_custom_call", output_to_operand_aliasing={{0}: (5, {}), {4}: (6, {})} | custom-call | flops 128849018880 | bytes 88080384 | tf_op jit(solution)/shard_map/expert_bwd/pallas_call | solution.py:361
  681.0 4.6 fusion
  685.6 122.6 %expert_fwd.2 = (f32[4,512,2048]{2,1,0:T(8,128)}, f32[4,512,2048]{2,1,0:T(8,128)}) custom-call(bf16[8,512,2048]{2,1,0:T(8,128)(2,1)} %get-tuple-element.22.x_ref, f32[8,512,4]{2,1,0:T(8,128)} %get-tuple-element.37.g_ref, bf16[4,2048,1024]{2,1,0:T(8,128)(2,1)} %pad_maximum_fusion.w13_hbm, bf16[4,512,2048]{2,1,0:T(8,128)(2,1)} %bitcast.62), custom_call_target="tpu_custom_call" | custom-call | flops 103079215104 | bytes 50331648 | tf_op jit(solution)/shard_map/expert_fwd/pallas_call | solution.py:286
  808.5 122.6 %expert_fwd.3 = (f32[4,512,2048]{2,1,0:T(8,128)}, f32[4,512,2048]{2,1,0:T(8,128)}) custom-call(bf16[8,512,2048]{2,1,0:T(8,128)(2,1)} %get-tuple-element.24.x_ref, f32[8,512,4]{2,1,0:T(8,128)} %get-tuple-element.38.g_ref, bf16[4,2048,1024]{2,1,0:T(8,128)(2,1)} %pad_maximum_fusion.w13_hbm, bf16[4,512,2048]{2,1,0:T(8,128)(2,1)} %bitcast.63), custom_call_target="tpu_custom_call" | custom-call | flops 103079215104 | bytes 50331648 | tf_op jit(solution)/shard_map/expert_fwd/pallas_call | solution.py:286
  931.2 3.3 convert_bitcast_fusion.3
  935.7 4.6 convert_bitcast_fusion
  941.1 235.8 %weight_grads.1 = (bf16[4,2048,512]{2,1,0:T(8,128)(2,1)}, bf16[4,2048,512]{2,1,0:T(8,128)(2,1)}, bf16[4,512,2048]{2,1,0:T(8,128)(2,1)}) custom-call(f32[8,1024,4]{2,1,0:T(8,128)} %bitcast.43, bf16[8,256,2048]{2,1,0:T(8,128)(2,1)} %bitcast.65, bf16[8,2,384,2048]{3,2,1,0:T(8,128)(2,1)} %bitcast.57, bf16[8,2,384,2048]{3,2,1,0:T(8,128)(2,1)} %bitcast.53, ...), custom_call_target="tpu_custom_call" | custom-call | flops 206158430208 | bytes 268435456 | tf_op jit(solution)/shard_map/weight_grads/pallas_call | solution.py:425
  1182.0 2.6 maximum_bitcast_fusion
  1184.5 4.8 maximum_bitcast_fusion.1
  (58 shorter events, 31.2 us)
Async XLA Ops:
  7.2 189.4 %all-gather.14.cloned.1.call-start = ((), (), s32[]{:S(2)}) async-start(), calls=%async_computation.8 | async-start | bytes 28311552 | tf_op jit(solution)/shard_map/all_gather | solution.py:466
  7.2 5.7 copy-start
  9.6 37.7 %collective-permute-start.4 = (bf16[384,2048]{1,0:T(8,128)(2,1)S(1)}, bf16[384,2048]{1,0:T(8,128)(2,1)S(1)}, u32[]{:S(2)}, u32[]{:S(2)}) collective-permute-start(bf16[384,2048]{1,0:T(8,128)(2,1)S(1)} %get-tuple-element.46), channel_id=1, source_target_pairs={{0,8},{8,0},{1,9},{9,1},{2,10},{10,2},{3,11},{11,3},{4,12},{12,4},... | collective-permute-start | bytes 4718600 | tf_op jit(solution)/shard_map/ppermute | solution.py:488
  49.2 360.7 %all-gather.8.cloned.1.call-start = ((), (), s32[]{:S(2)}) async-start(), calls=%async_computation.5 | async-start | bytes 9437184 | tf_op jit(solution)/shard_map/all_gather | solution.py:466
  51.6 358.3 %all-gather.12.cloned.1.call-start = ((), (), s32[]{:S(2)}) async-start(), calls=%async_computation.7 | async-start | bytes 9437184 | tf_op jit(solution)/shard_map/all_gather | solution.py:466
  53.0 24.5 %collective-permute-start.2 = (bf16[256,2048]{1,0:T(8,128)(2,1)S(1)}, bf16[256,2048]{1,0:T(8,128)(2,1)}, u32[]{:S(2)}, u32[]{:S(2)}) collective-permute-start(bf16[256,2048]{1,0:T(8,128)(2,1)S(1)} %slice_bitcast_fusion.4), channel_id=1, source_target_pairs={{0,8},{8,0},{1,9},{9,1},{2,10},{10,2},{3,11},{11,3},{4,12},{12,4},... | collective-permute-start | bytes 3145736 | tf_op jit(solution)/shard_map/ppermute | solution.py:488
  77.5 443.2 %all-gather.10.cloned.1.call-start = ((), (), s32[]{:S(2)}) async-start(), calls=%async_computation.6 | async-start | bytes 28311552 | tf_op jit(solution)/shard_map/all_gather | solution.py:466
  77.5 34.7 %collective-permute-start = (bf16[384,2048]{1,0:T(8,128)(2,1)S(1)}, bf16[384,2048]{1,0:T(8,128)(2,1)S(1)}, u32[]{:S(2)}, u32[]{:S(2)}) collective-permute-start(bf16[384,2048]{1,0:T(8,128)(2,1)S(1)} %get-tuple-element.45), channel_id=1, source_target_pairs={{0,8},{8,0},{1,9},{9,1},{2,10},{10,2},{3,11},{11,3},{4,12},{12,4},... | collective-permute-start | bytes 4718600 | tf_op jit(solution)/shard_map/ppermute | solution.py:488
  114.2 6.0 copy-start.3
  114.2 6.0 copy-start.4
  119.1 73.1 %collective-permute-start.5 = (bf16[512,2048]{1,0:T(8,128)(2,1)}, bf16[512,2048]{1,0:T(8,128)(2,1)S(1)}, u32[]{:S(2)}, u32[]{:S(2)}) collective-permute-start(bf16[512,2048]{1,0:T(8,128)(2,1)} %get-tuple-element.40), channel_id=1, source_target_pairs={{0,8},{8,0},{1,9},{9,1},{2,10},{10,2},{3,11},{11,3},{4,12},{12,4},... | collective-permute-start | bytes 6291464 | tf_op jit(solution)/shard_map/ppermute | solution.py:488
  120.5 46.8 %collective-permute-start.1 = (f32[8,4,1024]{2,0,1:T(8,128)S(1)}, f32[8,4,1024]{2,0,1:T(8,128)S(1)}, u32[]{:S(2)}, u32[]{:S(2)}) collective-permute-start(f32[8,4,1024]{2,0,1:T(8,128)S(1)} %copy.25), channel_id=1, source_target_pairs={{0,8},{8,0},{1,9},{9,1},{2,10},{10,2},{3,11},{11,3},{4,12},{12,4},... | collective-permute-start | bytes 393224 | tf_op jit(solution)/shard_map/ppermute | solution.py:474
  168.0 17.6 %all-to-all-start = ((f32[8,4,1024]{2,1,0:T(4,128)}), f32[8,4,1024]{2,1,0:T(4,128)S(1)}, u32[]{:S(2)}, u32[]{:S(2)}) async-start(f32[8,4,1024]{2,1,0:T(4,128)} %copy.26), calls=%async_computation | async-start | bytes 262144 | tf_op jit(solution)/shard_map/all_to_all | solution.py:475
  171.4 759.8 %reduce-scatter.19.cloned.1.call-start = ((), (), s32[]{:S(2)}) async-start(), calls=%async_computation.12 | async-start | bytes 15728640
  192.2 1.3 copy-start.1
  357.2 578.5 %reduce-scatter.17.cloned.1.call-start = ((), (), s32[]{:S(2)}) async-start(), calls=%async_computation.11 | async-start | bytes 26214400
  357.5 48.1 %collective-permute-start.3 = (bf16[512,2048]{1,0:T(8,128)(2,1)}, bf16[512,2048]{1,0:T(8,128)(2,1)S(1)}, u32[]{:S(2)}, u32[]{:S(2)}) collective-permute-start(bf16[512,2048]{1,0:T(8,128)(2,1)} %get-tuple-element.39), channel_id=1, source_target_pairs={{0,8},{8,0},{1,9},{9,1},{2,10},{10,2},{3,11},{11,3},{4,12},{12,4},... | collective-permute-start | bytes 6291464 | tf_op jit(solution)/shard_map/ppermute | solution.py:488
  405.6 1.3 copy-start.2
  680.4 496.5 %reduce-scatter.13.cloned.1.call-start = ((), (), s32[]{:S(2)}) async-start(), calls=%async_computation.9 | async-start | bytes 20971520
  808.3 371.2 %reduce-scatter.15.cloned.1.call-start = ((), (), s32[]{:S(2)}) async-start(), calls=%async_computation.10 | async-start | bytes 20971520
  934.5 250.1 %collective-permute-start.7 = (bf16[384,2048]{1,0:T(8,128)(2,1)}, bf16[384,2048]{1,0:T(8,128)(2,1)}, u32[]{:S(2)}, u32[]{:S(2)}) collective-permute-start(bf16[384,2048]{1,0:T(8,128)(2,1)} %convert_bitcast_fusion.3), channel_id=1, source_target_pairs={{8,0},{0,8},{9,1},{1,9},{10,2},{2,10},{11,3},{3,11},{12,4},{4,12},... | collective-permute-start | bytes 4718600 | tf_op jit(solution)/shard_map/ppermute | solution.py:515
  940.3 244.3 %collective-permute-start.6 = (bf16[640,2048]{1,0:T(8,128)(2,1)}, bf16[640,2048]{1,0:T(8,128)(2,1)}, u32[]{:S(2)}, u32[]{:S(2)}) collective-permute-start(bf16[640,2048]{1,0:T(8,128)(2,1)} %convert_bitcast_fusion), channel_id=1, source_target_pairs={{8,0},{0,8},{9,1},{1,9},{10,2},{2,10},{11,3},{3,11},{12,4},{4,12},... | collective-permute-start | bytes 7864328 | tf_op jit(solution)/shard_map/ppermute | solution.py:515
Sparse Core Ops, SparseCore 0:
  49.4 122.6 all-gather.13
  173.9 70.3 all-gather.7
  246.2 79.3 all-gather.11
  327.9 121.4 all-gather.9
  452.3 150.9 reduce-scatter.18
  680.5 185.1 reduce-scatter.16
  868.8 149.9 reduce-scatter.12
  1021.9 149.9 reduce-scatter.14

commit v6 on v5

v6 whole, which is shorter than its diff:
```python
import functools

import jax
import jax.numpy as jnp
from jax import lax
from jax.experimental import pallas as pl
from jax.experimental.pallas import tpu as pltpu
from jax.sharding import PartitionSpec as P


F32 = jnp.float32
BF16 = jnp.bfloat16
BWD_ROWS = (256, 384, 384)
FWD_ROWS = (512, 512)
STAGES = (((0, 2, 3, 7), (0, 4, 6, 7)), ((0, 2, 3, 5), (0, 4, 5, 7)), ((0, 3, 5, 7),))
VMEM_LIMIT = 65400 * 1024
N_ACC = 3
CORES = 2
UNROLL = 2
MESH = pl.DeviceIdType.MESH


def dot(lhs, rhs):
    return jnp.dot(lhs, rhs, preferred_element_type=F32)


def dot_t(lhs, rhs):
    return lax.dot_general(lhs, rhs, (((1,), (1,)), ((), ())), preferred_element_type=F32)


def dot_a(lhs, rhs):
    return lax.dot_general(lhs, rhs, (((0,), (0,)), ((), ())), preferred_element_type=F32)


def gate_column(gates, expert):
    lanes = lax.broadcasted_iota(jnp.int32, gates.shape, 1)
    return jnp.sum(jnp.where(lanes == expert, gates, 0.0), axis=1, keepdims=True)


def pair_source(step, half, steps):
    core = lax.rem(lax.axis_index('expert'), CORES)
    mine = step // half
    tile = lax.rem(step, half)
    lane = lax.rem(core + 1 + mine, CORES)
    return CORES * (tile // steps) + lane, lax.rem(tile, steps)


def pair_sum(compute, half, steps, tile, inbox_ref, out, exchanges, acc_ref, send_sem, recv_sem, in_sem, out_sem):
    step = pl.program_id(0)
    last = 2 * half - 1
    me = lax.axis_index('expert')
    other = me + 1 - 2 * lax.rem(me, CORES)

    def at(ref, job):
        return ref.at[job // steps, pl.ds(lax.rem(job, steps) * tile, tile)]

    def store(job):
        slot = lax.rem(job + half, N_ACC)
        out_ref, first = out
        rows = pl.ds(first + lax.rem(job, steps) * tile, tile)
        return pltpu.make_async_copy(acc_ref.at[slot], out_ref.at[job // steps, rows], out_sem.at[slot])

    def send(job):
        slot = lax.rem(job, N_ACC)
        return pltpu.make_async_remote_copy(
            src_ref=acc_ref.at[slot], dst_ref=at(inbox_ref, job), send_sem=send_sem.at[slot], recv_sem=recv_sem.at[job],
            device_id={'expert': other}, device_id_type=MESH)

    def fetch(job):
        slot = lax.rem(job + half, N_ACC)
        return pltpu.make_async_copy(at(inbox_ref, job), acc_ref.at[slot], in_sem.at[slot])

    @pl.when(step == 0)
    def _():
        peers = [other] + (exchanges[0].peers if exchanges else [])
        barrier = pltpu.get_barrier_semaphore()
        for peer in peers:
            pl.semaphore_signal(barrier, inc=1, device_id={'expert': peer}, device_id_type=MESH)
        pl.semaphore_wait(barrier, len(peers))

    for exchange in exchanges:
        exchange.advance(step)

    back = step - (N_ACC - 1)

    @pl.when((back >= 0) & (back < half))
    def _():
        send(back).wait_send()

    @pl.when(back >= half)
    def _():
        store(back - half).wait()

    ahead = step + 1 - half

    @pl.when((ahead >= 0) & (ahead < half))
    def _():
        send(ahead).wait_recv()
        fetch(ahead).start()

    acc = acc_ref.at[lax.rem(step, N_ACC)]

    @pl.when(step < half)
    def _():
        acc[...] = jnp.zeros_like(acc)

    @pl.when(step >= half)
    def _():
        fetch(step - half).wait()

    compute(acc)

    @pl.when(step < half)
    def _():
        send(step).start()

    @pl.when(step >= half)
    def _():
        store(step - half).start()

    @pl.when(step == last)
    def _():
        for job in range(half - N_ACC + 1, half):
            store(job).wait()
        for exchange in exchanges:
            exchange.finish()


class Exchange:
    def __init__(self, own_ref, first, ref, stage_ref, send_sem, recv_sem, local_sem, stages):
        me = lax.axis_index('expert')
        flip = lambda dev, bit: dev + bit - 2 * bit * lax.rem(dev // bit, 2)
        core, x, y = flip(me, 1), flip(me, 2), flip(me, 4)
        diag = flip(x, 4)
        self.peers = [x, y]
        self.stages = stages
        rows = ref.shape[1] // 2
        plan = [
            (0, rows, None, x, x),
            (rows, rows, None, y, y),
            (rows, rows, None, x, x),
            (0, rows, None, y, y),
            (0, 2 * rows, None, core, core),
            (0, rows, x, diag, y),
            (rows, rows, y, diag, x),
            (0, rows, x, flip(x, 1), core),
            (rows, rows, y, flip(y, 1), core),
            (rows, rows, x, flip(x, 1), core),
            (0, rows, y, flip(y, 1), core),
            (0, rows, diag, flip(diag, 1), core),
            (rows, rows, diag, flip(diag, 1), core),
        ]

        def copy(k, source, block):
            return pltpu.make_async_remote_copy(
                src_ref=source, dst_ref=ref.at[block, pl.ds(plan[k][0], plan[k][1])], send_sem=send_sem.at[k],
                recv_sem=recv_sem.at[k], device_id={'expert': plan[k][4]}, device_id_type=MESH)

        self.out, self.into = [], []
        for k, (row, n_rows, here, arrives, _) in enumerate(plan):
            own = own_ref.at[pl.ds(first + row, n_rows)]
            self.out.append(copy(k, own if here is None else ref.at[here, pl.ds(row, n_rows)], me if here is None else here))
            self.into.append(copy(k, own, arrives))
        self.take = pltpu.make_async_copy(own_ref.at[pl.ds(first, 2 * rows)], stage_ref, local_sem.at[0])
        self.put = pltpu.make_async_copy(stage_ref, ref.at[me], local_sem.at[1])

    def advance(self, step):
        for at, arrived, started in zip(self.stages, ((), (0, 1), (2, 3), (5, 6)), ((0, 1, 2, 3, 4), (5, 6, 7, 8), (9, 10), (11, 12))):
            @pl.when(step == at)
            def _(arrived=arrived, started=started):
                for k in arrived:
                    self.into[k].wait_recv()
                for k in started:
                    self.out[k].start()
                if not arrived:
                    self.take.start()

        @pl.when(step == 1)
        def _():
            self.take.wait()
            self.put.start()

    def finish(self):
        for k in (4,) + tuple(range(7, 13)):
            self.into[k].wait_recv()
        for copy in self.out:
            copy.wait_send()
        self.put.wait()


N_COPIES = 13


def exchange_scratch(rows, model):
    return [
        pltpu.VMEM((rows, model), BF16),
        pltpu.SemaphoreType.DMA((N_COPIES,)),
        pltpu.SemaphoreType.DMA((N_COPIES,)),
        pltpu.SemaphoreType.DMA((2,)),
    ]


class Weights:
    def __init__(self, hbm, vmem, sem):
        self.n_local = vmem[0].shape[0]
        self.copies = lambda e: [
            pltpu.make_async_copy(src.at[e], dst.at[e], sem.at[e, k]) for k, (src, dst) in enumerate(zip(hbm, vmem))]

        @pl.when(pl.program_id(0) == 0)
        def _():
            for e in range(self.n_local):
                for copy in self.copies(e):
                    copy.start()

    def for_each(self, expert):
        def group(k, carry):
            @pl.when(pl.program_id(0) == 0)
            def _():
                for u in range(UNROLL):
                    for copy in self.copies(k * UNROLL + u):
                        copy.wait()

            for u in range(UNROLL):
                expert(k * UNROLL + u)
            return carry

        lax.fori_loop(0, self.n_local // UNROLL, group, 0)


def weight_scratch(w13, w2):
    return [pltpu.VMEM(w13.shape, BF16), pltpu.VMEM(w2.shape, BF16), pltpu.SemaphoreType.DMA((w13.shape[0], 2))]


def fwd_body(ffn, half, start, n_carried, x_ref, g_ref, w13_hbm, w2_hbm, *refs):
    y_ref, inbox_ref, w13_ref, w2_ref, w_sem, *scratch = refs[n_carried:]
    tile = x_ref.shape[1]
    weights = Weights((w13_hbm, w2_hbm), (w13_ref, w2_ref), w_sem)

    def compute(acc):
        def expert(e):
            gate = gate_column(g_ref[0, start:start + tile], e)
            pre = dot(x_ref[0], w13_ref[e])
            one, three = pre[:, :ffn], pre[:, ffn:]
            hidden = jnp.where(gate > 0.0, one * jax.nn.sigmoid(one) * three, 0.0).astype(BF16)
            acc[...] += gate * dot(hidden, w2_ref[e]).astype(BF16).astype(F32)

        weights.for_each(expert)

    pair_sum(compute, half, 1, tile, inbox_ref, (y_ref, start), [], *scratch)


def pair_scratch(tile, model, half):
    return [
        pltpu.VMEM((N_ACC, tile, model), F32),
        pltpu.SemaphoreType.DMA((N_ACC,)),
        pltpu.SemaphoreType.DMA((half,)),
        pltpu.SemaphoreType.DMA((N_ACC,)),
        pltpu.SemaphoreType.DMA((N_ACC,)),
    ]


def pair_params(collective_id):
    return pltpu.CompilerParams(
        dimension_semantics=('arbitrary',), vmem_limit_bytes=VMEM_LIMIT, collective_id=collective_id, has_side_effects=True)


HBM = pl.BlockSpec(memory_space=pl.ANY)


def at_source(half):
    def index(i):
        return pair_source(i, half, 1)[0], 0, 0

    return index


def expert_fwd(x, gates, w13, w2, start, carried, collective_id):
    n_src, tile, model = x.shape
    n_tok = gates.shape[1]
    n_local, ffn = w2.shape[:2]
    half = n_src // CORES
    at = at_source(half)
    flops = 2 * n_src * tile * n_local * model * ffn * 3
    return pl.pallas_call(
        functools.partial(fwd_body, ffn, half, start, len(carried)),
        grid=(2 * half,),
        in_specs=[pl.BlockSpec((1, tile, model), at), pl.BlockSpec((1, n_tok, n_local), at), HBM, HBM] + [HBM] * len(carried),
        out_specs=[HBM, HBM],
        out_shape=[jax.ShapeDtypeStruct((half, n_tok, model), F32), jax.ShapeDtypeStruct((half, tile, model), F32)],
        scratch_shapes=weight_scratch(w13, w2) + pair_scratch(tile, model, half),
        input_output_aliases={4 + i: i for i in range(len(carried))},
        compiler_params=pair_params(collective_id),
        cost_estimate=pl.CostEstimate(flops=flops, bytes_accessed=n_src * tile * model * 6, transcendentals=0),
        name='expert_fwd',
    )(x, gates, w13, w2, *carried)[0]


def bwd_body(ffn, half, start, first, n_carried, hosted, stages, x_ref, dy_ref, g_ref, w13_hbm, w2_hbm, *refs):
    refs = list(refs[n_carried:])
    own_refs, refs = refs[:len(hosted)], refs[len(hosted):]
    (dx_ref, da_ref, h_ref, inbox_ref), refs = refs[:4], refs[4:]
    buf_refs, refs = refs[:len(hosted)], refs[len(hosted):]
    w13_ref, w2_ref, w_sem, *refs = refs
    scratch, refs = refs[:5], refs[5:]
    exchanges = [Exchange(own_refs[k], row, buf_refs[k], *refs[4 * k:4 * k + 4], stages[k]) for k, (row, _) in enumerate(hosted)]
    tile = x_ref.shape[1]
    weights = Weights((w13_hbm, w2_hbm), (w13_ref, w2_ref), w_sem)

    def compute(acc):
        def expert(e):
            gate = gate_column(g_ref[0, start:start + tile], e)
            live = gate > 0.0
            pre = dot(x_ref[0], w13_ref[e])
            one, three = pre[:, :ffn], pre[:, ffn:]
            sig = jax.nn.sigmoid(one)
            act = one * sig
            h_ref[0, :, pl.ds(pl.multiple_of(e * ffn, ffn), ffn)] = jnp.where(live, act * three, 0.0).astype(BF16)
            d_out = (gate * dy_ref[0].astype(F32)).astype(BF16)
            d_hid = dot_t(d_out, w2_ref[e]).astype(BF16).astype(F32)
            d_one = jnp.where(live, d_hid * three * sig * (1.0 + one * (1.0 - sig)), 0.0).astype(BF16)
            d_three = jnp.where(live, d_hid * act, 0.0).astype(BF16)
            d_pre = jnp.concatenate([d_one, d_three], axis=1)
            da_ref[0, :, pl.ds(pl.multiple_of(2 * e * ffn, 2 * ffn), 2 * ffn)] = d_pre
            acc[...] += dot_t(d_pre, w13_ref[e]).astype(BF16).astype(F32)

        weights.for_each(expert)

    pair_sum(compute, half, 1, tile, inbox_ref, (dx_ref, first), exchanges, *scratch)


def expert_bwd(x, dy, gates, w13, w2, start, dx_rows, first, carried, hosted, stages, collective_id):
    n_src, tile, model = x.shape
    n_tok = gates.shape[1]
    n_local, ffn = w2.shape[:2]
    half = n_src // CORES
    at = at_source(half)
    flops = 2 * n_src * tile * n_local * model * ffn * 5
    outs = pl.pallas_call(
        functools.partial(bwd_body, ffn, half, start, first, len(carried), [h[1:] for h in hosted], stages),
        grid=(2 * half,),
        in_specs=[pl.BlockSpec((1, tile, model), at)] * 2 + [pl.BlockSpec((1, n_tok, n_local), at)]
        + [HBM] * (2 + len(carried) + len(hosted)),
        out_specs=[
            HBM,
            pl.BlockSpec((1, tile, 2 * ffn * n_local), at),
            pl.BlockSpec((1, tile, ffn * n_local), at),
        ] + [HBM] * (1 + len(hosted)),
        out_shape=[
            jax.ShapeDtypeStruct((half, dx_rows, model), F32),
            jax.ShapeDtypeStruct((n_src, tile, 2 * ffn * n_local), BF16),
            jax.ShapeDtypeStruct((n_src, tile, ffn * n_local), BF16),
            jax.ShapeDtypeStruct((half, tile, model), F32),
        ] + [jax.ShapeDtypeStruct((n_src, rows, model), BF16) for _, _, rows in hosted],
        scratch_shapes=weight_scratch(w13, w2) + pair_scratch(tile, model, half)
        + [ref for _, _, rows in hosted for ref in exchange_scratch(rows, model)],
        input_output_aliases={5 + i: 0 for i in range(len(carried))},
        compiler_params=pair_params(collective_id),
        cost_estimate=pl.CostEstimate(flops=flops, bytes_accessed=n_src * tile * model * 14, transcendentals=0),
        name='expert_bwd',
    )(x, dy, gates, w13, w2, *carried, *[h[0] for h in hosted])
    return outs[0], outs[1], outs[2], outs[4:]


def rows_joined(refs, column=0, columns=None):
    parts = [ref[0, :, column:column + (columns or ref.shape[2])] for ref in refs]
    return parts[0] if len(parts) == 1 else jnp.concatenate(parts, axis=0)


def grad_body(ffn, n_parts, g_ref, *refs):
    x_refs, dy_refs, da_refs, h_refs = (refs[k * n_parts:(k + 1) * n_parts] for k in range(4))
    dw1_ref, dw3_ref, dw2_ref, acc13_ref, acc2_ref = refs[4 * n_parts:]
    e, k = pl.program_id(0), pl.program_id(1)

    @pl.when(k == 0)
    def _():
        acc13_ref[...] = jnp.zeros_like(acc13_ref)
        acc2_ref[...] = jnp.zeros_like(acc2_ref)

    for m in range(0, acc13_ref.shape[0], ffn):
        acc13_ref[m:m + ffn] += dot_a(rows_joined(x_refs, m, ffn), rows_joined(da_refs))
    d_out = (gate_column(g_ref[0], e) * rows_joined(dy_refs).astype(F32)).astype(BF16)
    acc2_ref[...] += dot_a(rows_joined(h_refs), d_out)

    @pl.when(k == pl.num_programs(1) - 1)
    def _():
        dw1_ref[0] = acc13_ref[:, :ffn].astype(BF16)
        dw3_ref[0] = acc13_ref[:, ffn:].astype(BF16)
        dw2_ref[0] = acc2_ref[...].astype(BF16)


def weight_grads(gates, xs, dys, d_pres, hiddens):
    n_src, n_tok, n_local = gates.shape
    model = xs[0].shape[2]
    ffn = hiddens[0].shape[2] // n_local
    flops = 2 * n_src * n_tok * n_local * model * ffn * 3
    at = lambda e, k: (k, 0, 0)
    at_e = lambda e, k: (k, 0, e)
    out = lambda e, k: (e, 0, 0)

    return pl.pallas_call(
        functools.partial(grad_body, ffn, len(xs)),
        grid=(n_local, n_src),
        in_specs=[pl.BlockSpec((1, n_tok, n_local), at)]
        + [pl.BlockSpec((1, x.shape[1], model), at) for x in list(xs) + list(dys)]
        + [pl.BlockSpec((1, d.shape[1], 2 * ffn), at_e) for d in d_pres]
        + [pl.BlockSpec((1, h.shape[1], ffn), at_e) for h in hiddens],
        out_specs=[
            pl.BlockSpec((1, model, ffn), out),
            pl.BlockSpec((1, model, ffn), out),
            pl.BlockSpec((1, ffn, model), out),
        ],
        out_shape=[
            jax.ShapeDtypeStruct((n_local, model, ffn), BF16),
            jax.ShapeDtypeStruct((n_local, model, ffn), BF16),
            jax.ShapeDtypeStruct((n_local, ffn, model), BF16),
        ],
        scratch_shapes=[pltpu.VMEM((model, 2 * ffn), F32), pltpu.VMEM((ffn, model), F32)],
        compiler_params=pltpu.CompilerParams(dimension_semantics=('arbitrary', 'arbitrary'), vmem_limit_bytes=VMEM_LIMIT),
        cost_estimate=pl.CostEstimate(flops=flops, bytes_accessed=n_src * n_tok * model * 4 * n_local, transcendentals=0),
        name='weight_grads',
    )(gates, *xs, *dys, *d_pres, *hiddens)


def solution(mesh):
    n_stage = mesh.shape['stage']
    n_dev = mesh.shape['expert']
    to_next = [(stage_idx, (stage_idx + 1) % n_stage) for stage_idx in range(n_stage)]
    to_prev = [((stage_idx + 1) % n_stage, stage_idx) for stage_idx in range(n_stage)]
    tok_spec = P('stage', 'expert', None)
    w_spec = P('stage', 'expert', None, None)
    same_core = [list(range(core, n_dev, CORES)) for core in range(CORES)]

    def moe_body(x_act, route_idx, route_wts, w_one, w_three, w_two, dy_act):
        x_src = x_act[0]
        n_tok, _ = x_src.shape
        n_local = w_one.shape[1]
        n_exp = n_local * n_dev

        def gather(rows):
            return lax.all_gather(rows, 'expert', axis=0, tiled=False)

        def reduce_rows(part):
            return lax.psum_scatter(part, 'expert', scatter_dimension=0, axis_index_groups=same_core, tiled=False).astype(BF16)

        hits = route_idx[0][:, :, None] == jnp.arange(n_exp, dtype=jnp.int32)
        gate_src = jnp.sum(jnp.where(hits, route_wts[0][:, :, None], 0.0), axis=1)
        gate_src = jnp.transpose(gate_src.reshape(n_tok, n_dev, n_local), (1, 2, 0))
        gate_dst = lax.ppermute(gate_src, 'stage', to_next)
        gates = jnp.transpose(lax.all_to_all(gate_dst, 'expert', 0, 0), (0, 2, 1))

        w13 = jnp.concatenate([w_one[0], w_three[0]], axis=2)
        w2 = w_two[0]

        def spans(sizes):
            ends = [sum(sizes[:k + 1]) for k in range(len(sizes))]
            return [slice(end - size, end) for end, size in zip(ends, sizes)]

        bwd, fwd = spans(BWD_ROWS), spans(FWD_ROWS)
        dx_rows = sum(BWD_ROWS[:2]), BWD_ROWS[2]

        def hop(rows):
            return lax.ppermute(x_src[rows], 'stage', to_next)

        dys = [gather(dy_act[0, bwd[0]])]
        xs = [gather(hop(bwd[0]))]

        d_pres, hiddens = [], []
        dx_parts = []
        for k in range(3):
            if k < 2:
                rows = BWD_ROWS[k + 1]
                hosted = ((dy_act[0], bwd[k + 1].start, rows), (hop(bwd[k + 1]), 0, rows))
            else:
                hosted = ((hop(fwd[1]), 0, FWD_ROWS[1]),)
            dx_part, d_pre, hidden, arrived = expert_bwd(
                xs[k], dys[k], gates, w13, w2, bwd[k].start, dx_rows[k // 2], BWD_ROWS[0] if k == 1 else 0,
                (dx_part,) if k == 1 else (), hosted, STAGES[k], k)
            if k < 2:
                dys.append(arrived[0])
                xs.append(arrived[1])
            d_pres.append(d_pre)
            hiddens.append(hidden)
            if k > 0:
                dx_dst = reduce_rows(dx_part)
                dx_parts.append(lax.ppermute(dx_dst, 'stage', to_prev))
        dx_out = jnp.concatenate(dx_parts, axis=0)

        x_dst = hop(fwd[0])
        x_fwd = gather(x_dst), arrived[0]
        y_part = ()
        for k in range(2):
            y_part = (expert_fwd(x_fwd[k], gates, w13, w2, fwd[k].start, y_part, 3 + k),)
        y_out = reduce_rows(y_part[0])

        g_one, g_three, g_two = weight_grads(gates, xs, dys, d_pres, hiddens)
        return y_out[None], dx_out[None], g_one[None], g_three[None], g_two[None]

    return jax.shard_map(moe_body, mesh=mesh, in_specs=(tok_spec, tok_spec, tok_spec, w_spec, w_spec, w_spec, tok_spec), out_specs=(tok_spec, tok_spec, w_spec, w_spec, w_spec), check_vma=False)
```

time: 1200 us -> 1270 us (1.058)
  Pallas kernels: 918 us -> 980 us
  waiting for transfers between devices: 181 us -> 204 us
    ppermute x5, waiting for transfers between devices: 135 us -> 23.2 us  [hop(): return lax.ppermute(x_src[rows], 'stage', to_next)]
    unnamed x12 -> x9, waiting for transfers between devices: 0.2 us -> 104 us
    pallas_call x7 -> x5, Pallas kernels: 682 us -> 746 us  [the longest x3 508 us: expert_bwd(): pl.pallas_call(functools.partial(bwd_body, ffn, half, start, first, len(c...]
    ppermute x1, waiting for transfers between devices: 45.9 us -> 77.1 us  [moe_body(): gate_dst = lax.ppermute(gate_src, 'stage', to_next)]
  transfers between devices with their start and end apart: 17 -> 15, of which waited for: 5 -> 4; matrix products, arithmetic and copies ran while one was open for 5% -> 3% of each run, Pallas kernels for 77% -> 77%
where the time goes in v6:
time: 1270 us; the launch traced here: 1260 us
  Pallas kernels  980 us (77%)
  waiting for transfers between devices  204 us (16%)
  other arithmetic  32.9 us (3%)
  local copies, waits for them, and re-layouts  16.5 us (1%)
  starting transfers between devices  16.3 us (1%)
  between operations  14.5 us (1%)
    pallas_call x3, Pallas kernels, expert_bwd(): pl.pallas_call(functools.partial(bwd_body, ffn, half, start, first, len(c...  508 us
    pallas_call x2, Pallas kernels, expert_fwd(): pl.pallas_call(functools.partial(fwd_body, ffn, half, start, len(carried)...  238 us
    pallas_call x1, Pallas kernels, weight_grads(): pl.pallas_call(functools.partial(grad_body, ffn, len(xs)), grid=(n_local,...  234 us
    unnamed x9, waiting for transfers between devices  104 us
    ppermute x1, waiting for transfers between devices, moe_body(): gate_dst = lax.ppermute(gate_src, 'stage', to_next)  77.1 us
  transfers between devices with their start and end apart: 15, of which 4 were waited for; matrix products, arithmetic and copies ran while one was open for 3% of the time, Pallas kernels for 77%

profile of v6, /device:TPU:0, one launch (start us, length us, event | category | flops | bytes accessed | tf_op | source)
XLA Modules:
  0.0 1264.1 jit_solution(17333813156036913830)
XLA Ops:
  7.2 2.3 slice.35
  11.0 3.3 collective-permute-start
  14.3 23.2 %collective-permute-done = bf16[256,2048]{1,0:T(8,128)(2,1)S(1)} collective-permute-done((bf16[256,2048]{1,0:T(8,128)(2,1)S(1)}, bf16[256,2048]{1,0:T(8,128)(2,1)S(1)}, u32[]{:S(2)}, u32[]{:S(2)}) %collective-permute-start) | collective-permute-done | bytes 1048608 | tf_op jit(solution)/shard_map/ppermute | solution.py:462
  38.4 5.0 slice_bitcast_fusion
  43.4 1.7 collective-permute-start.5
  45.2 2.0 slice_bitcast_fusion.2
  47.7 1.8 collective-permute-start.1
  49.8 1.7 collective-permute-start.4
  51.5 77.1 %collective-permute-done.1 = f32[8,4,1024]{2,0,1:T(8,128)S(1)} collective-permute-done((f32[8,4,1024]{2,0,1:T(8,128)S(1)}, f32[8,4,1024]{2,0,1:T(8,128)S(1)}, u32[]{:S(2)}, u32[]{:S(2)}) %collective-permute-start.1) | collective-permute-done | bytes 131104 | tf_op jit(solution)/shard_map/ppermute | solution.py:448
  129.4 3.9 all-to-all-start
  133.3 14.0 %pad_maximum_fusion.w13_hbm = bf16[4,2048,1024]{2,1,0:T(8,128)(2,1)} fusion(bf16[4,2048,512]{2,1,0:T(8,128)(2,1)} %bitcast.32, bf16[4,2048,512]{2,1,0:T(8,128)(2,1)} %bitcast.33), kind=kLoop, calls=%fused_computation | loop fusion | flops 33554432 | bytes 33554432 | tf_op jit(solution)/shard_map/concatenate | solution.py:451
  147.3 2.7 copy.26
  151.5 190.8 %expert_bwd.3 = (f32[4,640,2048]{2,1,0:T(8,128)}, bf16[8,256,4096]{2,1,0:T(8,128)(2,1)}, bf16[8,256,2048]{2,1,0:T(8,128)(2,1)}, f32[4,256,2048]{2,1,0:T(8,128)},...) custom-call(bf16[8,256,2048]{2,1,0:T(8,128)(2,1)} %bitcast.51, ...), custom_call_target="tpu_custom_call" | custom-call | flops 85899345920 | bytes 58720256 | tf_op jit(solution)/shard_map/expert_bwd/pallas_call | solution.py:338
  342.3 158.6 %expert_bwd.4 = (f32[4,640,2048]{2,1,0:T(8,128)}, bf16[8,384,4096]{2,1,0:T(8,128)(2,1)}, bf16[8,384,2048]{2,1,0:T(8,128)(2,1)}, f32[4,384,2048]{2,1,0:T(8,128)},...) custom-call(bf16[8,384,2048]{2,1,0:T(8,128)(2,1)} %get-tuple-element.24.x_ref.refs_1, ...), custom_call_target="tpu_custom_call", output_to_operand_aliasing={{0}: (5, {})} | custom-call | flops 128849018880 | bytes 88080384 | tf_op jit(solution)/shard_map/expert_bwd/pallas_call | solution.py:338
  501.0 158.2 %expert_bwd.5 = (f32[4,384,2048]{2,1,0:T(8,128)}, bf16[8,384,4096]{2,1,0:T(8,128)(2,1)}, bf16[8,384,2048]{2,1,0:T(8,128)(2,1)}, f32[4,384,2048]{2,1,0:T(8,128)}, bf16[8,512,2048]{2,1,0:T(8,128)(2,1)}) custom-call(bf16[8,384,2048]{2,1,0:T(8,128)(2,1)} %get-tuple-element.27.x_ref.refs_2_, bf16[8,384,2048]{2,1,0:T(8,128)(2,1)} %get-tuple-element.28.dy_ref.refs_5_, ...), custom_call_target="tpu_custom_call" | custom-call | flops 128849018880 | bytes 88080384 | tf_op jit(solution)/shard_map/expert_bwd/pallas_call | solution.py:338
  659.9 119.4 %expert_fwd.2 = (f32[4,1024,2048]{2,1,0:T(8,128)}, f32[4,512,2048]{2,1,0:T(8,128)}) custom-call(bf16[8,512,2048]{2,1,0:T(8,128)(2,1)} %bitcast.45, f32[8,1024,4]{2,1,0:T(8,128)} %bitcast.37, bf16[4,2048,1024]{2,1,0:T(8,128)(2,1)} %pad_maximum_fusion.w13_hbm, bf16[4,512,2048]{2,1,0:T(8,128)(2,1)} %bitcast.49), custom_call_target="tpu_custom_call" | custom-call | flops 103079215104 | bytes 50331648 | tf_op jit(solution)/shard_map/expert_fwd/pallas_call | solution.py:284
  779.3 118.8 %expert_fwd.3 = (f32[4,1024,2048]{2,1,0:T(8,128)}, f32[4,512,2048]{2,1,0:T(8,128)}) custom-call(bf16[8,512,2048]{2,1,0:T(8,128)(2,1)} %get-tuple-element.29.x_ref, f32[8,1024,4]{2,1,0:T(8,128)} %bitcast.38, bf16[4,2048,1024]{2,1,0:T(8,128)(2,1)} %pad_maximum_fusion.w13_hbm, bf16[4,512,2048]{2,1,0:T(8,128)(2,1)} %bitcast.50, ...), custom_call_target="tpu_custom_call", output_to_operand_aliasing={{0}: (4, {})} | custom-call | flops 103079215104 | bytes 50331648 | tf_op jit(solution)/shard_map/expert_fwd/pallas_call | solution.py:284
  898.1 3.3 convert_bitcast_fusion.1
  903.0 60.2 %reduce-scatter.12.cloned.1.call-done = f32[1,640,2048]{2,1,0:T(8,128)} async-done(((f32[4,640,2048]{2,1,0:T(8,128)}), f32[1,640,2048]{2,1,0:T(8,128)}) %reduce-scatter.12.cloned.1.call-update) | async-done | bytes 5242896
  963.3 4.4 convert_bitcast_fusion
  969.1 233.7 %weight_grads.1 = (bf16[4,2048,512]{2,1,0:T(8,128)(2,1)}, bf16[4,2048,512]{2,1,0:T(8,128)(2,1)}, bf16[4,512,2048]{2,1,0:T(8,128)(2,1)}) custom-call(f32[8,1024,4]{2,1,0:T(8,128)} %bitcast.39, bf16[8,256,2048]{2,1,0:T(8,128)(2,1)} %bitcast.52, bf16[8,384,2048]{2,1,0:T(8,128)(2,1)} %get-tuple-element.24.x_ref.refs_1_, ...), custom_call_target="tpu_custom_call" | custom-call | flops 206158430208 | bytes 268435456 | tf_op jit(solution)/shard_map/weight_grads/pallas_call | solution.py:400
  1202.9 5.0 maximum_bitcast_fusion
  1207.9 43.1 %reduce-scatter.10.cloned.1.call-done = f32[1,1024,2048]{2,1,0:T(8,128)} async-done(((f32[4,1024,2048]{2,1,0:T(8,128)}), f32[1,1024,2048]{2,1,0:T(8,128)}) %reduce-scatter.10.cloned.1.call-update) | async-done | bytes 8388624
  1251.0 6.0 convert_element_type.16
  (42 shorter events, 9.2 us)
Async XLA Ops:
  7.2 144.3 %all-gather.6.cloned.1.call-start = ((), (), s32[]{:S(2)}) async-start(), calls=%async_computation.4 | async-start | bytes 9437184 | tf_op jit(solution)/shard_map/all_gather | solution.py:440
  9.6 141.9 %all-gather.8.cloned.1.call-start = ((), (), s32[]{:S(2)}) async-start(), calls=%async_computation.5 | async-start | bytes 9437184 | tf_op jit(solution)/shard_map/all_gather | solution.py:440
  10.9 36.6 %copy-start.3 = (f32[1,1024,8]{1,2,0:T(8,128)S(1)}, f32[1,1024,8]{1,2,0:T(8,128)}, u32[]{:S(2)}) copy-start(f32[1,1024,8]{1,2,0:T(8,128)} %param.9) | copy-start | bytes 98308
  10.9 36.6 %copy-start.4 = (s32[1,1024,8]{1,2,0:T(8,128)S(1)}, s32[1,1024,8]{1,2,0:T(8,128)}, u32[]{:S(2)}) copy-start(s32[1,1024,8]{1,2,0:T(8,128)} %param.8) | copy-start | bytes 98308
  11.0 26.5 %collective-permute-start = (bf16[256,2048]{1,0:T(8,128)(2,1)S(1)}, bf16[256,2048]{1,0:T(8,128)(2,1)S(1)}, u32[]{:S(2)}, u32[]{:S(2)}) collective-permute-start(bf16[256,2048]{1,0:T(8,128)(2,1)S(1)} %slice_bitcast_fusion.4), channel_id=1, source_target_pairs={{0,8},{8,0},{1,9},{9,1},{2,10},{10,2},{3,11},{11,3},{4,12},{12,4},... | collective-permute-start | bytes 3145736 | tf_op jit(solution)/shard_map/ppermute | solution.py:462
  37.4 1.0 copy-start.2
  38.4 6.7 copy-start
  43.4 106.6 %collective-permute-start.5 = (bf16[512,2048]{1,0:T(8,128)(2,1)}, bf16[512,2048]{1,0:T(8,128)(2,1)S(1)}, u32[]{:S(2)}, u32[]{:S(2)}) collective-permute-start(bf16[512,2048]{1,0:T(8,128)(2,1)} %get-tuple-element.43), channel_id=1, source_target_pairs={{0,8},{8,0},{1,9},{9,1},{2,10},{10,2},{3,11},{11,3},{4,12},{12,4},... | collective-permute-start | bytes 6291464 | tf_op jit(solution)/shard_map/ppermute | solution.py:462
  47.2 104.2 %collective-permute-start.2 = (bf16[384,2048]{1,0:T(8,128)(2,1)}, bf16[384,2048]{1,0:T(8,128)(2,1)}, u32[]{:S(2)}, u32[]{:S(2)}) collective-permute-start(bf16[384,2048]{1,0:T(8,128)(2,1)} %get-tuple-element.46), channel_id=1, source_target_pairs={{0,8},{8,0},{1,9},{9,1},{2,10},{10,2},{3,11},{11,3},{4,12},{12,4},... | collective-permute-start | bytes 4718600 | tf_op jit(solution)/shard_map/ppermute | solution.py:462
  47.7 80.9 %collective-permute-start.1 = (f32[8,4,1024]{2,0,1:T(8,128)S(1)}, f32[8,4,1024]{2,0,1:T(8,128)S(1)}, u32[]{:S(2)}, u32[]{:S(2)}) collective-permute-start(f32[8,4,1024]{2,0,1:T(8,128)S(1)} %copy.24), channel_id=1, source_target_pairs={{0,8},{8,0},{1,9},{9,1},{2,10},{10,2},{3,11},{11,3},{4,12},{12,4},... | collective-permute-start | bytes 393224 | tf_op jit(solution)/shard_map/ppermute | solution.py:448
  49.5 292.8 %collective-permute-start.3 = (bf16[384,2048]{1,0:T(8,128)(2,1)}, bf16[384,2048]{1,0:T(8,128)(2,1)}, u32[]{:S(2)}, u32[]{:S(2)}) collective-permute-start(bf16[384,2048]{1,0:T(8,128)(2,1)} %get-tuple-element.45), channel_id=1, source_target_pairs={{0,8},{8,0},{1,9},{9,1},{2,10},{10,2},{3,11},{11,3},{4,12},{12,4},... | collective-permute-start | bytes 4718600 | tf_op jit(solution)/shard_map/ppermute | solution.py:462
  49.8 451.2 %collective-permute-start.4 = (bf16[512,2048]{1,0:T(8,128)(2,1)}, bf16[512,2048]{1,0:T(8,128)(2,1)}, u32[]{:S(2)}, u32[]{:S(2)}) collective-permute-start(bf16[512,2048]{1,0:T(8,128)(2,1)} %get-tuple-element.44), channel_id=1, source_target_pairs={{0,8},{8,0},{1,9},{9,1},{2,10},{10,2},{3,11},{11,3},{4,12},{12,4},... | collective-permute-start | bytes 6291464 | tf_op jit(solution)/shard_map/ppermute | solution.py:462
  129.4 17.9 %all-to-all-start = ((f32[8,4,1024]{2,1,0:T(4,128)}), f32[8,4,1024]{2,1,0:T(4,128)S(1)}, u32[]{:S(2)}, u32[]{:S(2)}) async-start(f32[8,4,1024]{2,1,0:T(4,128)} %copy.25), calls=%async_computation | async-start | bytes 262144 | tf_op jit(solution)/shard_map/all_to_all | solution.py:449
  133.3 526.6 %all-gather.10.cloned.1.call-start = ((), (), s32[]{:S(2)}) async-start(), calls=%async_computation.6 | async-start | bytes 18874368 | tf_op jit(solution)/shard_map/all_gather | solution.py:440
  150.0 1.3 copy-start.1
  151.4 746.8 %reduce-scatter.14.cloned.1.call-start = ((), (), s32[]{:S(2)}) async-start(), calls=%async_computation.9 | async-start | bytes 15728640
  659.2 304.1 %reduce-scatter.12.cloned.1.call-start = ((), (), s32[]{:S(2)}) async-start(), calls=%async_computation.8 | async-start | bytes 26214400
  659.8 591.2 %reduce-scatter.10.cloned.1.call-start = ((), (), s32[]{:S(2)}) async-start(), calls=%async_computation.7 | async-start | bytes 41943040
  901.4 301.4 %collective-permute-start.7 = (bf16[384,2048]{1,0:T(8,128)(2,1)}, bf16[384,2048]{1,0:T(8,128)(2,1)}, u32[]{:S(2)}, u32[]{:S(2)}) collective-permute-start(bf16[384,2048]{1,0:T(8,128)(2,1)} %convert_bitcast_fusion.1), channel_id=1, source_target_pairs={{8,0},{0,8},{9,1},{1,9},{10,2},{2,10},{11,3},{3,11},{12,4},{4,12},... | collective-permute-start | bytes 4718600 | tf_op jit(solution)/shard_map/ppermute | solution.py:485
  967.6 235.2 %collective-permute-start.6 = (bf16[640,2048]{1,0:T(8,128)(2,1)}, bf16[640,2048]{1,0:T(8,128)(2,1)}, u32[]{:S(2)}, u32[]{:S(2)}) collective-permute-start(bf16[640,2048]{1,0:T(8,128)(2,1)} %convert_bitcast_fusion), channel_id=1, source_target_pairs={{8,0},{0,8},{9,1},{1,9},{10,2},{2,10},{11,3},{3,11},{12,4},{4,12},... | collective-permute-start | bytes 7864328 | tf_op jit(solution)/shard_map/ppermute | solution.py:485
Sparse Core Ops, SparseCore 0:
  9.8 53.2 all-gather.5
  65.0 50.4 all-gather.7
  151.5 155.1 all-gather.9
  659.3 116.9 reduce-scatter.13
  779.2 183.9 reduce-scatter.11
  966.1 284.7 reduce-scatter.9

commit v7 on v6

--- a/solution.py
+++ b/solution.py
@@ -12,7 +12,8 @@
 BF16 = jnp.bfloat16
 BWD_ROWS = (256, 384, 384)
 FWD_ROWS = (512, 512)
-STAGES = (((0, 2, 3, 7), (0, 4, 6, 7)), ((0, 2, 3, 5), (0, 4, 5, 7)), ((0, 3, 5, 7),))
+X_ROWS = 256
+STAGES = {'bwd_1': ((0, 2, 4, 6),), 'bwd_2': ((0, 2, 4, 6), (0, 3, 5, 7)), 'fwd_0': ((0, 2, 4, 6),)}
 VMEM_LIMIT = 65400 * 1024
 N_ACC = 3
 CORES = 2
@@ -35,6 +36,13 @@
 def gate_column(gates, expert):
     lanes = lax.broadcasted_iota(jnp.int32, gates.shape, 1)
     return jnp.sum(jnp.where(lanes == expert, gates, 0.0), axis=1, keepdims=True)
+
+
+def meet(peers):
+    barrier = pltpu.get_barrier_semaphore()
+    for peer in peers:
+        pl.semaphore_signal(barrier, inc=1, device_id={'expert': peer}, device_id_type=MESH)
+    pl.semaphore_wait(barrier, len(peers))
 
 
 def pair_source(step, half, steps):
@@ -72,11 +80,7 @@
 
     @pl.when(step == 0)
     def _():
-        peers = [other] + (exchanges[0].peers if exchanges else [])
-        barrier = pltpu.get_barrier_semaphore()
-        for peer in peers:
-            pl.semaphore_signal(barrier, inc=1, device_id={'expert': peer}, device_id_type=MESH)
-        pl.semaphore_wait(barrier, len(peers))
+        meet(exchanges[0].peers if exchanges else [other])
 
     for exchange in exchanges:
         exchange.advance(step)
@@ -127,12 +131,12 @@
 
 
 class Exchange:
-    def __init__(self, own_ref, first, ref, stage_ref, send_sem, recv_sem, local_sem, stages):
+    def __init__(self, own_ref, first, ref, stage_ref, send_sem, recv_sem, local_sem, stages=()):
         me = lax.axis_index('expert')
         flip = lambda dev, bit: dev + bit - 2 * bit * lax.rem(dev // bit, 2)
         core, x, y = flip(me, 1), flip(me, 2), flip(me, 4)
         diag = flip(x, 4)
-        self.peers = [x, y]
+        self.peers = [core, x, y]
         self.stages = stages
         rows = ref.shape[1] // 2
         plan = [
@@ -164,21 +168,30 @@
         self.take = pltpu.make_async_copy(own_ref.at[pl.ds(first, 2 * rows)], stage_ref, local_sem.at[0])
         self.put = pltpu.make_async_copy(stage_ref, ref.at[me], local_sem.at[1])
 
+    def stage(self, k):
+        arrived, started = (((), (0, 1, 2, 3, 4)), ((0, 1), (5, 6, 7, 8)), ((2, 3), (9, 10)), ((5, 6), (11, 12)))[k]
+        for n in arrived:
+            self.into[n].wait_recv()
+        for n in started:
+            self.out[n].start()
+        if k == 0:
+            self.take.start()
+
+    def settle(self):
+        self.take.wait()
+        self.put.start()
+
     def advance(self, step):
-        for at, arrived, started in zip(self.stages, ((), (0, 1), (2, 3), (5, 6)), ((0, 1, 2, 3, 4), (5, 6, 7, 8), (9, 10), (11, 12))):
-            @pl.when(step == at)
-            def _(arrived=arrived, started=started):
-                for k in arrived:
-                    self.into[k].wait_recv()
-                for k in started:
-                    self.out[k].start()
-                if not arrived:
-                    self.take.start()
-
-        @pl.when(step == 1)
-        def _():
-            self.take.wait()
-            self.put.start()
+        for k, at in enumerate(self.stages):
+            pl.when(step == at)(functools.partial(self.stage, k))
+        pl.when(step == 1)(self.settle)
+
+    def run(self):
+        for k in range(4):
+            self.stage(k)
+            if k == 0:
+                self.settle()
+        self.finish()
 
     def finish(self):
         for k in (4,) + tuple(range(7, 13)):
@@ -200,6 +213,29 @@
     ]
 
 
+def gather_body(first, own_ref, buf_ref, *scratch):
+    exchange = Exchange(own_ref, first, buf_ref, *scratch)
+    meet(exchange.peers)
+    exchange.run()
+
+
+def gather_now(array, first, rows, n_dev, collective_id):
+    model = array.shape[1]
+    return pl.pallas_call(
+        functools.partial(gather_body, first),
+        in_specs=[pl.BlockSpec(memory_space=pl.ANY)],
+        out_specs=pl.BlockSpec(memory_space=pl.ANY),
+        out_shape=jax.ShapeDtypeStruct((n_dev, rows, model), array.dtype),
+        scratch_shapes=exchange_scratch(rows, model),
+        compiler_params=pltpu.CompilerParams(collective_id=collective_id, has_side_effects=True),
+        name='gather_now',
+    )(array)
+
+
+def hosted_parts(hosted, stages, own_refs, buf_refs, scratch):
+    return [Exchange(own_refs[k], row, buf_refs[k], *scratch[4 * k:4 * k + 4], stages[k]) for k, (row, _) in enumerate(hosted)]
+
+
 class Weights:
     def __init__(self, hbm, vmem, sem):
         self.n_local = vmem[0].shape[0]
@@ -212,7 +248,7 @@
                 for copy in self.copies(e):
                     copy.start()
 
-    def for_each(self, expert):
+    def for_each(self, experts):
         def group(k, carry):
             @pl.when(pl.program_id(0) == 0)
             def _():
@@ -220,8 +256,7 @@
                     for copy in self.copies(k * UNROLL + u):
                         copy.wait()
 
-            for u in range(UNROLL):
-                expert(k * UNROLL + u)
+            experts([k * UNROLL + u for u in range(UNROLL)])
             return carry
 
         lax.fori_loop(0, self.n_local // UNROLL, group, 0)
@@ -231,22 +266,30 @@
     return [pltpu.VMEM(w13.shape, BF16), pltpu.VMEM(w2.shape, BF16), pltpu.SemaphoreType.DMA((w13.shape[0], 2))]
 
 
-def fwd_body(ffn, half, start, n_carried, x_ref, g_ref, w13_hbm, w2_hbm, *refs):
-    y_ref, inbox_ref, w13_ref, w2_ref, w_sem, *scratch = refs[n_carried:]
-    tile = x_ref.shape[1]
+def fwd_body(ffn, half, tile, start, n_x, n_carried, hosted, stages, *refs):
+    refs = list(refs)
+    x_refs, (g_ref, w13_hbm, w2_hbm), refs = refs[:n_x], refs[n_x:n_x + 3], refs[n_x + 3 + n_carried:]
+    own_refs, refs = refs[:len(hosted)], refs[len(hosted):]
+    (y_ref, inbox_ref), refs = refs[:2], refs[2:]
+    buf_refs, refs = refs[:len(hosted)], refs[len(hosted):]
+    w13_ref, w2_ref, w_sem, *refs = refs
+    scratch, refs = refs[:5], refs[5:]
+    exchanges = hosted_parts(hosted, stages, own_refs, buf_refs, refs)
     weights = Weights((w13_hbm, w2_hbm), (w13_ref, w2_ref), w_sem)
 
     def compute(acc):
-        def expert(e):
-            gate = gate_column(g_ref[0, start:start + tile], e)
-            pre = dot(x_ref[0], w13_ref[e])
-            one, three = pre[:, :ffn], pre[:, ffn:]
-            hidden = jnp.where(gate > 0.0, one * jax.nn.sigmoid(one) * three, 0.0).astype(BF16)
-            acc[...] += gate * dot(hidden, w2_ref[e]).astype(BF16).astype(F32)
-
-        weights.for_each(expert)
-
-    pair_sum(compute, half, 1, tile, inbox_ref, (y_ref, start), [], *scratch)
+        def experts(es):
+            gates = [gate_column(g_ref[0, start:start + tile], e) for e in es]
+            x = rows_joined(x_refs)
+            pres = [dot(x, w13_ref[e]) for e in es]
+            for gate, pre, e in zip(gates, pres, es):
+                one, three = pre[:, :ffn], pre[:, ffn:]
+                hidden = jnp.where(gate > 0.0, one * jax.nn.sigmoid(one) * three, 0.0).astype(BF16)
+                acc[...] += gate * dot(hidden, w2_ref[e]).astype(BF16).astype(F32)
+
+        weights.for_each(experts)
+
+    pair_sum(compute, half, 1, tile, inbox_ref, (y_ref, start), exchanges, *scratch)
 
 
 def pair_scratch(tile, model, half):
@@ -274,25 +317,30 @@
     return index
 
 
-def expert_fwd(x, gates, w13, w2, start, carried, collective_id):
-    n_src, tile, model = x.shape
+def expert_fwd(xs, gates, w13, w2, start, carried, hosted, stages, collective_id):
+    n_src, _, model = xs[0].shape
+    tile = sum(x.shape[1] for x in xs)
     n_tok = gates.shape[1]
     n_local, ffn = w2.shape[:2]
     half = n_src // CORES
     at = at_source(half)
     flops = 2 * n_src * tile * n_local * model * ffn * 3
-    return pl.pallas_call(
-        functools.partial(fwd_body, ffn, half, start, len(carried)),
+    outs = pl.pallas_call(
+        functools.partial(fwd_body, ffn, half, tile, start, len(xs), len(carried), [h[1:] for h in hosted], stages),
         grid=(2 * half,),
-        in_specs=[pl.BlockSpec((1, tile, model), at), pl.BlockSpec((1, n_tok, n_local), at), HBM, HBM] + [HBM] * len(carried),
-        out_specs=[HBM, HBM],
-        out_shape=[jax.ShapeDtypeStruct((half, n_tok, model), F32), jax.ShapeDtypeStruct((half, tile, model), F32)],
-        scratch_shapes=weight_scratch(w13, w2) + pair_scratch(tile, model, half),
-        input_output_aliases={4 + i: i for i in range(len(carried))},
+        in_specs=[pl.BlockSpec((1, x.shape[1], model), at) for x in xs] + [pl.BlockSpec((1, n_tok, n_local), at)]
+        + [HBM] * (2 + len(carried) + len(hosted)),
+        out_specs=[HBM] * (2 + len(hosted)),
+        out_shape=[jax.ShapeDtypeStruct((half, n_tok, model), F32), jax.ShapeDtypeStruct((half, tile, model), F32)]
+        + [jax.ShapeDtypeStruct((n_src, rows, model), BF16) for _, _, rows in hosted],
+        scratch_shapes=weight_scratch(w13, w2) + pair_scratch(tile, model, half)
+        + [ref for _, _, rows in hosted for ref in exchange_scratch(rows, model)],
+        input_output_aliases={len(xs) + 3 + i: i for i in range(len(carried))},
         compiler_params=pair_params(collective_id),
         cost_estimate=pl.CostEstimate(flops=flops, bytes_accessed=n_src * tile * model * 6, transcendentals=0),
         name='expert_fwd',
-    )(x, gates, w13, w2, *carried)[0]
+    )(*xs, gates, w13, w2, *carried, *[h[0] for h in hosted])
+    return outs[0], outs[2:]
 
 
 def bwd_body(ffn, half, start, first, n_carried, hosted, stages, x_ref, dy_ref, g_ref, w13_hbm, w2_hbm, *refs):
@@ -302,43 +350,53 @@
     buf_refs, refs = refs[:len(hosted)], refs[len(hosted):]
     w13_ref, w2_ref, w_sem, *refs = refs
     scratch, refs = refs[:5], refs[5:]
-    exchanges = [Exchange(own_refs[k], row, buf_refs[k], *refs[4 * k:4 * k + 4], stages[k]) for k, (row, _) in enumerate(hosted)]
-    tile = x_ref.shape[1]
+    exchanges = hosted_parts(hosted, stages, own_refs, buf_refs, refs)
+    tile = x_ref.shape[-2]
     weights = Weights((w13_hbm, w2_hbm), (w13_ref, w2_ref), w_sem)
 
     def compute(acc):
-        def expert(e):
-            gate = gate_column(g_ref[0, start:start + tile], e)
-            live = gate > 0.0
-            pre = dot(x_ref[0], w13_ref[e])
-            one, three = pre[:, :ffn], pre[:, ffn:]
-            sig = jax.nn.sigmoid(one)
-            act = one * sig
-            h_ref[0, :, pl.ds(pl.multiple_of(e * ffn, ffn), ffn)] = jnp.where(live, act * three, 0.0).astype(BF16)
-            d_out = (gate * dy_ref[0].astype(F32)).astype(BF16)
-            d_hid = dot_t(d_out, w2_ref[e]).astype(BF16).astype(F32)
-            d_one = jnp.where(live, d_hid * three * sig * (1.0 + one * (1.0 - sig)), 0.0).astype(BF16)
-            d_three = jnp.where(live, d_hid * act, 0.0).astype(BF16)
-            d_pre = jnp.concatenate([d_one, d_three], axis=1)
-            da_ref[0, :, pl.ds(pl.multiple_of(2 * e * ffn, 2 * ffn), 2 * ffn)] = d_pre
-            acc[...] += dot_t(d_pre, w13_ref[e]).astype(BF16).astype(F32)
-
-        weights.for_each(expert)
+        def experts(es):
+            gates = [gate_column(g_ref[0, start:start + tile], e) for e in es]
+            x = rows_joined([x_ref])
+            pres = [dot(x, w13_ref[e]) for e in es]
+            d_hids = []
+            for gate, e in zip(gates, es):
+                d_out = (gate * rows_joined([dy_ref]).astype(F32)).astype(BF16)
+                d_hids.append(dot_t(d_out, w2_ref[e]).astype(BF16).astype(F32))
+            for gate, pre, d_hid, e in zip(gates, pres, d_hids, es):
+                live = gate > 0.0
+                one, three = pre[:, :ffn], pre[:, ffn:]
+                sig = jax.nn.sigmoid(one)
+                act = one * sig
+                h_ref[0, :, pl.ds(pl.multiple_of(e * ffn, ffn), ffn)] = jnp.where(live, act * three, 0.0).astype(BF16)
+                d_one = jnp.where(live, d_hid * three * sig * (1.0 + one * (1.0 - sig)), 0.0).astype(BF16)
+                d_three = jnp.where(live, d_hid * act, 0.0).astype(BF16)
+                d_pre = jnp.concatenate([d_one, d_three], axis=1)
+                da_ref[0, :, pl.ds(pl.multiple_of(2 * e * ffn, 2 * ffn), 2 * ffn)] = d_pre
+                acc[...] += dot_t(d_pre, w13_ref[e]).astype(BF16).astype(F32)
+
+        weights.for_each(experts)
 
     pair_sum(compute, half, 1, tile, inbox_ref, (dx_ref, first), exchanges, *scratch)
 
 
 def expert_bwd(x, dy, gates, w13, w2, start, dx_rows, first, carried, hosted, stages, collective_id):
-    n_src, tile, model = x.shape
+    n_src, tile, model = x[0].shape[0], x[0].shape[-2], x[0].shape[-1]
     n_tok = gates.shape[1]
     n_local, ffn = w2.shape[:2]
     half = n_src // CORES
     at = at_source(half)
     flops = 2 * n_src * tile * n_local * model * ffn * 5
+
+    def rows_of(array, which):
+        if array.ndim == 3:
+            return pl.BlockSpec((1, tile, model), at)
+        return pl.BlockSpec((1, 1, tile, model), lambda i: (pair_source(i, half, 1)[0], which, 0, 0))
+
     outs = pl.pallas_call(
         functools.partial(bwd_body, ffn, half, start, first, len(carried), [h[1:] for h in hosted], stages),
         grid=(2 * half,),
-        in_specs=[pl.BlockSpec((1, tile, model), at)] * 2 + [pl.BlockSpec((1, n_tok, n_local), at)]
+        in_specs=[rows_of(*x), rows_of(*dy), pl.BlockSpec((1, n_tok, n_local), at)]
         + [HBM] * (2 + len(carried) + len(hosted)),
         out_specs=[
             HBM,
@@ -357,12 +415,12 @@
         compiler_params=pair_params(collective_id),
         cost_estimate=pl.CostEstimate(flops=flops, bytes_accessed=n_src * tile * model * 14, transcendentals=0),
         name='expert_bwd',
-    )(x, dy, gates, w13, w2, *carried, *[h[0] for h in hosted])
+    )(x[0], dy[0], gates, w13, w2, *carried, *[h[0] for h in hosted])
     return outs[0], outs[1], outs[2], outs[4:]
 
 
 def rows_joined(refs, column=0, columns=None):
-    parts = [ref[0, :, column:column + (columns or ref.shape[2])] for ref in refs]
+    parts = [ref[(0,) * (len(ref.shape) - 2) + (slice(None), slice(column, column + (columns or ref.shape[-1])))] for ref in refs]
     return parts[0] if len(parts) == 1 else jnp.concatenate(parts, axis=0)
 
 
@@ -390,18 +448,23 @@
 
 def weight_grads(gates, xs, dys, d_pres, hiddens):
     n_src, n_tok, n_local = gates.shape
-    model = xs[0].shape[2]
+    model = xs[0][0].shape[-1]
     ffn = hiddens[0].shape[2] // n_local
     flops = 2 * n_src * n_tok * n_local * model * ffn * 3
     at = lambda e, k: (k, 0, 0)
     at_e = lambda e, k: (k, 0, e)
     out = lambda e, k: (e, 0, 0)
 
+    def rows_of(array, which):
+        block = (1,) * (array.ndim - 2) + array.shape[-2:]
+        return pl.BlockSpec(block, at if array.ndim == 3 else (lambda e, k: (k, which, 0, 0)))
+
+
     return pl.pallas_call(
         functools.partial(grad_body, ffn, len(xs)),
         grid=(n_local, n_src),
         in_specs=[pl.BlockSpec((1, n_tok, n_local), at)]
-        + [pl.BlockSpec((1, x.shape[1], model), at) for x in list(xs) + list(dys)]
+        + [rows_of(*x) for x in list(xs) + list(dys)]
         + [pl.BlockSpec((1, d.shape[1], 2 * ffn), at_e) for d in d_pres]
         + [pl.BlockSpec((1, h.shape[1], ffn), at_e) for h in hiddens],
         out_specs=[
@@ -418,7 +481,7 @@
         compiler_params=pltpu.CompilerParams(dimension_semantics=('arbitrary', 'arbitrary'), vmem_limit_bytes=VMEM_LIMIT),
         cost_estimate=pl.CostEstimate(flops=flops, bytes_accessed=n_src * n_tok * model * 4 * n_local, transcendentals=0),
         name='weight_grads',
-    )(gates, *xs, *dys, *d_pres, *hiddens)
+    )(gates, *[x for x, _ in xs], *[dy for dy, _ in dys], *d_pres, *hiddens)
 
 
 def solution(mesh):
@@ -461,23 +524,24 @@
         def hop(rows):
             return lax.ppermute(x_src[rows], 'stage', to_next)
 
-        dys = [gather(dy_act[0, bwd[0]])]
-        xs = [gather(hop(bwd[0]))]
-
-        d_pres, hiddens = [], []
+        dys = [(gather_now(dy_act[0], 0, BWD_ROWS[0], n_dev, 5), 0)]
+        xs = [(gather(hop(bwd[0])), 0)]
+        for k in (1, 2):
+            x_dst = hop(bwd[k])
+            both = gather(jnp.stack([dy_act[0, bwd[k]], x_dst]))
+            dys.append((both, 0))
+            xs.append((both, 1))
+        x_half = [hop(fwd[k]) for k in range(2)]
+        pieces = [(x_half[k], first, X_ROWS) for k in range(2) for first in range(0, FWD_ROWS[k], X_ROWS)]
+        hosts = {'bwd_1': pieces[:1], 'bwd_2': pieces[1:3], 'fwd_0': pieces[3:]}
+
+        x_fwd, d_pres, hiddens = [], [], []
         dx_parts = []
         for k in range(3):
-            if k < 2:
-                rows = BWD_ROWS[k + 1]
-                hosted = ((dy_act[0], bwd[k + 1].start, rows), (hop(bwd[k + 1]), 0, rows))
-            else:
-                hosted = ((hop(fwd[1]), 0, FWD_ROWS[1]),)
             dx_part, d_pre, hidden, arrived = expert_bwd(
                 xs[k], dys[k], gates, w13, w2, bwd[k].start, dx_rows[k // 2], BWD_ROWS[0] if k == 1 else 0,
-                (dx_part,) if k == 1 else (), hosted, STAGES[k], k)
-            if k < 2:
-                dys.append(arrived[0])
-                xs.append(arrived[1])
+                (dx_part,) if k == 1 else (), hosts.get(f'bwd_{k}', ()), STAGES.get(f'bwd_{k}'), k)
+            x_fwd += arrived
             d_pres.append(d_pre)
             hiddens.append(hidden)
             if k > 0:
@@ -485,11 +549,12 @@
                 dx_parts.append(lax.ppermute(dx_dst, 'stage', to_prev))
         dx_out = jnp.concatenate(dx_parts, axis=0)
 
-        x_dst = hop(fwd[0])
-        x_fwd = gather(x_dst), arrived[0]
         y_part = ()
         for k in range(2):
-            y_part = (expert_fwd(x_fwd[k], gates, w13, w2, fwd[k].start, y_part, 3 + k),)
+            out, arrived = expert_fwd(
+                x_fwd[2 * k:2 * k + 2], gates, w13, w2, fwd[k].start, y_part, hosts.get(f'fwd_{k}', ()), STAGES.get(f'fwd_{k}'), 3 + k)
+            y_part = (out,)
+            x_fwd += arrived
         y_out = reduce_rows(y_part[0])
 
         g_one, g_three, g_two = weight_grads(gates, xs, dys, d_pres, hiddens)

time: 1270 us -> 1270 us (level)
  Pallas kernels: 980 us -> 966 us
    pallas_call x3, Pallas kernels: 508 us -> 433 us  [expert_bwd(): pl.pallas_call(functools.partial(bwd_body, ffn, half, start, first, len(c...]
    unnamed x9, waiting for transfers between devices: 104 us -> 36 us
    ppermute x5, waiting for transfers between devices: 23.2 us -> 90 us  [hop(): return lax.ppermute(x_src[rows], 'stage', to_next)]
    pallas_call x2 -> x3, Pallas kernels: 238 us -> 299 us  [the longest x2 238 us: expert_fwd(): pl.pallas_call(functools.partial(fwd_body, ffn, half, tile, start, len(xs...]
  transfers between devices with their start and end apart: 15 -> 15, of which waited for: 4 -> 5; matrix products, arithmetic and copies ran while one was open for 3% -> 3% of each run, Pallas kernels for 77% -> 77%
where the time goes in v7:
time: 1270 us; the launch traced here: 1260 us
  Pallas kernels  966 us (76%)
  waiting for transfers between devices  216 us (17%)
  other arithmetic  37 us (3%)
  starting transfers between devices  16.5 us (1%)
  between operations  14.5 us (1%)
    pallas_call x3, Pallas kernels, expert_bwd(): pl.pallas_call(functools.partial(bwd_body, ffn, half, start, first, len(c...  433 us
    pallas_call x2, Pallas kernels, expert_fwd(): pl.pallas_call(functools.partial(fwd_body, ffn, half, tile, start, len(xs...  238 us
    pallas_call x1, Pallas kernels, weight_grads(): pl.pallas_call(functools.partial(grad_body, ffn, len(xs)), grid=(n_local,...  234 us
    ppermute x5, waiting for transfers between devices, hop(): return lax.ppermute(x_src[rows], 'stage', to_next)  90 us
    ppermute x1, waiting for transfers between devices, moe_body(): gate_dst = lax.ppermute(gate_src, 'stage', to_next)  89.8 us
    pallas_call x1, Pallas kernels, gather_now(): pl.pallas_call(functools.partial(gather_body, first), in_specs=[pl.BlockS...  61.1 us
    unnamed x9, waiting for transfers between devices  36 us
  transfers between devices with their start and end apart: 15, of which 5 were waited for; matrix products, arithmetic and copies ran while one was open for 3% of the time, Pallas kernels for 77%

profile of v7, /device:TPU:0, one launch (start us, length us, event | category | flops | bytes accessed | tf_op | source)
XLA Modules:
  0.0 1261.3 jit_solution(14776864002796665277)
XLA Ops:
  7.2 2.3 slice_bitcast_fusion.2
  9.6 3.3 collective-permute-start
  13.2 34.1 %collective-permute-done = bf16[384,2048]{1,0:T(8,128)(2,1)S(1)} collective-permute-done((bf16[384,2048]{1,0:T(8,128)(2,1)S(1)}, bf16[384,2048]{1,0:T(8,128)(2,1)S(1)}, u32[]{:S(2)}, u32[]{:S(2)}) %collective-permute-start) | collective-permute-done | bytes 1572896 | tf_op jit(solution)/shard_map/ppermute | solution.py:525
  47.3 1.9 pad_maximum_fusion.1
  52.4 22.7 %collective-permute-done.5 = bf16[256,2048]{1,0:T(8,128)(2,1)} collective-permute-done((bf16[256,2048]{1,0:T(8,128)(2,1)S(1)}, bf16[256,2048]{1,0:T(8,128)(2,1)}, u32[]{:S(2)}, u32[]{:S(2)}) %collective-permute-start.5) | collective-permute-done | bytes 1048608 | tf_op jit(solution)/shard_map/ppermute | solution.py:525
  76.6 33.2 %collective-permute-done.4 = bf16[384,2048]{1,0:T(8,128)(2,1)S(1)} collective-permute-done((bf16[384,2048]{1,0:T(8,128)(2,1)S(1)}, bf16[384,2048]{1,0:T(8,128)(2,1)S(1)}, u32[]{:S(2)}, u32[]{:S(2)}) %collective-permute-start.4) | collective-permute-done | bytes 1572896 | tf_op jit(solution)/shard_map/ppermute | solution.py:525
  109.9 1.9 pad_maximum_fusion.2
  111.9 4.0 slice_bitcast_fusion
  119.3 89.8 %collective-permute-done.1 = f32[8,4,1024]{2,0,1:T(8,128)S(1)} collective-permute-done((f32[8,4,1024]{2,0,1:T(8,128)S(1)}, f32[8,4,1024]{2,0,1:T(8,128)S(1)}, u32[]{:S(2)}, u32[]{:S(2)}) %collective-permute-start.1) | collective-permute-done | bytes 131104 | tf_op jit(solution)/shard_map/ppermute | solution.py:511
  209.9 3.4 all-to-all-start
  213.3 14.2 %pad_maximum_fusion.w13_hbm.refs_3_ = bf16[4,2048,1024]{2,1,0:T(8,128)(2,1)} fusion(bf16[4,2048,512]{2,1,0:T(8,128)(2,1)} %bitcast.36, bf16[4,2048,512]{2,1,0:T(8,128)(2,1)} %bitcast.37), kind=kLoop, calls=%fused_computation | loop fusion | flops 33554432 | bytes 33554432 | tf_op jit(solution)/shard_map/concatenate | solution.py:514
  227.5 2.7 copy.26
  230.2 167.5 %expert_bwd.3 = (f32[4,384,2048]{2,1,0:T(8,128)}, bf16[8,384,4096]{2,1,0:T(8,128)(2,1)}, bf16[8,384,2048]{2,1,0:T(8,128)(2,1)}, f32[4,384,2048]{2,1,0:T(8,128)},...) custom-call(bf16[8,2,384,2048]{3,2,1,0:T(8,128)(2,1)} %bitcast.49, bf16[8,2,384,2048]{3,2,1,0:T(8,128)(2,1)} %bitcast.50, ...), custom_call_target="tpu_custom_call" | custom-call | flops 128849018880 | bytes 88080384 | tf_op jit(solution)/shard_map/expert_bwd/pallas_call | solution.py:396
  398.3 61.1 %gather_now.1.dy_ref.refs_3_ = bf16[8,256,2048]{2,1,0:T(8,128)(2,1)} custom-call(bf16[1024,2048]{1,0:T(8,128)(2,1)} %bitcast.35), custom_call_target="tpu_custom_call" | custom-call | tf_op jit(solution)/shard_map/gather_now/pallas_call | solution.py:224
  459.4 109.5 %expert_bwd.4 = (f32[4,640,2048]{2,1,0:T(8,128)}, bf16[8,256,4096]{2,1,0:T(8,128)(2,1)}, bf16[8,256,2048]{2,1,0:T(8,128)(2,1)}, f32[4,256,2048]{2,1,0:T(8,128)}) custom-call(bf16[8,256,2048]{2,1,0:T(8,128)(2,1)} %bitcast.62, bf16[8,256,2048]{2,1,0:T(8,128)(2,1)} %gather_now.1.dy_ref.refs_3_, f32[8,1024,4]{2,1,0:T(8,128)} %bitcast.39, ...), custom_call_target="tpu_custom_call" | custom-call | flops 85899345920 | bytes 58720256 | tf_op jit(solution)/shard_map/expert_bwd/pallas_call | solution.py:396
  568.9 156.0 %expert_bwd.5 = (f32[4,640,2048]{2,1,0:T(8,128)}, bf16[8,384,4096]{2,1,0:T(8,128)(2,1)}, bf16[8,384,2048]{2,1,0:T(8,128)(2,1)}, f32[4,384,2048]{2,1,0:T(8,128)}, bf16[8,256,2048]{2,1,0:T(8,128)(2,1)}) custom-call(bf16[8,2,384,2048]{3,2,1,0:T(8,128)(2,1)} %bitcast.53, bf16[8,2,384,2048]{3,2,1,0:T(8,128)(2,1)} %bitcast.54, ...), custom_call_target="tpu_custom_call", output_to_operand_aliasing={{0}: (5, {})} | custom-call | flops 128849018880 | bytes 88080384 | tf_op jit(solution)/shard_map/expert_bwd/pallas_call | solution.py:396
  725.0 119.8 %expert_fwd.2 = (f32[4,1024,2048]{2,1,0:T(8,128)}, f32[4,512,2048]{2,1,0:T(8,128)}, bf16[8,256,2048]{2,1,0:T(8,128)(2,1)}) custom-call(bf16[8,256,2048]{2,1,0:T(8,128)(2,1)} %get-tuple-element.25.refs_0_, bf16[8,256,2048]{2,1,0:T(8,128)(2,1)} %get-tuple-element.26.refs_1_, f32[8,1024,4]{2,1,0:T(8,128)} %bitcast.41, ...), custom_call_target="tpu_custom_call" | custom-call | flops 103079215104 | bytes 50331648 | tf_op jit(solution)/shard_map/expert_fwd/pallas_call | solution.py:328
  844.8 118.6 %expert_fwd.3 = (f32[4,1024,2048]{2,1,0:T(8,128)}, f32[4,512,2048]{2,1,0:T(8,128)}) custom-call(bf16[8,256,2048]{2,1,0:T(8,128)(2,1)} %get-tuple-element.23.refs_0_, bf16[8,256,2048]{2,1,0:T(8,128)(2,1)} %get-tuple-element.27.refs_1_, f32[8,1024,4]{2,1,0:T(8,128)} %bitcast.42, ...), custom_call_target="tpu_custom_call", output_to_operand_aliasing={{0}: (5, {})} | custom-call | flops 103079215104 | bytes 50331648 | tf_op jit(solution)/shard_map/expert_fwd/pallas_call | solution.py:328
  963.4 3.3 convert_bitcast_fusion.1
  967.9 4.5 convert_bitcast_fusion
  973.8 233.5 %weight_grads.1 = (bf16[4,2048,512]{2,1,0:T(8,128)(2,1)}, bf16[4,2048,512]{2,1,0:T(8,128)(2,1)}, bf16[4,512,2048]{2,1,0:T(8,128)(2,1)}) custom-call(f32[8,1024,4]{2,1,0:T(8,128)} %bitcast.43, bf16[8,256,2048]{2,1,0:T(8,128)(2,1)} %bitcast.63, bf16[8,2,384,2048]{3,2,1,0:T(8,128)(2,1)} %bitcast.55, bf16[8,2,384,2048]{3,2,1,0:T(8,128)(2,1)} %bitcast.51, ...), custom_call_target="tpu_custom_call" | custom-call | flops 206158430208 | bytes 268435456 | tf_op jit(solution)/shard_map/weight_grads/pallas_call | solution.py:463
  1207.4 5.0 maximum_bitcast_fusion
  1212.4 35.8 %reduce-scatter.10.cloned.1.call-done = f32[1,1024,2048]{2,1,0:T(8,128)} async-done(((f32[4,1024,2048]{2,1,0:T(8,128)}), f32[1,1024,2048]{2,1,0:T(8,128)}) %reduce-scatter.10.cloned.1.call-update) | async-done | bytes 8388624
  1248.2 6.0 convert_element_type.16
  (41 shorter events, 12.6 us)
Async XLA Ops:
  7.2 223.0 %all-gather.7.cloned.1.call-start = ((), (), s32[]{:S(2)}) async-start(), calls=%async_computation.4 | async-start | bytes 28311552 | tf_op jit(solution)/shard_map/all_gather | solution.py:503
  7.2 5.7 copy-start
  9.6 37.7 %collective-permute-start = (bf16[384,2048]{1,0:T(8,128)(2,1)S(1)}, bf16[384,2048]{1,0:T(8,128)(2,1)S(1)}, u32[]{:S(2)}, u32[]{:S(2)}) collective-permute-start(bf16[384,2048]{1,0:T(8,128)(2,1)S(1)} %get-tuple-element.44), channel_id=1, source_target_pairs={{0,8},{8,0},{1,9},{9,1},{2,10},{10,2},{3,11},{11,3},{4,12},{12,4},... | collective-permute-start | bytes 4718600 | tf_op jit(solution)/shard_map/ppermute | solution.py:525
  49.2 410.1 %all-gather.11.cloned.1.call-start = ((), (), s32[]{:S(2)}) async-start(), calls=%async_computation.6 | async-start | bytes 9437184 | tf_op jit(solution)/shard_map/all_gather | solution.py:503
  50.6 24.5 %collective-permute-start.5 = (bf16[256,2048]{1,0:T(8,128)(2,1)S(1)}, bf16[256,2048]{1,0:T(8,128)(2,1)}, u32[]{:S(2)}, u32[]{:S(2)}) collective-permute-start(bf16[256,2048]{1,0:T(8,128)(2,1)S(1)} %slice_bitcast_fusion.4), channel_id=1, source_target_pairs={{0,8},{8,0},{1,9},{9,1},{2,10},{10,2},{3,11},{11,3},{4,12},{12,4},... | collective-permute-start | bytes 3145736 | tf_op jit(solution)/shard_map/ppermute | solution.py:525
  75.1 493.8 %all-gather.9.cloned.1.call-start = ((), (), s32[]{:S(2)}) async-start(), calls=%async_computation.5 | async-start | bytes 28311552 | tf_op jit(solution)/shard_map/all_gather | solution.py:503
  75.1 34.7 %collective-permute-start.4 = (bf16[384,2048]{1,0:T(8,128)(2,1)S(1)}, bf16[384,2048]{1,0:T(8,128)(2,1)S(1)}, u32[]{:S(2)}, u32[]{:S(2)}) collective-permute-start(bf16[384,2048]{1,0:T(8,128)(2,1)S(1)} %get-tuple-element.43), channel_id=1, source_target_pairs={{0,8},{8,0},{1,9},{9,1},{2,10},{10,2},{3,11},{11,3},{4,12},{12,4},... | collective-permute-start | bytes 4718600 | tf_op jit(solution)/shard_map/ppermute | solution.py:525
  111.8 6.1 copy-start.1
  111.8 6.0 copy-start.2
  115.9 114.3 %collective-permute-start.3 = (bf16[512,2048]{1,0:T(8,128)(2,1)}, bf16[512,2048]{1,0:T(8,128)(2,1)}, u32[]{:S(2)}, u32[]{:S(2)}) collective-permute-start(bf16[512,2048]{1,0:T(8,128)(2,1)} %get-tuple-element.45), channel_id=1, source_target_pairs={{0,8},{8,0},{1,9},{9,1},{2,10},{10,2},{3,11},{11,3},{4,12},{12,4},... | collective-permute-start | bytes 6291464 | tf_op jit(solution)/shard_map/ppermute | solution.py:525
  117.0 113.2 %collective-permute-start.2 = (bf16[512,2048]{1,0:T(8,128)(2,1)S(1)}, bf16[512,2048]{1,0:T(8,128)(2,1)}, u32[]{:S(2)}, u32[]{:S(2)}) collective-permute-start(bf16[512,2048]{1,0:T(8,128)(2,1)S(1)} %get-tuple-element.46), channel_id=1, source_target_pairs={{0,8},{8,0},{1,9},{9,1},{2,10},{10,2},{3,11},{11,3},{4,12},{12,4},... | collective-permute-start | bytes 6291464 | tf_op jit(solution)/shard_map/ppermute | solution.py:525
  118.1 91.0 %collective-permute-start.1 = (f32[8,4,1024]{2,0,1:T(8,128)S(1)}, f32[8,4,1024]{2,0,1:T(8,128)S(1)}, u32[]{:S(2)}, u32[]{:S(2)}) collective-permute-start(f32[8,4,1024]{2,0,1:T(8,128)S(1)} %copy.24), channel_id=1, source_target_pairs={{0,8},{8,0},{1,9},{9,1},{2,10},{10,2},{3,11},{11,3},{4,12},{12,4},... | collective-permute-start | bytes 393224 | tf_op jit(solution)/shard_map/ppermute | solution.py:511
  209.9 17.6 %all-to-all-start = ((f32[8,4,1024]{2,1,0:T(4,128)}), f32[8,4,1024]{2,1,0:T(4,128)S(1)}, u32[]{:S(2)}, u32[]{:S(2)}) async-start(f32[8,4,1024]{2,1,0:T(4,128)} %copy.25), calls=%async_computation | async-start | bytes 262144 | tf_op jit(solution)/shard_map/all_to_all | solution.py:512
  213.3 750.2 %reduce-scatter.14.cloned.1.call-start = ((), (), s32[]{:S(2)}) async-start(), calls=%async_computation.9 | async-start | bytes 15728640
  397.8 570.1 %reduce-scatter.12.cloned.1.call-start = ((), (), s32[]{:S(2)}) async-start(), calls=%async_computation.8 | async-start | bytes 26214400
  725.0 523.2 %reduce-scatter.10.cloned.1.call-start = ((), (), s32[]{:S(2)}) async-start(), calls=%async_computation.7 | async-start | bytes 41943040
  966.7 240.6 %collective-permute-start.7 = (bf16[384,2048]{1,0:T(8,128)(2,1)}, bf16[384,2048]{1,0:T(8,128)(2,1)}, u32[]{:S(2)}, u32[]{:S(2)}) collective-permute-start(bf16[384,2048]{1,0:T(8,128)(2,1)} %convert_bitcast_fusion.1), channel_id=1, source_target_pairs={{8,0},{0,8},{9,1},{1,9},{10,2},{2,10},{11,3},{3,11},{12,4},{4,12},... | collective-permute-start | bytes 4718600 | tf_op jit(solution)/shard_map/ppermute | solution.py:549
  972.4 235.0 %collective-permute-start.6 = (bf16[640,2048]{1,0:T(8,128)(2,1)}, bf16[640,2048]{1,0:T(8,128)(2,1)}, u32[]{:S(2)}, u32[]{:S(2)}) collective-permute-start(bf16[640,2048]{1,0:T(8,128)(2,1)} %convert_bitcast_fusion), channel_id=1, source_target_pairs={{8,0},{0,8},{9,1},{1,9},{10,2},{2,10},{11,3},{3,11},{12,4},{4,12},... | collective-permute-start | bytes 7864328 | tf_op jit(solution)/shard_map/ppermute | solution.py:549
Sparse Core Ops, SparseCore 0:
  49.4 122.6 all-gather.6
  173.9 51.9 all-gather.10
  228.3 183.9 all-gather.8
  415.2 133.5 reduce-scatter.13
  725.1 215.9 reduce-scatter.11
  963.5 284.6 reduce-scatter.9

commit v8 on v7

--- a/solution.py
+++ b/solution.py
@@ -12,12 +12,13 @@
 BF16 = jnp.bfloat16
 BWD_ROWS = (256, 384, 384)
 FWD_ROWS = (512, 512)
-X_ROWS = 256
-STAGES = {'bwd_1': ((0, 2, 4, 6),), 'bwd_2': ((0, 2, 4, 6), (0, 3, 5, 7)), 'fwd_0': ((0, 2, 4, 6),)}
+X_ROWS = (256, 512, 256)
+STAGES = (0, 2, 4, 6), (0, 3, 5, 7), (0, 2, 4, 6)
 VMEM_LIMIT = 65400 * 1024
 N_ACC = 3
 CORES = 2
 UNROLL = 2
+BLOCK = 256
 MESH = pl.DeviceIdType.MESH
 
 
@@ -104,15 +105,15 @@
 
     acc = acc_ref.at[lax.rem(step, N_ACC)]
 
-    @pl.when(step < half)
-    def _():
-        acc[...] = jnp.zeros_like(acc)
-
     @pl.when(step >= half)
     def _():
         fetch(step - half).wait()
 
-    compute(acc)
+    def add(expert, rows):
+        fresh = (expert == 0) & (step < half)
+        acc[...] = jnp.where(fresh, 0.0, acc[...]) + rows
+
+    compute(add)
 
     @pl.when(step < half)
     def _():
@@ -277,7 +278,7 @@
     exchanges = hosted_parts(hosted, stages, own_refs, buf_refs, refs)
     weights = Weights((w13_hbm, w2_hbm), (w13_ref, w2_ref), w_sem)
 
-    def compute(acc):
+    def compute(add):
         def experts(es):
             gates = [gate_column(g_ref[0, start:start + tile], e) for e in es]
             x = rows_joined(x_refs)
@@ -285,7 +286,7 @@
             for gate, pre, e in zip(gates, pres, es):
                 one, three = pre[:, :ffn], pre[:, ffn:]
                 hidden = jnp.where(gate > 0.0, one * jax.nn.sigmoid(one) * three, 0.0).astype(BF16)
-                acc[...] += gate * dot(hidden, w2_ref[e]).astype(BF16).astype(F32)
+                add(e, gate * dot(hidden, w2_ref[e]).astype(BF16).astype(F32))
 
         weights.for_each(experts)
 
@@ -318,17 +319,21 @@
 
 
 def expert_fwd(xs, gates, w13, w2, start, carried, hosted, stages, collective_id):
-    n_src, _, model = xs[0].shape
-    tile = sum(x.shape[1] for x in xs)
+    n_src, _, model = xs[0][0].shape
+    tile = BLOCK * len(xs)
     n_tok = gates.shape[1]
     n_local, ffn = w2.shape[:2]
     half = n_src // CORES
     at = at_source(half)
     flops = 2 * n_src * tile * n_local * model * ffn * 3
+
+    def rows_of(block):
+        return pl.BlockSpec((1, BLOCK, model), lambda i: (pair_source(i, half, 1)[0], block, 0))
+
     outs = pl.pallas_call(
         functools.partial(fwd_body, ffn, half, tile, start, len(xs), len(carried), [h[1:] for h in hosted], stages),
         grid=(2 * half,),
-        in_specs=[pl.BlockSpec((1, x.shape[1], model), at) for x in xs] + [pl.BlockSpec((1, n_tok, n_local), at)]
+        in_specs=[rows_of(block) for _, block in xs] + [pl.BlockSpec((1, n_tok, n_local), at)]
         + [HBM] * (2 + len(carried) + len(hosted)),
         out_specs=[HBM] * (2 + len(hosted)),
         out_shape=[jax.ShapeDtypeStruct((half, n_tok, model), F32), jax.ShapeDtypeStruct((half, tile, model), F32)]
@@ -339,7 +344,7 @@
         compiler_params=pair_params(collective_id),
         cost_estimate=pl.CostEstimate(flops=flops, bytes_accessed=n_src * tile * model * 6, transcendentals=0),
         name='expert_fwd',
-    )(*xs, gates, w13, w2, *carried, *[h[0] for h in hosted])
+    )(*[x for x, _ in xs], gates, w13, w2, *carried, *[h[0] for h in hosted])
     return outs[0], outs[2:]
 
 
@@ -354,7 +359,7 @@
     tile = x_ref.shape[-2]
     weights = Weights((w13_hbm, w2_hbm), (w13_ref, w2_ref), w_sem)
 
-    def compute(acc):
+    def compute(add):
         def experts(es):
             gates = [gate_column(g_ref[0, start:start + tile], e) for e in es]
             x = rows_joined([x_ref])
@@ -373,7 +378,7 @@
                 d_three = jnp.where(live, d_hid * act, 0.0).astype(BF16)
                 d_pre = jnp.concatenate([d_one, d_three], axis=1)
                 da_ref[0, :, pl.ds(pl.multiple_of(2 * e * ffn, 2 * ffn), 2 * ffn)] = d_pre
-                acc[...] += dot_t(d_pre, w13_ref[e]).astype(BF16).astype(F32)
+                add(e, dot_t(d_pre, w13_ref[e]).astype(BF16).astype(F32))
 
         weights.for_each(experts)
 
@@ -531,33 +536,36 @@
             both = gather(jnp.stack([dy_act[0, bwd[k]], x_dst]))
             dys.append((both, 0))
             xs.append((both, 1))
-        x_half = [hop(fwd[k]) for k in range(2)]
-        pieces = [(x_half[k], first, X_ROWS) for k in range(2) for first in range(0, FWD_ROWS[k], X_ROWS)]
-        hosts = {'bwd_1': pieces[:1], 'bwd_2': pieces[1:3], 'fwd_0': pieces[3:]}
+        cut = sum(X_ROWS[:2])
+        x_lo, x_hi = hop(slice(0, cut)), hop(slice(cut, n_tok))
+        pieces = (x_lo, 0, X_ROWS[0]), (x_lo, X_ROWS[0], X_ROWS[1]), (x_hi, 0, X_ROWS[2])
+
+        def blocks(arrived):
+            return [(x, block) for x in arrived for block in range(x.shape[1] // BLOCK)]
 
         x_fwd, d_pres, hiddens = [], [], []
         dx_parts = []
         for k in range(3):
             dx_part, d_pre, hidden, arrived = expert_bwd(
                 xs[k], dys[k], gates, w13, w2, bwd[k].start, dx_rows[k // 2], BWD_ROWS[0] if k == 1 else 0,
-                (dx_part,) if k == 1 else (), hosts.get(f'bwd_{k}', ()), STAGES.get(f'bwd_{k}'), k)
-            x_fwd += arrived
+                (dx_part,) if k == 1 else (), pieces[k - 1:k] if k else (), STAGES[k - 1:k], k)
+            x_fwd += blocks(arrived)
             d_pres.append(d_pre)
             hiddens.append(hidden)
             if k > 0:
                 dx_dst = reduce_rows(dx_part)
                 dx_parts.append(lax.ppermute(dx_dst, 'stage', to_prev))
-        dx_out = jnp.concatenate(dx_parts, axis=0)
+        dx_out = jnp.concatenate(dx_parts, axis=0)[None]
 
         y_part = ()
         for k in range(2):
             out, arrived = expert_fwd(
-                x_fwd[2 * k:2 * k + 2], gates, w13, w2, fwd[k].start, y_part, hosts.get(f'fwd_{k}', ()), STAGES.get(f'fwd_{k}'), 3 + k)
+                x_fwd[2 * k:2 * k + 2], gates, w13, w2, fwd[k].start, y_part, () if k else pieces[2:], STAGES[2:], 3 + k)
             y_part = (out,)
-            x_fwd += arrived
+            x_fwd += blocks(arrived)
         y_out = reduce_rows(y_part[0])
 
         g_one, g_three, g_two = weight_grads(gates, xs, dys, d_pres, hiddens)
-        return y_out[None], dx_out[None], g_one[None], g_three[None], g_two[None]
+        return y_out[None], dx_out, g_one[None], g_three[None], g_two[None]
 
     return jax.shard_map(moe_body, mesh=mesh, in_specs=(tok_spec, tok_spec, tok_spec, w_spec, w_spec, w_spec, tok_spec), out_specs=(tok_spec, tok_spec, w_spec, w_spec, w_spec), check_vma=False)

time: 1270 us -> 1270 us (level)
    ppermute x5, waiting for transfers between devices: 90 us -> 114 us  [hop(): return lax.ppermute(x_src[rows], 'stage', to_next)]
    ppermute x1, waiting for transfers between devices: 89.8 us -> 68.2 us  [moe_body(): gate_dst = lax.ppermute(gate_src, 'stage', to_next)]
  transfers between devices with their start and end apart: 15 -> 15, of which waited for: 5 -> 6; matrix products, arithmetic and copies ran while one was open for 3% -> 3% of each run, Pallas kernels for 77% -> 76%
where the time goes in v8:
time: 1270 us; the launch traced here: 1260 us
  Pallas kernels  957 us (75%)
  waiting for transfers between devices  220 us (17%)
  other arithmetic  37.6 us (3%)
  starting transfers between devices  16 us (1%)
  between operations  14.5 us (1%)
  local copies, waits for them, and re-layouts  13.1 us (1%)
    pallas_call x3, Pallas kernels, expert_bwd(): pl.pallas_call(functools.partial(bwd_body, ffn, half, start, first, len(c...  422 us
    pallas_call x2, Pallas kernels, expert_fwd(): pl.pallas_call(functools.partial(fwd_body, ffn, half, tile, start, len(xs...  236 us
    pallas_call x1, Pallas kernels, weight_grads(): pl.pallas_call(functools.partial(grad_body, ffn, len(xs)), grid=(n_local,...  233 us
    ppermute x5, waiting for transfers between devices, hop(): return lax.ppermute(x_src[rows], 'stage', to_next)  114 us
    ppermute x1, waiting for transfers between devices, moe_body(): gate_dst = lax.ppermute(gate_src, 'stage', to_next)  68.2 us
    pallas_call x1, Pallas kernels, gather_now(): pl.pallas_call(functools.partial(gather_body, first), in_specs=[pl.BlockS...  65.9 us
    unnamed x9, waiting for transfers between devices  37.6 us
  transfers between devices with their start and end apart: 15, of which 6 were waited for; matrix products, arithmetic and copies ran while one was open for 3% of the time, Pallas kernels for 76%

profile of v8, /device:TPU:0, one launch (start us, length us, event | category | flops | bytes accessed | tf_op | source)
XLA Modules:
  0.0 1257.6 jit_solution(13063415276123837012)
XLA Ops:
  7.2 2.3 slice_bitcast_fusion.1
  9.6 3.3 collective-permute-start
  13.2 34.1 %collective-permute-done = bf16[384,2048]{1,0:T(8,128)(2,1)S(1)} collective-permute-done((bf16[384,2048]{1,0:T(8,128)(2,1)S(1)}, bf16[384,2048]{1,0:T(8,128)(2,1)S(1)}, u32[]{:S(2)}, u32[]{:S(2)}) %collective-permute-start) | collective-permute-done | bytes 1572896 | tf_op jit(solution)/shard_map/ppermute | solution.py:530
  49.3 2.7 slice_bitcast_fusion.3
  53.7 22.7 %collective-permute-done.4 = bf16[256,2048]{1,0:T(8,128)(2,1)} collective-permute-done((bf16[256,2048]{1,0:T(8,128)(2,1)S(1)}, bf16[256,2048]{1,0:T(8,128)(2,1)}, u32[]{:S(2)}, u32[]{:S(2)}) %collective-permute-start.4) | collective-permute-done | bytes 1048608 | tf_op jit(solution)/shard_map/ppermute | solution.py:530
  78.0 33.2 %collective-permute-done.3 = bf16[384,2048]{1,0:T(8,128)(2,1)S(1)} collective-permute-done((bf16[384,2048]{1,0:T(8,128)(2,1)S(1)}, bf16[384,2048]{1,0:T(8,128)(2,1)S(1)}, u32[]{:S(2)}, u32[]{:S(2)}) %collective-permute-start.3) | collective-permute-done | bytes 1572896 | tf_op jit(solution)/shard_map/ppermute | solution.py:530
  113.2 2.1 slice_bitcast_fusion
  117.7 68.2 %collective-permute-done.1 = f32[8,4,1024]{2,0,1:T(8,128)S(1)} collective-permute-done((f32[8,4,1024]{2,0,1:T(8,128)S(1)}, f32[8,4,1024]{2,0,1:T(8,128)S(1)}, u32[]{:S(2)}, u32[]{:S(2)}) %collective-permute-start.1) | collective-permute-done | bytes 131104 | tf_op jit(solution)/shard_map/ppermute | solution.py:516
  186.6 3.4 all-to-all-start
  190.0 14.3 %pad_maximum_fusion.w13_hbm.refs_3_ = bf16[4,2048,1024]{2,1,0:T(8,128)(2,1)} fusion(bf16[4,2048,512]{2,1,0:T(8,128)(2,1)} %bitcast.36, bf16[4,2048,512]{2,1,0:T(8,128)(2,1)} %bitcast.37), kind=kLoop, calls=%fused_computation | loop fusion | flops 33554432 | bytes 33554432 | tf_op jit(solution)/shard_map/concatenate | solution.py:519
  204.3 2.7 copy.26
  207.0 155.9 %expert_bwd.3 = (f32[4,384,2048]{2,1,0:T(8,128)}, bf16[8,384,4096]{2,1,0:T(8,128)(2,1)}, bf16[8,384,2048]{2,1,0:T(8,128)(2,1)}, f32[4,384,2048]{2,1,0:T(8,128)}, bf16[8,512,2048]{2,1,0:T(8,128)(2,1)}) custom-call(bf16[8,2,384,2048]{3,2,1,0:T(8,128)(2,1)} %bitcast.49, bf16[8,2,384,2048]{3,2,1,0:T(8,128)(2,1)} %bitcast.50, f32[8,1024,4]{2,1,0:T(8,128)} %bitcast.38, ...), custom_call_target="tpu_custom_call" | custom-call | flops 128849018880 | bytes 88080384 | tf_op jit(solution)/shard_map/expert_bwd/pallas_call | solution.py:401
  363.2 65.9 %gather_now.1.dy_ref.refs_3_ = bf16[8,256,2048]{2,1,0:T(8,128)(2,1)} custom-call(bf16[1024,2048]{1,0:T(8,128)(2,1)} %bitcast.35), custom_call_target="tpu_custom_call" | custom-call | tf_op jit(solution)/shard_map/gather_now/pallas_call | solution.py:225
  429.2 109.2 %expert_bwd.4 = (f32[4,640,2048]{2,1,0:T(8,128)}, bf16[8,256,4096]{2,1,0:T(8,128)(2,1)}, bf16[8,256,2048]{2,1,0:T(8,128)(2,1)}, f32[4,256,2048]{2,1,0:T(8,128)}) custom-call(bf16[8,256,2048]{2,1,0:T(8,128)(2,1)} %bitcast.62, bf16[8,256,2048]{2,1,0:T(8,128)(2,1)} %gather_now.1.dy_ref.refs_3_, f32[8,1024,4]{2,1,0:T(8,128)} %bitcast.39, ...), custom_call_target="tpu_custom_call" | custom-call | flops 85899345920 | bytes 58720256 | tf_op jit(solution)/shard_map/expert_bwd/pallas_call | solution.py:401
  538.5 156.4 %expert_bwd.5 = (f32[4,640,2048]{2,1,0:T(8,128)}, bf16[8,384,4096]{2,1,0:T(8,128)(2,1)}, bf16[8,384,2048]{2,1,0:T(8,128)(2,1)}, f32[4,384,2048]{2,1,0:T(8,128)}, bf16[8,256,2048]{2,1,0:T(8,128)(2,1)}) custom-call(bf16[8,2,384,2048]{3,2,1,0:T(8,128)(2,1)} %bitcast.53, bf16[8,2,384,2048]{3,2,1,0:T(8,128)(2,1)} %bitcast.54, ...), custom_call_target="tpu_custom_call", output_to_operand_aliasing={{0}: (5, {})} | custom-call | flops 128849018880 | bytes 88080384 | tf_op jit(solution)/shard_map/expert_bwd/pallas_call | solution.py:401
  697.9 23.8 %collective-permute-done.5.refs_5_ = bf16[256,2048]{1,0:T(8,128)(2,1)S(1)} collective-permute-done((bf16[256,2048]{1,0:T(8,128)(2,1)S(1)}, bf16[256,2048]{1,0:T(8,128)(2,1)S(1)}, u32[]{:S(2)}, u32[]{:S(2)}) %collective-permute-start.5) | collective-permute-done | bytes 1048608 | tf_op jit(solution)/shard_map/ppermute | solution.py:530
  722.6 118.6 %expert_fwd.2 = (f32[4,1024,2048]{2,1,0:T(8,128)}, f32[4,512,2048]{2,1,0:T(8,128)}, bf16[8,256,2048]{2,1,0:T(8,128)(2,1)}) custom-call(bf16[8,256,2048]{2,1,0:T(8,128)(2,1)} %get-tuple-element.24.refs_0_, bf16[8,512,2048]{2,1,0:T(8,128)(2,1)} %get-tuple-element.22.refs_1_.refs_0_, f32[8,1024,4]{2,1,0:T(8,128)} %bitcast.41, ...), custom_call_target="tpu_custom_call" | custom-call | flops 103079215104 | bytes 50331648 | tf_op jit(solution)/shard_map/expert_fwd/pallas_call | solution.py:333
  841.2 117.4 %expert_fwd.3 = (f32[4,1024,2048]{2,1,0:T(8,128)}, f32[4,512,2048]{2,1,0:T(8,128)}) custom-call(bf16[8,512,2048]{2,1,0:T(8,128)(2,1)} %get-tuple-element.22.refs_1_.refs_0_, bf16[8,256,2048]{2,1,0:T(8,128)(2,1)} %get-tuple-element.25.refs_1_, f32[8,1024,4]{2,1,0:T(8,128)} %bitcast.42, ...), custom_call_target="tpu_custom_call", output_to_operand_aliasing={{0}: (5, {})} | custom-call | flops 103079215104 | bytes 50331648 | tf_op jit(solution)/shard_map/expert_fwd/pallas_call | solution.py:333
  958.7 3.3 convert_bitcast_fusion.1
  963.6 4.9 convert_bitcast_fusion
  968.7 233.3 %weight_grads.1 = (bf16[4,2048,512]{2,1,0:T(8,128)(2,1)}, bf16[4,2048,512]{2,1,0:T(8,128)(2,1)}, bf16[4,512,2048]{2,1,0:T(8,128)(2,1)}) custom-call(f32[8,1024,4]{2,1,0:T(8,128)} %bitcast.43, bf16[8,256,2048]{2,1,0:T(8,128)(2,1)} %bitcast.63, bf16[8,2,384,2048]{3,2,1,0:T(8,128)(2,1)} %bitcast.55, bf16[8,2,384,2048]{3,2,1,0:T(8,128)(2,1)} %bitcast.51, ...), custom_call_target="tpu_custom_call" | custom-call | flops 206158430208 | bytes 268435456 | tf_op jit(solution)/shard_map/weight_grads/pallas_call | solution.py:468
  1202.0 5.0 maximum_bitcast_fusion
  1207.1 37.5 %reduce-scatter.10.cloned.1.call-done = f32[1,1024,2048]{2,1,0:T(8,128)} async-done(((f32[4,1024,2048]{2,1,0:T(8,128)}), f32[1,1024,2048]{2,1,0:T(8,128)}) %reduce-scatter.10.cloned.1.call-update) | async-done | bytes 8388624
  1244.5 6.0 convert_element_type.16
  (45 shorter events, 16.8 us)
Async XLA Ops:
  7.2 199.8 %all-gather.7.cloned.1.call-start = ((), (), s32[]{:S(2)}) async-start(), calls=%async_computation.4 | async-start | bytes 28311552 | tf_op jit(solution)/shard_map/all_gather | solution.py:508
  7.2 5.7 copy-start
  9.6 37.7 %collective-permute-start = (bf16[384,2048]{1,0:T(8,128)(2,1)S(1)}, bf16[384,2048]{1,0:T(8,128)(2,1)S(1)}, u32[]{:S(2)}, u32[]{:S(2)}) collective-permute-start(bf16[384,2048]{1,0:T(8,128)(2,1)S(1)} %get-tuple-element.44), channel_id=1, source_target_pairs={{0,8},{8,0},{1,9},{9,1},{2,10},{10,2},{3,11},{11,3},{4,12},{12,4},... | collective-permute-start | bytes 4718600 | tf_op jit(solution)/shard_map/ppermute | solution.py:530
  49.2 380.0 %all-gather.11.cloned.1.call-start = ((), (), s32[]{:S(2)}) async-start(), calls=%async_computation.6 | async-start | bytes 9437184 | tf_op jit(solution)/shard_map/all_gather | solution.py:508
  52.0 24.4 %collective-permute-start.4 = (bf16[256,2048]{1,0:T(8,128)(2,1)S(1)}, bf16[256,2048]{1,0:T(8,128)(2,1)}, u32[]{:S(2)}, u32[]{:S(2)}) collective-permute-start(bf16[256,2048]{1,0:T(8,128)(2,1)S(1)} %get-tuple-element.40), channel_id=1, source_target_pairs={{0,8},{8,0},{1,9},{9,1},{2,10},{10,2},{3,11},{11,3},{4,12},{12,4},... | collective-permute-start | bytes 3145736 | tf_op jit(solution)/shard_map/ppermute | solution.py:530
  76.4 462.0 %all-gather.9.cloned.1.call-start = ((), (), s32[]{:S(2)}) async-start(), calls=%async_computation.5 | async-start | bytes 28311552 | tf_op jit(solution)/shard_map/all_gather | solution.py:508
  76.5 34.7 %collective-permute-start.3 = (bf16[384,2048]{1,0:T(8,128)(2,1)S(1)}, bf16[384,2048]{1,0:T(8,128)(2,1)S(1)}, u32[]{:S(2)}, u32[]{:S(2)}) collective-permute-start(bf16[384,2048]{1,0:T(8,128)(2,1)S(1)} %get-tuple-element.43), channel_id=1, source_target_pairs={{0,8},{8,0},{1,9},{9,1},{2,10},{10,2},{3,11},{11,3},{4,12},{12,4},... | collective-permute-start | bytes 4718600 | tf_op jit(solution)/shard_map/ppermute | solution.py:530
  113.2 3.4 copy-start.2
  113.2 3.4 copy-start.3
  115.3 91.7 %collective-permute-start.2 = (bf16[768,2048]{1,0:T(8,128)(2,1)S(1)}, bf16[768,2048]{1,0:T(8,128)(2,1)}, u32[]{:S(2)}, u32[]{:S(2)}) collective-permute-start(bf16[768,2048]{1,0:T(8,128)(2,1)S(1)} %slice_bitcast_fusion), channel_id=1, source_target_pairs={{0,8},{8,0},{1,9},{9,1},{2,10},{10,2},{3,11},{11,3},{4,12},{12,4},... | collective-permute-start | bytes 9437192 | tf_op jit(solution)/shard_map/ppermute | solution.py:530
  116.8 69.0 %collective-permute-start.1 = (f32[8,4,1024]{2,0,1:T(8,128)S(1)}, f32[8,4,1024]{2,0,1:T(8,128)S(1)}, u32[]{:S(2)}, u32[]{:S(2)}) collective-permute-start(f32[8,4,1024]{2,0,1:T(8,128)S(1)} %copy.24), channel_id=1, source_target_pairs={{0,8},{8,0},{1,9},{9,1},{2,10},{10,2},{3,11},{11,3},{4,12},{12,4},... | collective-permute-start | bytes 393224 | tf_op jit(solution)/shard_map/ppermute | solution.py:516
  186.6 17.7 %all-to-all-start = ((f32[8,4,1024]{2,1,0:T(4,128)}), f32[8,4,1024]{2,1,0:T(4,128)S(1)}, u32[]{:S(2)}, u32[]{:S(2)}) async-start(f32[8,4,1024]{2,1,0:T(4,128)} %copy.25), calls=%async_computation | async-start | bytes 262144 | tf_op jit(solution)/shard_map/all_to_all | solution.py:517
  189.9 768.8 %reduce-scatter.14.cloned.1.call-start = ((), (), s32[]{:S(2)}) async-start(), calls=%async_computation.9 | async-start | bytes 15728640
  362.9 600.7 %reduce-scatter.12.cloned.1.call-start = ((), (), s32[]{:S(2)}) async-start(), calls=%async_computation.8 | async-start | bytes 26214400
  694.9 1.2 copy-start.1
  695.0 549.6 %reduce-scatter.10.cloned.1.call-start = ((), (), s32[]{:S(2)}) async-start(), calls=%async_computation.7 | async-start | bytes 41943040
  696.2 25.5 %collective-permute-start.5 = (bf16[256,2048]{1,0:T(8,128)(2,1)S(1)}, bf16[256,2048]{1,0:T(8,128)(2,1)S(1)}, u32[]{:S(2)}, u32[]{:S(2)}) collective-permute-start(bf16[256,2048]{1,0:T(8,128)(2,1)S(1)} %copy-done.1), channel_id=1, source_target_pairs={{0,8},{8,0},{1,9},{9,1},{2,10},{10,2},{3,11},{11,3},{4,12},{12,4},... | collective-permute-start | bytes 3145736 | tf_op jit(solution)/shard_map/ppermute | solution.py:530
  721.6 1.0 copy-start.4
  962.0 240.0 %collective-permute-start.7 = (bf16[384,2048]{1,0:T(8,128)(2,1)}, bf16[384,2048]{1,0:T(8,128)(2,1)}, u32[]{:S(2)}, u32[]{:S(2)}) collective-permute-start(bf16[384,2048]{1,0:T(8,128)(2,1)} %convert_bitcast_fusion.1), channel_id=1, source_target_pairs={{8,0},{0,8},{9,1},{1,9},{10,2},{2,10},{11,3},{3,11},{12,4},{4,12},... | collective-permute-start | bytes 4718600 | tf_op jit(solution)/shard_map/ppermute | solution.py:557
  968.6 233.5 %collective-permute-start.6 = (bf16[640,2048]{1,0:T(8,128)(2,1)}, bf16[640,2048]{1,0:T(8,128)(2,1)}, u32[]{:S(2)}, u32[]{:S(2)}) collective-permute-start(bf16[640,2048]{1,0:T(8,128)(2,1)} %convert_bitcast_fusion), channel_id=1, source_target_pairs={{8,0},{0,8},{9,1},{1,9},{10,2},{2,10},{11,3},{3,11},{12,4},{4,12},... | collective-permute-start | bytes 7864328 | tf_op jit(solution)/shard_map/ppermute | solution.py:557
Sparse Core Ops, SparseCore 0:
  49.4 122.6 all-gather.6
  173.9 63.0 all-gather.10
  239.4 180.9 all-gather.8
  423.4 117.7 reduce-scatter.13
  695.1 218.4 reduce-scatter.11
  958.8 285.6 reduce-scatter.9

commit v9 on v8

--- a/solution.py
+++ b/solution.py
@@ -42,7 +42,7 @@
 def meet(peers):
     barrier = pltpu.get_barrier_semaphore()
     for peer in peers:
-        pl.semaphore_signal(barrier, inc=1, device_id={'expert': peer}, device_id_type=MESH)
+        pl.semaphore_signal(barrier, inc=1, device_id=peer, device_id_type=MESH)
     pl.semaphore_wait(barrier, len(peers))
 
 
@@ -81,7 +81,7 @@
 
     @pl.when(step == 0)
     def _():
-        meet(exchanges[0].peers if exchanges else [other])
+        meet([{'expert': peer} for peer in (exchanges[0].peers if exchanges else [other])])
 
     for exchange in exchanges:
         exchange.advance(step)
@@ -187,13 +187,6 @@
             pl.when(step == at)(functools.partial(self.stage, k))
         pl.when(step == 1)(self.settle)
 
-    def run(self):
-        for k in range(4):
-            self.stage(k)
-            if k == 0:
-                self.settle()
-        self.finish()
-
     def finish(self):
         for k in (4,) + tuple(range(7, 13)):
             self.into[k].wait_recv()
@@ -214,23 +207,51 @@
     ]
 
 
-def gather_body(first, own_ref, buf_ref, *scratch):
-    exchange = Exchange(own_ref, first, buf_ref, *scratch)
-    meet(exchange.peers)
-    exchange.run()
-
-
-def gather_now(array, first, rows, n_dev, collective_id):
-    model = array.shape[1]
-    return pl.pallas_call(
-        functools.partial(gather_body, first),
-        in_specs=[pl.BlockSpec(memory_space=pl.ANY)],
-        out_specs=pl.BlockSpec(memory_space=pl.ANY),
-        out_shape=jax.ShapeDtypeStruct((n_dev, rows, model), array.dtype),
-        scratch_shapes=exchange_scratch(rows, model),
+def opening_body(n_stage, x_ref, dy_ref, own_ref, next_ref, x_all_ref, dy_all_ref, hop_sem, *scratch):
+    me = {axis: lax.axis_index(axis) for axis in ('stage', 'expert')}
+    beside = dict(me, stage=lax.rem(me['stage'] + 1, n_stage))
+    first = 0
+    hops = []
+    for k, ref in enumerate((own_ref, next_ref)):
+        hops.append(pltpu.make_async_remote_copy(
+            src_ref=x_ref.at[pl.ds(first, ref.shape[0])], dst_ref=ref, send_sem=hop_sem.at[k, 0], recv_sem=hop_sem.at[k, 1],
+            device_id=beside, device_id_type=MESH))
+        first += ref.shape[0]
+    dy = Exchange(dy_ref, 0, dy_all_ref, *scratch[:4])
+    x = Exchange(own_ref, 0, x_all_ref, *scratch[4:])
+    meet([{'expert': peer} for peer in dy.peers] + [beside])
+    for hop in hops:
+        hop.start()
+    dy.stage(0)
+    dy.settle()
+    dy.stage(1)
+    dy.stage(2)
+    hops[0].wait_recv()
+    x.stage(0)
+    x.settle()
+    dy.stage(3)
+    for k in (1, 2, 3):
+        x.stage(k)
+    dy.finish()
+    x.finish()
+    hops[1].wait_recv()
+    for hop in hops:
+        hop.wait_send()
+
+
+def opening(x, dy, rows, more, n_dev, n_stage, collective_id):
+    model = x.shape[1]
+    full = jax.ShapeDtypeStruct((n_dev, rows, model), x.dtype)
+    outs = pl.pallas_call(
+        functools.partial(opening_body, n_stage),
+        in_specs=[HBM] * 2,
+        out_specs=[HBM] * 4,
+        out_shape=[jax.ShapeDtypeStruct((n, model), x.dtype) for n in (rows, more)] + [full, full],
+        scratch_shapes=[pltpu.SemaphoreType.DMA((2, 2))] + exchange_scratch(rows, model) * 2,
         compiler_params=pltpu.CompilerParams(collective_id=collective_id, has_side_effects=True),
-        name='gather_now',
-    )(array)
+        name='opening',
+    )(x, dy)
+    return outs[1:]
 
 
 def hosted_parts(hosted, stages, own_refs, buf_refs, scratch):
@@ -238,10 +259,15 @@
 
 
 class Weights:
-    def __init__(self, hbm, vmem, sem):
-        self.n_local = vmem[0].shape[0]
+    def __init__(self, hbm, w13_ref, w2_ref, sem):
+        self.n_local = w2_ref.shape[0]
+        ffn = w2_ref.shape[1]
+        one, three, two = hbm
         self.copies = lambda e: [
-            pltpu.make_async_copy(src.at[e], dst.at[e], sem.at[e, k]) for k, (src, dst) in enumerate(zip(hbm, vmem))]
+            pltpu.make_async_copy(one.at[e], w13_ref.at[e, :, pl.ds(0, ffn)], sem.at[e, 0]),
+            pltpu.make_async_copy(three.at[e], w13_ref.at[e, :, pl.ds(ffn, ffn)], sem.at[e, 1]),
+            pltpu.make_async_copy(two.at[e], w2_ref.at[e], sem.at[e, 2]),
+        ]
 
         @pl.when(pl.program_id(0) == 0)
         def _():
@@ -263,20 +289,21 @@
         lax.fori_loop(0, self.n_local // UNROLL, group, 0)
 
 
-def weight_scratch(w13, w2):
-    return [pltpu.VMEM(w13.shape, BF16), pltpu.VMEM(w2.shape, BF16), pltpu.SemaphoreType.DMA((w13.shape[0], 2))]
+def weight_scratch(w2):
+    n_local, ffn, model = w2.shape
+    return [pltpu.VMEM((n_local, model, 2 * ffn), BF16), pltpu.VMEM(w2.shape, BF16), pltpu.SemaphoreType.DMA((n_local, 3))]
 
 
 def fwd_body(ffn, half, tile, start, n_x, n_carried, hosted, stages, *refs):
     refs = list(refs)
-    x_refs, (g_ref, w13_hbm, w2_hbm), refs = refs[:n_x], refs[n_x:n_x + 3], refs[n_x + 3 + n_carried:]
+    x_refs, (g_ref, *weights_hbm), refs = refs[:n_x], refs[n_x:n_x + 4], refs[n_x + 4 + n_carried:]
     own_refs, refs = refs[:len(hosted)], refs[len(hosted):]
     (y_ref, inbox_ref), refs = refs[:2], refs[2:]
     buf_refs, refs = refs[:len(hosted)], refs[len(hosted):]
     w13_ref, w2_ref, w_sem, *refs = refs
     scratch, refs = refs[:5], refs[5:]
     exchanges = hosted_parts(hosted, stages, own_refs, buf_refs, refs)
-    weights = Weights((w13_hbm, w2_hbm), (w13_ref, w2_ref), w_sem)
+    weights = Weights(weights_hbm, w13_ref, w2_ref, w_sem)
 
     def compute(add):
         def experts(es):
@@ -318,10 +345,11 @@
     return index
 
 
-def expert_fwd(xs, gates, w13, w2, start, carried, hosted, stages, collective_id):
+def expert_fwd(xs, gates, w, start, carried, hosted, stages, collective_id):
     n_src, _, model = xs[0][0].shape
     tile = BLOCK * len(xs)
     n_tok = gates.shape[1]
+    w2 = w[2]
     n_local, ffn = w2.shape[:2]
     half = n_src // CORES
     at = at_source(half)
@@ -334,21 +362,22 @@
         functools.partial(fwd_body, ffn, half, tile, start, len(xs), len(carried), [h[1:] for h in hosted], stages),
         grid=(2 * half,),
         in_specs=[rows_of(block) for _, block in xs] + [pl.BlockSpec((1, n_tok, n_local), at)]
-        + [HBM] * (2 + len(carried) + len(hosted)),
+        + [HBM] * (3 + len(carried) + len(hosted)),
         out_specs=[HBM] * (2 + len(hosted)),
         out_shape=[jax.ShapeDtypeStruct((half, n_tok, model), F32), jax.ShapeDtypeStruct((half, tile, model), F32)]
         + [jax.ShapeDtypeStruct((n_src, rows, model), BF16) for _, _, rows in hosted],
-        scratch_shapes=weight_scratch(w13, w2) + pair_scratch(tile, model, half)
+        scratch_shapes=weight_scratch(w2) + pair_scratch(tile, model, half)
         + [ref for _, _, rows in hosted for ref in exchange_scratch(rows, model)],
-        input_output_aliases={len(xs) + 3 + i: i for i in range(len(carried))},
+        input_output_aliases={len(xs) + 4 + i: i for i in range(len(carried))},
         compiler_params=pair_params(collective_id),
         cost_estimate=pl.CostEstimate(flops=flops, bytes_accessed=n_src * tile * model * 6, transcendentals=0),
         name='expert_fwd',
-    )(*[x for x, _ in xs], gates, w13, w2, *carried, *[h[0] for h in hosted])
+    )(*[x for x, _ in xs], gates, *w, *carried, *[h[0] for h in hosted])
     return outs[0], outs[2:]
 
 
-def bwd_body(ffn, half, start, first, n_carried, hosted, stages, x_ref, dy_ref, g_ref, w13_hbm, w2_hbm, *refs):
+def bwd_body(ffn, half, start, first, n_carried, hosted, stages, x_ref, dy_ref, g_ref, one_hbm, three_hbm, two_hbm, *refs):
+    weights_hbm = one_hbm, three_hbm, two_hbm
     refs = list(refs[n_carried:])
     own_refs, refs = refs[:len(hosted)], refs[len(hosted):]
     (dx_ref, da_ref, h_ref, inbox_ref), refs = refs[:4], refs[4:]
@@ -357,7 +386,7 @@
     scratch, refs = refs[:5], refs[5:]
     exchanges = hosted_parts(hosted, stages, own_refs, buf_refs, refs)
     tile = x_ref.shape[-2]
-    weights = Weights((w13_hbm, w2_hbm), (w13_ref, w2_ref), w_sem)
+    weights = Weights(weights_hbm, w13_ref, w2_ref, w_sem)
 
     def compute(add):
         def experts(es):
@@ -385,9 +414,10 @@
     pair_sum(compute, half, 1, tile, inbox_ref, (dx_ref, first), exchanges, *scratch)
 
 
-def expert_bwd(x, dy, gates, w13, w2, start, dx_rows, first, carried, hosted, stages, collective_id):
+def expert_bwd(x, dy, gates, w, start, dx_rows, first, carried, hosted, stages, collective_id):
     n_src, tile, model = x[0].shape[0], x[0].shape[-2], x[0].shape[-1]
     n_tok = gates.shape[1]
+    w2 = w[2]
     n_local, ffn = w2.shape[:2]
     half = n_src // CORES
     at = at_source(half)
@@ -402,7 +432,7 @@
         functools.partial(bwd_body, ffn, half, start, first, len(carried), [h[1:] for h in hosted], stages),
         grid=(2 * half,),
         in_specs=[rows_of(*x), rows_of(*dy), pl.BlockSpec((1, n_tok, n_local), at)]
-        + [HBM] * (2 + len(carried) + len(hosted)),
+        + [HBM] * (3 + len(carried) + len(hosted)),
         out_specs=[
             HBM,
             pl.BlockSpec((1, tile, 2 * ffn * n_local), at),
@@ -414,13 +444,13 @@
             jax.ShapeDtypeStruct((n_src, tile, ffn * n_local), BF16),
             jax.ShapeDtypeStruct((half, tile, model), F32),
         ] + [jax.ShapeDtypeStruct((n_src, rows, model), BF16) for _, _, rows in hosted],
-        scratch_shapes=weight_scratch(w13, w2) + pair_scratch(tile, model, half)
+        scratch_shapes=weight_scratch(w2) + pair_scratch(tile, model, half)
         + [ref for _, _, rows in hosted for ref in exchange_scratch(rows, model)],
-        input_output_aliases={5 + i: 0 for i in range(len(carried))},
+        input_output_aliases={6 + i: 0 for i in range(len(carried))},
         compiler_params=pair_params(collective_id),
         cost_estimate=pl.CostEstimate(flops=flops, bytes_accessed=n_src * tile * model * 14, transcendentals=0),
         name='expert_bwd',
-    )(x[0], dy[0], gates, w13, w2, *carried, *[h[0] for h in hosted])
+    )(x[0], dy[0], gates, *w, *carried, *[h[0] for h in hosted])
     return outs[0], outs[1], outs[2], outs[4:]
 
 
@@ -516,8 +546,7 @@
         gate_dst = lax.ppermute(gate_src, 'stage', to_next)
         gates = jnp.transpose(lax.all_to_all(gate_dst, 'expert', 0, 0), (0, 2, 1))
 
-        w13 = jnp.concatenate([w_one[0], w_three[0]], axis=2)
-        w2 = w_two[0]
+        w = w_one[0], w_three[0], w_two[0]
 
         def spans(sizes):
             ends = [sum(sizes[:k + 1]) for k in range(len(sizes))]
@@ -529,10 +558,9 @@
         def hop(rows):
             return lax.ppermute(x_src[rows], 'stage', to_next)
 
-        dys = [(gather_now(dy_act[0], 0, BWD_ROWS[0], n_dev, 5), 0)]
-        xs = [(gather(hop(bwd[0])), 0)]
-        for k in (1, 2):
-            x_dst = hop(bwd[k])
+        x_next, x_all, dy_all = opening(x_src, dy_act[0], BWD_ROWS[0], BWD_ROWS[1], n_dev, n_stage, 5)
+        dys, xs = [(dy_all, 0)], [(x_all, 0)]
+        for k, x_dst in ((1, x_next), (2, hop(bwd[2]))):
             both = gather(jnp.stack([dy_act[0, bwd[k]], x_dst]))
             dys.append((both, 0))
             xs.append((both, 1))
@@ -547,7 +575,7 @@
         dx_parts = []
         for k in range(3):
             dx_part, d_pre, hidden, arrived = expert_bwd(
-                xs[k], dys[k], gates, w13, w2, bwd[k].start, dx_rows[k // 2], BWD_ROWS[0] if k == 1 else 0,
+                xs[k], dys[k], gates, w, bwd[k].start, dx_rows[k // 2], BWD_ROWS[0] if k == 1 else 0,
                 (dx_part,) if k == 1 else (), pieces[k - 1:k] if k else (), STAGES[k - 1:k], k)
             x_fwd += blocks(arrived)
             d_pres.append(d_pre)
@@ -560,7 +588,7 @@
         y_part = ()
         for k in range(2):
             out, arrived = expert_fwd(
-                x_fwd[2 * k:2 * k + 2], gates, w13, w2, fwd[k].start, y_part, () if k else pieces[2:], STAGES[2:], 3 + k)
+                x_fwd[2 * k:2 * k + 2], gates, w, fwd[k].start, y_part, () if k else pieces[2:], STAGES[2:], 3 + k)
             y_part = (out,)
             x_fwd += blocks(arrived)
         y_out = reduce_rows(y_part[0])

time: 1270 us -> 1260 us (level)
  Pallas kernels: 957 us -> 1020 us
  waiting for transfers between devices: 220 us -> 160 us
  other arithmetic: 37.6 us -> 24.2 us
    pallas_call x1, Pallas kernels: 65.9 us -> 128 us  [opening(): pl.pallas_call(functools.partial(opening_body, n_stage), in_specs=[HBM] *...]
    ppermute x5 -> x3, waiting for transfers between devices: 114 us -> 53.6 us  [hop(): return lax.ppermute(x_src[rows], 'stage', to_next)]
    concatenate x1 -> x0, other arithmetic: 14.3 us -> none  [moe_body(): w13 = jnp.concatenate([w_one[0], w_three[0]], axis=2)]
    unnamed x9 -> x8, waiting for transfers between devices: 37.6 us -> 35.7 us
  transfers between devices with their start and end apart: 15 -> 11, of which waited for: 6 -> 4; matrix products, arithmetic and copies ran while one was open for 3% -> 2% of each run, Pallas kernels for 76% -> 82%
where the time goes in v9:
time: 1260 us; the launch traced here: 1250 us
  Pallas kernels  1020 us (81%)
  waiting for transfers between devices  160 us (13%)
  other arithmetic  24.2 us (2%)
  between operations  14.1 us (1%)
    pallas_call x3, Pallas kernels, expert_bwd(): pl.pallas_call(functools.partial(bwd_body, ffn, half, start, first, len(c...  422 us
    pallas_call x2, Pallas kernels, expert_fwd(): pl.pallas_call(functools.partial(fwd_body, ffn, half, tile, start, len(xs...  236 us
    pallas_call x1, Pallas kernels, weight_grads(): pl.pallas_call(functools.partial(grad_body, ffn, len(xs)), grid=(n_local,...  233 us
    pallas_call x1, Pallas kernels, opening(): pl.pallas_call(functools.partial(opening_body, n_stage), in_specs=[HBM] *...  128 us
    ppermute x1, waiting for transfers between devices, moe_body(): gate_dst = lax.ppermute(gate_src, 'stage', to_next)  70.9 us
    ppermute x3, waiting for transfers between devices, hop(): return lax.ppermute(x_src[rows], 'stage', to_next)  53.6 us
    unnamed x8, waiting for transfers between devices  35.7 us
  transfers between devices with their start and end apart: 11, of which 4 were waited for; matrix products, arithmetic and copies ran while one was open for 2% of the time, Pallas kernels for 82%

profile of v9, /device:TPU:0, one launch (start us, length us, event | category | flops | bytes accessed | tf_op | source)
XLA Modules:
  0.0 1249.5 jit_solution(5180767550135075333)
XLA Ops:
  7.2 1.6 slice_bitcast_fusion.1
  8.8 3.3 collective-permute-start
  12.1 2.2 fusion
  14.3 32.2 %collective-permute-done = bf16[384,2048]{1,0:T(8,128)(2,1)S(1)} collective-permute-done((bf16[384,2048]{1,0:T(8,128)(2,1)S(1)}, bf16[384,2048]{1,0:T(8,128)(2,1)S(1)}, u32[]{:S(2)}, u32[]{:S(2)}) %collective-permute-start) | collective-permute-done | bytes 1572896 | tf_op jit(solution)/shard_map/ppermute | solution.py:559
  46.5 1.9 pad_maximum_fusion
  48.5 127.7 %opening.1 = (bf16[256,2048]{1,0:T(8,128)(2,1)}, bf16[384,2048]{1,0:T(8,128)(2,1)}, bf16[8,256,2048]{2,1,0:T(8,128)(2,1)}, bf16[8,256,2048]{2,1,0:T(8,128)(2,1)}) custom-call(bf16[1024,2048]{1,0:T(8,128)(2,1)} %bitcast.31, bf16[1024,2048]{1,0:T(8,128)(2,1)} %bitcast.32), custom_call_target="tpu_custom_call" | custom-call | tf_op jit(solution)/shard_map/opening/pallas_call | solution.py:245
  176.2 3.4 pad_maximum_fusion.1
  179.7 2.1 slice_bitcast_fusion
  181.8 1.6 collective-permute-start.2
  184.1 70.9 %collective-permute-done.1 = f32[8,4,1024]{2,0,1:T(8,128)S(1)} collective-permute-done((f32[8,4,1024]{2,0,1:T(8,128)S(1)}, f32[8,4,1024]{2,0,1:T(8,128)S(1)}, u32[]{:S(2)}, u32[]{:S(2)}) %collective-permute-start.1) | collective-permute-done | bytes 131104 | tf_op jit(solution)/shard_map/ppermute | solution.py:546
  255.1 9.9 all_to_all.5
  265.0 2.7 copy.26
  267.7 156.0 %expert_bwd.3 = (f32[4,384,2048]{2,1,0:T(8,128)}, bf16[8,384,4096]{2,1,0:T(8,128)(2,1)}, bf16[8,384,2048]{2,1,0:T(8,128)(2,1)}, f32[4,384,2048]{2,1,0:T(8,128)}, bf16[8,512,2048]{2,1,0:T(8,128)(2,1)}) custom-call(bf16[8,2,384,2048]{3,2,1,0:T(8,128)(2,1)} %bitcast.44, bf16[8,2,384,2048]{3,2,1,0:T(8,128)(2,1)} %bitcast.45, f32[8,1024,4]{2,1,0:T(8,128)} %bitcast.33, ...), custom_call_target="tpu_custom_call" | custom-call | flops 128849018880 | bytes 88080384 | tf_op jit(solution)/shard_map/expert_bwd/pallas_call | solution.py:431
  424.2 110.3 %expert_bwd.4 = (f32[4,640,2048]{2,1,0:T(8,128)}, bf16[8,256,4096]{2,1,0:T(8,128)(2,1)}, bf16[8,256,2048]{2,1,0:T(8,128)(2,1)}, f32[4,256,2048]{2,1,0:T(8,128)}) custom-call(bf16[8,256,2048]{2,1,0:T(8,128)(2,1)} %get-tuple-element.27.x_ref.refs_0_, bf16[8,256,2048]{2,1,0:T(8,128)(2,1)} %get-tuple-element.28.dy_ref.refs_3_, f32[8,1024,4]{2,1,0:T(8,128)} %bitcast.34, ...), custom_call_target="tpu_custom_call" | custom-call | flops 85899345920 | bytes 58720256 | tf_op jit(solution)/shard_map/expert_bwd/pallas_call | solution.py:431
  534.5 156.1 %expert_bwd.5 = (f32[4,640,2048]{2,1,0:T(8,128)}, bf16[8,384,4096]{2,1,0:T(8,128)(2,1)}, bf16[8,384,2048]{2,1,0:T(8,128)(2,1)}, f32[4,384,2048]{2,1,0:T(8,128)}, bf16[8,256,2048]{2,1,0:T(8,128)(2,1)}) custom-call(bf16[8,2,384,2048]{3,2,1,0:T(8,128)(2,1)} %bitcast.48, bf16[8,2,384,2048]{3,2,1,0:T(8,128)(2,1)} %bitcast.49, ...), custom_call_target="tpu_custom_call", output_to_operand_aliasing={{0}: (6, {})} | custom-call | flops 128849018880 | bytes 88080384 | tf_op jit(solution)/shard_map/expert_bwd/pallas_call | solution.py:431
  693.5 21.4 %collective-permute-done.3.refs_6_ = bf16[256,2048]{1,0:T(8,128)(2,1)S(1)} collective-permute-done((bf16[256,2048]{1,0:T(8,128)(2,1)S(1)}, bf16[256,2048]{1,0:T(8,128)(2,1)S(1)}, u32[]{:S(2)}, u32[]{:S(2)}) %collective-permute-start.3) | collective-permute-done | bytes 1048608 | tf_op jit(solution)/shard_map/ppermute | solution.py:559
  715.9 118.8 %expert_fwd.2 = (f32[4,1024,2048]{2,1,0:T(8,128)}, f32[4,512,2048]{2,1,0:T(8,128)}, bf16[8,256,2048]{2,1,0:T(8,128)(2,1)}) custom-call(bf16[8,256,2048]{2,1,0:T(8,128)(2,1)} %get-tuple-element.30.refs_0_, bf16[8,512,2048]{2,1,0:T(8,128)(2,1)} %get-tuple-element.25.refs_1_.refs_0_, f32[8,1024,4]{2,1,0:T(8,128)} %bitcast.36, bf16[4,2048,512]{2,1,0:T(8,128)(2,1)} %bitcast.55, ...), custom_call_target="tpu_custom_call" | custom-call | flops 103079215104 | bytes 50331648 | tf_op jit(solution)/shard_map/expert_fwd/pallas_call | solution.py:361
  834.7 117.5 %expert_fwd.3 = (f32[4,1024,2048]{2,1,0:T(8,128)}, f32[4,512,2048]{2,1,0:T(8,128)}) custom-call(bf16[8,512,2048]{2,1,0:T(8,128)(2,1)} %get-tuple-element.25.refs_1_.refs_0_, bf16[8,256,2048]{2,1,0:T(8,128)(2,1)} %get-tuple-element.31.refs_1_, f32[8,1024,4]{2,1,0:T(8,128)} %bitcast.37, ...), custom_call_target="tpu_custom_call", output_to_operand_aliasing={{0}: (6, {})} | custom-call | flops 103079215104 | bytes 50331648 | tf_op jit(solution)/shard_map/expert_fwd/pallas_call | solution.py:361
  952.3 3.3 convert_bitcast_fusion.1
  957.0 4.4 convert_bitcast_fusion
  962.6 233.4 %weight_grads.1 = (bf16[4,2048,512]{2,1,0:T(8,128)(2,1)}, bf16[4,2048,512]{2,1,0:T(8,128)(2,1)}, bf16[4,512,2048]{2,1,0:T(8,128)(2,1)}) custom-call(f32[8,1024,4]{2,1,0:T(8,128)} %bitcast.38, bf16[8,256,2048]{2,1,0:T(8,128)(2,1)} %get-tuple-element.27.x_ref.refs_0_, bf16[8,2,384,2048]{3,2,1,0:T(8,128)(2,1)} %bitcast.50, bf16[8,2,384,2048]{3,2,1,0:T(8,128)(2,1)} %bitcast.46, ...), custom_call_target="tpu_custom_call" | custom-call | flops 206158430208 | bytes 268435456 | tf_op jit(solution)/shard_map/weight_grads/pallas_call | solution.py:498
  1196.1 5.1 maximum_bitcast_fusion
  1201.1 35.6 %reduce-scatter.10.cloned.1.call-done = f32[1,1024,2048]{2,1,0:T(8,128)} async-done(((f32[4,1024,2048]{2,1,0:T(8,128)}), f32[1,1024,2048]{2,1,0:T(8,128)}) %reduce-scatter.10.cloned.1.call-update) | async-done | bytes 8388624
  1236.7 6.0 convert_element_type.16
  (32 shorter events, 8.0 us)
Async XLA Ops:
  7.2 260.5 %all-gather.5.cloned.1.call-start = ((), (), s32[]{:S(2)}) async-start(), calls=%async_computation.4 | async-start | bytes 28311552 | tf_op jit(solution)/shard_map/all_gather | solution.py:538
  8.8 37.7 %collective-permute-start = (bf16[384,2048]{1,0:T(8,128)(2,1)S(1)}, bf16[384,2048]{1,0:T(8,128)(2,1)S(1)}, u32[]{:S(2)}, u32[]{:S(2)}) collective-permute-start(bf16[384,2048]{1,0:T(8,128)(2,1)S(1)} %slice_bitcast_fusion.1), channel_id=1, source_target_pairs={{0,8},{8,0},{1,9},{9,1},{2,10},{10,2},{3,11},{11,3},{4,12},{12,4},... | collective-permute-start | bytes 4718600 | tf_op jit(solution)/shard_map/ppermute | solution.py:559
  48.5 486.1 %all-gather.7.cloned.1.call-start = ((), (), s32[]{:S(2)}) async-start(), calls=%async_computation.5 | async-start | bytes 28311552 | tf_op jit(solution)/shard_map/all_gather | solution.py:538
  179.6 3.8 copy-start
  179.6 3.8 copy-start.1
  179.6 772.7 %reduce-scatter.14.cloned.1.call-start = ((), (), s32[]{:S(2)}) async-start(), calls=%async_computation.8 | async-start | bytes 15728640
  181.8 85.9 %collective-permute-start.2 = (bf16[768,2048]{1,0:T(8,128)(2,1)S(1)}, bf16[768,2048]{1,0:T(8,128)(2,1)}, u32[]{:S(2)}, u32[]{:S(2)}) collective-permute-start(bf16[768,2048]{1,0:T(8,128)(2,1)S(1)} %slice_bitcast_fusion), channel_id=1, source_target_pairs={{0,8},{8,0},{1,9},{9,1},{2,10},{10,2},{3,11},{11,3},{4,12},{12,4},... | collective-permute-start | bytes 9437192 | tf_op jit(solution)/shard_map/ppermute | solution.py:559
  183.7 71.4 %collective-permute-start.1 = (f32[8,4,1024]{2,0,1:T(8,128)S(1)}, f32[8,4,1024]{2,0,1:T(8,128)S(1)}, u32[]{:S(2)}, u32[]{:S(2)}) collective-permute-start(f32[8,4,1024]{2,0,1:T(8,128)S(1)} %copy.24), channel_id=1, source_target_pairs={{0,8},{8,0},{1,9},{9,1},{2,10},{10,2},{3,11},{11,3},{4,12},{12,4},... | collective-permute-start | bytes 393224 | tf_op jit(solution)/shard_map/ppermute | solution.py:546
  423.7 533.3 %reduce-scatter.12.cloned.1.call-start = ((), (), s32[]{:S(2)}) async-start(), calls=%async_computation.7 | async-start | bytes 26214400
  690.6 546.0 %reduce-scatter.10.cloned.1.call-start = ((), (), s32[]{:S(2)}) async-start(), calls=%async_computation.6 | async-start | bytes 41943040
  692.0 22.9 %collective-permute-start.3 = (bf16[256,2048]{1,0:T(8,128)(2,1)S(1)}, bf16[256,2048]{1,0:T(8,128)(2,1)S(1)}, u32[]{:S(2)}, u32[]{:S(2)}) collective-permute-start(bf16[256,2048]{1,0:T(8,128)(2,1)S(1)} %slice_bitcast_fusion.2), channel_id=1, source_target_pairs={{0,8},{8,0},{1,9},{9,1},{2,10},{10,2},{3,11},{11,3},{4,12},{12,4},... | collective-permute-start | bytes 3145736 | tf_op jit(solution)/shard_map/ppermute | solution.py:559
  714.9 1.0 copy-start.2
  955.6 240.4 %collective-permute-start.5 = (bf16[384,2048]{1,0:T(8,128)(2,1)}, bf16[384,2048]{1,0:T(8,128)(2,1)}, u32[]{:S(2)}, u32[]{:S(2)}) collective-permute-start(bf16[384,2048]{1,0:T(8,128)(2,1)} %convert_bitcast_fusion.1), channel_id=1, source_target_pairs={{8,0},{0,8},{9,1},{1,9},{10,2},{2,10},{11,3},{3,11},{12,4},{4,12},... | collective-permute-start | bytes 4718600 | tf_op jit(solution)/shard_map/ppermute | solution.py:585
  961.4 234.7 %collective-permute-start.4 = (bf16[640,2048]{1,0:T(8,128)(2,1)}, bf16[640,2048]{1,0:T(8,128)(2,1)}, u32[]{:S(2)}, u32[]{:S(2)}) collective-permute-start(bf16[640,2048]{1,0:T(8,128)(2,1)} %convert_bitcast_fusion), channel_id=1, source_target_pairs={{8,0},{0,8},{9,1},{1,9},{10,2},{2,10},{11,3},{3,11},{12,4},{4,12},... | collective-permute-start | bytes 7864328 | tf_op jit(solution)/shard_map/ppermute | solution.py:585
Sparse Core Ops, SparseCore 0:
  48.6 174.8 all-gather.4
  225.9 184.6 all-gather.6
  423.8 116.8 reduce-scatter.13
  690.8 217.3 reduce-scatter.11
  952.4 284.2 reduce-scatter.9

commit v10 on v9

--- a/solution.py
+++ b/solution.py
@@ -207,23 +207,27 @@
     ]
 
 
-def opening_body(n_stage, x_ref, dy_ref, own_ref, next_ref, x_all_ref, dy_all_ref, hop_sem, *scratch):
+def opening_body(n_stage, x_ref, dy_ref, own_ref, next_ref, x_all_ref, dy_all_ref, hop_sem, stage_ref, stage_sem, *scratch):
     me = {axis: lax.axis_index(axis) for axis in ('stage', 'expert')}
     beside = dict(me, stage=lax.rem(me['stage'] + 1, n_stage))
-    first = 0
-    hops = []
-    for k, ref in enumerate((own_ref, next_ref)):
-        hops.append(pltpu.make_async_remote_copy(
+    rows, more = own_ref.shape[0], next_ref.shape[1]
+    hops = [
+        pltpu.make_async_remote_copy(
             src_ref=x_ref.at[pl.ds(first, ref.shape[0])], dst_ref=ref, send_sem=hop_sem.at[k, 0], recv_sem=hop_sem.at[k, 1],
-            device_id=beside, device_id_type=MESH))
-        first += ref.shape[0]
+            device_id=beside, device_id_type=MESH)
+        for k, (first, ref) in enumerate(((0, own_ref), (rows, next_ref.at[1])))]
+    take = pltpu.make_async_copy(dy_ref.at[pl.ds(rows, more)], stage_ref, stage_sem.at[0])
+    put = pltpu.make_async_copy(stage_ref, next_ref.at[0], stage_sem.at[1])
     dy = Exchange(dy_ref, 0, dy_all_ref, *scratch[:4])
     x = Exchange(own_ref, 0, x_all_ref, *scratch[4:])
     meet([{'expert': peer} for peer in dy.peers] + [beside])
     for hop in hops:
         hop.start()
     dy.stage(0)
+    take.start()
     dy.settle()
+    take.wait()
+    put.start()
     dy.stage(1)
     dy.stage(2)
     hops[0].wait_recv()
@@ -234,6 +238,7 @@
         x.stage(k)
     dy.finish()
     x.finish()
+    put.wait()
     hops[1].wait_recv()
     for hop in hops:
         hop.wait_send()
@@ -241,13 +246,14 @@
 
 def opening(x, dy, rows, more, n_dev, n_stage, collective_id):
     model = x.shape[1]
-    full = jax.ShapeDtypeStruct((n_dev, rows, model), x.dtype)
+    shapes = (rows, model), (2, more, model), (n_dev, rows, model), (n_dev, rows, model)
     outs = pl.pallas_call(
         functools.partial(opening_body, n_stage),
         in_specs=[HBM] * 2,
         out_specs=[HBM] * 4,
-        out_shape=[jax.ShapeDtypeStruct((n, model), x.dtype) for n in (rows, more)] + [full, full],
-        scratch_shapes=[pltpu.SemaphoreType.DMA((2, 2))] + exchange_scratch(rows, model) * 2,
+        out_shape=[jax.ShapeDtypeStruct(shape, x.dtype) for shape in shapes],
+        scratch_shapes=[pltpu.SemaphoreType.DMA((2, 2)), pltpu.VMEM((more, model), BF16), pltpu.SemaphoreType.DMA((2,))]
+        + exchange_scratch(rows, model) * 2,
         compiler_params=pltpu.CompilerParams(collective_id=collective_id, has_side_effects=True),
         name='opening',
     )(x, dy)
@@ -558,10 +564,10 @@
         def hop(rows):
             return lax.ppermute(x_src[rows], 'stage', to_next)
 
-        x_next, x_all, dy_all = opening(x_src, dy_act[0], BWD_ROWS[0], BWD_ROWS[1], n_dev, n_stage, 5)
+        both, x_all, dy_all = opening(x_src, dy_act[0], BWD_ROWS[0], BWD_ROWS[1], n_dev, n_stage, 5)
         dys, xs = [(dy_all, 0)], [(x_all, 0)]
-        for k, x_dst in ((1, x_next), (2, hop(bwd[2]))):
-            both = gather(jnp.stack([dy_act[0, bwd[k]], x_dst]))
+        for stacked in (both, jnp.stack([dy_act[0, bwd[2]], hop(bwd[2])])):
+            both = gather(stacked)
             dys.append((both, 0))
             xs.append((both, 1))
         cut = sum(X_ROWS[:2])

time: 1260 us -> 1250 us (level)
  no operation moved by 1% of the time
where the time goes in v10:
time: 1250 us
  Pallas kernels  1020 us (82%)
  waiting for transfers between devices  163 us (13%)
  other arithmetic  20.8 us (2%)
  between operations  14.1 us (1%)
    pallas_call x3, Pallas kernels, expert_bwd(): pl.pallas_call(functools.partial(bwd_body, ffn, half, start, first, len(c...  423 us
    pallas_call x2, Pallas kernels, expert_fwd(): pl.pallas_call(functools.partial(fwd_body, ffn, half, tile, start, len(xs...  236 us
    pallas_call x1, Pallas kernels, weight_grads(): pl.pallas_call(functools.partial(grad_body, ffn, len(xs)), grid=(n_local,...  233 us
    pallas_call x1, Pallas kernels, opening(): pl.pallas_call(functools.partial(opening_body, n_stage), in_specs=[HBM] *...  128 us
    ppermute x1, waiting for transfers between devices, moe_body(): gate_dst = lax.ppermute(gate_src, 'stage', to_next)  70.9 us
    ppermute x3, waiting for transfers between devices, hop(): return lax.ppermute(x_src[rows], 'stage', to_next)  55.9 us
    unnamed x8, waiting for transfers between devices  35.7 us
  transfers between devices with their start and end apart: 11, of which 4 were waited for; matrix products, arithmetic and copies ran while one was open for 2% of the time, Pallas kernels for 82%

profile of v10, /device:TPU:0, one launch (start us, length us, event | category | flops | bytes accessed | tf_op | source)
XLA Modules:
  0.0 1246.6 jit_solution(2865314497284646372)
XLA Ops:
  7.2 1.6 slice_bitcast_fusion.1
  8.9 3.3 collective-permute-start
  12.2 34.4 %collective-permute-done = bf16[384,2048]{1,0:T(8,128)(2,1)S(1)} collective-permute-done((bf16[384,2048]{1,0:T(8,128)(2,1)S(1)}, bf16[384,2048]{1,0:T(8,128)(2,1)S(1)}, u32[]{:S(2)}, u32[]{:S(2)}) %collective-permute-start) | collective-permute-done | bytes 1572896 | tf_op jit(solution)/shard_map/ppermute | solution.py:565
  46.6 1.9 pad_maximum_fusion
  48.6 127.7 %opening.1 = (bf16[256,2048]{1,0:T(8,128)(2,1)}, bf16[2,384,2048]{2,1,0:T(8,128)(2,1)}, bf16[8,256,2048]{2,1,0:T(8,128)(2,1)}, bf16[8,256,2048]{2,1,0:T(8,128)(2,1)}) custom-call(bf16[1024,2048]{1,0:T(8,128)(2,1)} %bitcast.30, bf16[1024,2048]{1,0:T(8,128)(2,1)} %bitcast.31), custom_call_target="tpu_custom_call" | custom-call | tf_op jit(solution)/shard_map/opening/pallas_call | solution.py:250
  176.4 2.1 slice_bitcast_fusion
  178.5 1.6 collective-permute-start.2
  180.9 70.9 %collective-permute-done.1 = f32[8,4,1024]{2,0,1:T(8,128)S(1)} collective-permute-done((f32[8,4,1024]{2,0,1:T(8,128)S(1)}, f32[8,4,1024]{2,0,1:T(8,128)S(1)}, u32[]{:S(2)}, u32[]{:S(2)}) %collective-permute-start.1) | collective-permute-done | bytes 131104 | tf_op jit(solution)/shard_map/ppermute | solution.py:552
  251.9 10.0 all_to_all.5
  261.8 2.7 copy.26
  264.5 156.0 %expert_bwd.3 = (f32[4,384,2048]{2,1,0:T(8,128)}, bf16[8,384,4096]{2,1,0:T(8,128)(2,1)}, bf16[8,384,2048]{2,1,0:T(8,128)(2,1)}, f32[4,384,2048]{2,1,0:T(8,128)}, bf16[8,512,2048]{2,1,0:T(8,128)(2,1)}) custom-call(bf16[8,2,384,2048]{3,2,1,0:T(8,128)(2,1)} %bitcast.42, bf16[8,2,384,2048]{3,2,1,0:T(8,128)(2,1)} %bitcast.43, f32[8,1024,4]{2,1,0:T(8,128)} %bitcast.32, ...), custom_call_target="tpu_custom_call" | custom-call | flops 128849018880 | bytes 88080384 | tf_op jit(solution)/shard_map/expert_bwd/pallas_call | solution.py:437
  420.8 110.3 %expert_bwd.4 = (f32[4,640,2048]{2,1,0:T(8,128)}, bf16[8,256,4096]{2,1,0:T(8,128)(2,1)}, bf16[8,256,2048]{2,1,0:T(8,128)(2,1)}, f32[4,256,2048]{2,1,0:T(8,128)}) custom-call(bf16[8,256,2048]{2,1,0:T(8,128)(2,1)} %get-tuple-element.27.x_ref.refs_0_, bf16[8,256,2048]{2,1,0:T(8,128)(2,1)} %get-tuple-element.28.dy_ref.refs_3_, f32[8,1024,4]{2,1,0:T(8,128)} %bitcast.33, ...), custom_call_target="tpu_custom_call" | custom-call | flops 85899345920 | bytes 58720256 | tf_op jit(solution)/shard_map/expert_bwd/pallas_call | solution.py:437
  531.2 156.6 %expert_bwd.5 = (f32[4,640,2048]{2,1,0:T(8,128)}, bf16[8,384,4096]{2,1,0:T(8,128)(2,1)}, bf16[8,384,2048]{2,1,0:T(8,128)(2,1)}, f32[4,384,2048]{2,1,0:T(8,128)}, bf16[8,256,2048]{2,1,0:T(8,128)(2,1)}) custom-call(bf16[8,2,384,2048]{3,2,1,0:T(8,128)(2,1)} %bitcast.46, bf16[8,2,384,2048]{3,2,1,0:T(8,128)(2,1)} %bitcast.47, ...), custom_call_target="tpu_custom_call", output_to_operand_aliasing={{0}: (6, {})} | custom-call | flops 128849018880 | bytes 88080384 | tf_op jit(solution)/shard_map/expert_bwd/pallas_call | solution.py:437
  689.2 1.5 collective-permute-start.3
  690.7 21.5 %collective-permute-done.3.refs_6_ = bf16[256,2048]{1,0:T(8,128)(2,1)S(1)} collective-permute-done((bf16[256,2048]{1,0:T(8,128)(2,1)S(1)}, bf16[256,2048]{1,0:T(8,128)(2,1)S(1)}, u32[]{:S(2)}, u32[]{:S(2)}) %collective-permute-start.3) | collective-permute-done | bytes 1048608 | tf_op jit(solution)/shard_map/ppermute | solution.py:565
  713.1 118.7 %expert_fwd.2 = (f32[4,1024,2048]{2,1,0:T(8,128)}, f32[4,512,2048]{2,1,0:T(8,128)}, bf16[8,256,2048]{2,1,0:T(8,128)(2,1)}) custom-call(bf16[8,256,2048]{2,1,0:T(8,128)(2,1)} %get-tuple-element.30.refs_0_, bf16[8,512,2048]{2,1,0:T(8,128)(2,1)} %get-tuple-element.25.refs_1_.refs_0_, f32[8,1024,4]{2,1,0:T(8,128)} %bitcast.35, bf16[4,2048,512]{2,1,0:T(8,128)(2,1)} %bitcast.53, ...), custom_call_target="tpu_custom_call" | custom-call | flops 103079215104 | bytes 50331648 | tf_op jit(solution)/shard_map/expert_fwd/pallas_call | solution.py:367
  831.9 117.5 %expert_fwd.3 = (f32[4,1024,2048]{2,1,0:T(8,128)}, f32[4,512,2048]{2,1,0:T(8,128)}) custom-call(bf16[8,512,2048]{2,1,0:T(8,128)(2,1)} %get-tuple-element.25.refs_1_.refs_0_, bf16[8,256,2048]{2,1,0:T(8,128)(2,1)} %get-tuple-element.31.refs_1_, f32[8,1024,4]{2,1,0:T(8,128)} %bitcast.36, ...), custom_call_target="tpu_custom_call", output_to_operand_aliasing={{0}: (6, {})} | custom-call | flops 103079215104 | bytes 50331648 | tf_op jit(solution)/shard_map/expert_fwd/pallas_call | solution.py:367
  949.5 3.3 convert_bitcast_fusion.1
  952.8 1.3 collective-permute-start.5
  954.1 4.4 convert_bitcast_fusion
  959.7 233.4 %weight_grads.1 = (bf16[4,2048,512]{2,1,0:T(8,128)(2,1)}, bf16[4,2048,512]{2,1,0:T(8,128)(2,1)}, bf16[4,512,2048]{2,1,0:T(8,128)(2,1)}) custom-call(f32[8,1024,4]{2,1,0:T(8,128)} %bitcast.37, bf16[8,256,2048]{2,1,0:T(8,128)(2,1)} %get-tuple-element.27.x_ref.refs_0_, bf16[8,2,384,2048]{3,2,1,0:T(8,128)(2,1)} %bitcast.48, bf16[8,2,384,2048]{3,2,1,0:T(8,128)(2,1)} %bitcast.44, ...), custom_call_target="tpu_custom_call" | custom-call | flops 206158430208 | bytes 268435456 | tf_op jit(solution)/shard_map/weight_grads/pallas_call | solution.py:504
  1193.2 5.1 maximum_bitcast_fusion
  1198.3 35.6 %reduce-scatter.10.cloned.1.call-done = f32[1,1024,2048]{2,1,0:T(8,128)} async-done(((f32[4,1024,2048]{2,1,0:T(8,128)}), f32[1,1024,2048]{2,1,0:T(8,128)}) %reduce-scatter.10.cloned.1.call-update) | async-done | bytes 8388624
  1233.8 6.0 convert_element_type.16
  (32 shorter events, 5.0 us)
Async XLA Ops:
  7.2 39.4 %slice-start = ((bf16[1,1024,2048]{2,1,0:T(8,128)(2,1)}), bf16[1,384,2048]{2,1,0:T(8,128)(2,1)S(1)}, s32[]{:S(2)}) async-start(bf16[1,1024,2048]{2,1,0:T(8,128)(2,1)} %param.13), calls=%async_computation.9 | async-start | bytes 3145728 | tf_op jit(solution)/shard_map/slice | solution.py:569
  7.2 257.3 %all-gather.5.cloned.1.call-start = ((), (), s32[]{:S(2)}) async-start(), calls=%async_computation.4 | async-start | bytes 28311552 | tf_op jit(solution)/shard_map/all_gather | solution.py:544
  8.9 37.7 %collective-permute-start = (bf16[384,2048]{1,0:T(8,128)(2,1)S(1)}, bf16[384,2048]{1,0:T(8,128)(2,1)S(1)}, u32[]{:S(2)}, u32[]{:S(2)}) collective-permute-start(bf16[384,2048]{1,0:T(8,128)(2,1)S(1)} %slice_bitcast_fusion.1), channel_id=1, source_target_pairs={{0,8},{8,0},{1,9},{9,1},{2,10},{10,2},{3,11},{11,3},{4,12},{12,4},... | collective-permute-start | bytes 4718600 | tf_op jit(solution)/shard_map/ppermute | solution.py:565
  48.5 482.6 %all-gather.7.cloned.1.call-start = ((), (), s32[]{:S(2)}) async-start(), calls=%async_computation.5 | async-start | bytes 28311552 | tf_op jit(solution)/shard_map/all_gather | solution.py:544
  176.3 3.8 copy-start
  176.3 3.8 copy-start.1
  176.4 773.1 %reduce-scatter.14.cloned.1.call-start = ((), (), s32[]{:S(2)}) async-start(), calls=%async_computation.8 | async-start | bytes 15728640
  178.5 86.0 %collective-permute-start.2 = (bf16[768,2048]{1,0:T(8,128)(2,1)S(1)}, bf16[768,2048]{1,0:T(8,128)(2,1)}, u32[]{:S(2)}, u32[]{:S(2)}) collective-permute-start(bf16[768,2048]{1,0:T(8,128)(2,1)S(1)} %slice_bitcast_fusion), channel_id=1, source_target_pairs={{0,8},{8,0},{1,9},{9,1},{2,10},{10,2},{3,11},{11,3},{4,12},{12,4},... | collective-permute-start | bytes 9437192 | tf_op jit(solution)/shard_map/ppermute | solution.py:565
  180.4 71.4 %collective-permute-start.1 = (f32[8,4,1024]{2,0,1:T(8,128)S(1)}, f32[8,4,1024]{2,0,1:T(8,128)S(1)}, u32[]{:S(2)}, u32[]{:S(2)}) collective-permute-start(f32[8,4,1024]{2,0,1:T(8,128)S(1)} %copy.24), channel_id=1, source_target_pairs={{0,8},{8,0},{1,9},{9,1},{2,10},{10,2},{3,11},{11,3},{4,12},{12,4},... | collective-permute-start | bytes 393224 | tf_op jit(solution)/shard_map/ppermute | solution.py:552
  420.5 533.6 %reduce-scatter.12.cloned.1.call-start = ((), (), s32[]{:S(2)}) async-start(), calls=%async_computation.7 | async-start | bytes 26214400
  687.8 546.0 %reduce-scatter.10.cloned.1.call-start = ((), (), s32[]{:S(2)}) async-start(), calls=%async_computation.6 | async-start | bytes 41943040
  689.2 23.0 %collective-permute-start.3 = (bf16[256,2048]{1,0:T(8,128)(2,1)S(1)}, bf16[256,2048]{1,0:T(8,128)(2,1)S(1)}, u32[]{:S(2)}, u32[]{:S(2)}) collective-permute-start(bf16[256,2048]{1,0:T(8,128)(2,1)S(1)} %slice_bitcast_fusion.2), channel_id=1, source_target_pairs={{0,8},{8,0},{1,9},{9,1},{2,10},{10,2},{3,11},{11,3},{4,12},{12,4},... | collective-permute-start | bytes 3145736 | tf_op jit(solution)/shard_map/ppermute | solution.py:565
  712.2 1.0 copy-start.2
  952.8 240.4 %collective-permute-start.5 = (bf16[384,2048]{1,0:T(8,128)(2,1)}, bf16[384,2048]{1,0:T(8,128)(2,1)}, u32[]{:S(2)}, u32[]{:S(2)}) collective-permute-start(bf16[384,2048]{1,0:T(8,128)(2,1)} %convert_bitcast_fusion.1), channel_id=1, source_target_pairs={{8,0},{0,8},{9,1},{1,9},{10,2},{2,10},{11,3},{3,11},{12,4},{4,12},... | collective-permute-start | bytes 4718600 | tf_op jit(solution)/shard_map/ppermute | solution.py:591
  958.5 234.7 %collective-permute-start.4 = (bf16[640,2048]{1,0:T(8,128)(2,1)}, bf16[640,2048]{1,0:T(8,128)(2,1)}, u32[]{:S(2)}, u32[]{:S(2)}) collective-permute-start(bf16[640,2048]{1,0:T(8,128)(2,1)} %convert_bitcast_fusion), channel_id=1, source_target_pairs={{8,0},{0,8},{9,1},{1,9},{10,2},{2,10},{11,3},{3,11},{12,4},{4,12},... | collective-permute-start | bytes 7864328 | tf_op jit(solution)/shard_map/ppermute | solution.py:591
Sparse Core Ops, SparseCore 0:
  48.6 174.8 all-gather.4
  225.3 184.6 all-gather.6
  420.6 116.5 reduce-scatter.13
  688.0 217.1 reduce-scatter.11
  949.6 284.2 reduce-scatter.9
